TPU v7x, 32 devices: a whole 2x2x4 slice. The times are simulated.
32 devices in a mesh: groups: 2 (over y), seq: 4 (over z), head: 4 (over x, core).
Axes of the slice: x: 2, y: 2, z: 4, core: 2. Of those that a mesh axis runs over, the one named last changes fastest.
Arguments:
- tile_rows: bfloat16 [8192, 1536], P(('groups', 'seq', 'head')), parts along dimension 0, may hold values from -6 to 6
- tile_route: int32 [8192, 2], P(('groups', 'seq', 'head')), parts along dimension 0, may hold values from 0 to 255, as said below
- embed_weight: bfloat16 [1536, 768], replicated, may hold values from -0.15625 to 0.15625
- norm_gain: float32 [768], replicated, may hold values from 0.1 to 1.9
- qkv_weight: bfloat16 [768, 16, 3, 48], P(None, 'head'), may hold values from -1 to 1
- out_weight: bfloat16 [768, 768], P('head'), may hold values from -0.21875 to 0.21875
Outputs:
- mixed: bfloat16 [8192, 768], P(('groups', 'seq', 'head')), parts along dimension 0
There are 2 independent parts, one for each index of `groups`. A program takes and returns all parts, laid end to end along the dimension named above; an argument that names none is the same for every part. Nothing has to cross between parts.
Inputs may be any that keep to these rules, and one draw needn't show every extreme that they name: `tile_route`: A tile's owner holds the same head class as the tile's own device. From one device at most 128 tiles go to one index of seq, and some device sends exactly 128 to one index in every draw; every slot of every owner receives exactly one tile.
All inputs are finite; a program needn't handle non-finite values.
Results may differ from a plain program's by a relative error of at most 0.0075.
Values may be sent and summed in bfloat16 or wider, within the bound.
No kernel may reach another device: no remote copies, remote signals or barrier semaphores. Data moves between devices by JAX's collectives and lax.ppermute only.
A program may use at most 64 MiB of HBM per device.

v0:
```python
import jax
import jax.numpy as jnp
from jax import lax
from jax.sharding import PartitionSpec as P

EPSILON = 1e-05
DILATIONS = (1, 4, 16)
FRACTIONS = (16, 4, 1)


def from_partner(block, axis, apart):
    count = lax.axis_size(axis)
    route = []
    for low in range(count):
        high = low | 1 << apart
        if high != low and high < count:
            route += [(low, high), (high, low)]
    return lax.ppermute(block, axis, route)


def layer_norm(rows, gain):
    row_mean = jnp.mean(rows, axis=-1, keepdims=True)
    centered = rows - row_mean
    row_var = jnp.mean(centered * centered, axis=-1, keepdims=True)
    return (centered * lax.rsqrt(row_var + EPSILON) * gain).astype(jnp.bfloat16)


def attend_block(queries, key_rows, values):
    score_scale = queries.shape[-1] ** (-0.5)
    scores = jnp.dot(queries, key_rows.T, preferred_element_type=jnp.float32) * score_scale
    row_max = jnp.max(scores, axis=-1)
    expo = jnp.exp(scores - row_max[:, None])
    denominator = jnp.sum(expo, axis=-1)
    weights = (expo / denominator[:, None]).astype(jnp.bfloat16)
    head_out = jnp.dot(weights, values, preferred_element_type=jnp.float32)
    return (head_out, row_max + jnp.log(denominator))


def attend(queries, key_rows, values):
    count = queries.shape[0]
    if count > 512 and count % 512 == 0:
        blocks = queries.reshape(count // 512, 512, queries.shape[1])
        head_out, log_total = lax.map(
            lambda block_in: attend_block(block_in, key_rows, values), blocks
        )
        return (head_out.reshape(count, -1), log_total.reshape(count))
    return attend_block(queries, key_rows, values)


def expand_rows(head_out, log_total, offset, dilation):
    count = head_out.shape[0]
    pick_mask = jnp.arange(dilation, dtype=jnp.int32) == offset
    full_out = jnp.where(pick_mask[None, :, None], head_out[:, None, :], 0.0).reshape(
        count * dilation, -1
    )
    full_total = jnp.where(pick_mask[None, :], log_total[:, None], -1e30).reshape(count * dilation)
    return (full_out, full_total)


def merge_scales(outputs, totals):
    row_max = jnp.maximum(jnp.maximum(totals[0], totals[1]), totals[2])
    numer = jnp.zeros_like(outputs[0])
    denom = jnp.zeros_like(totals[0])
    for full_out, full_total in zip(outputs, totals):
        factor = jnp.exp(full_total - row_max)
        numer = numer + factor[:, None] * full_out
        denom = denom + factor
    return numer / denom[:, None]


def collect_segment(flat_rows, levels, seq_index):
    for level in range(levels):
        partner = from_partner(flat_rows, "seq", level)
        upper_half = seq_index >> level & 1 == 1
        lower_rows = jnp.where(upper_half, partner, flat_rows)
        upper_rows = jnp.where(upper_half, flat_rows, partner)
        flat_rows = jnp.concatenate([lower_rows, upper_rows], axis=0)
    return flat_rows


def local(tile_rows, tile_route, embed_weight, norm_gain, qkv_weight, out_weight):
    seq_count = lax.axis_size("seq")
    seq_index = lax.axis_index("seq")
    in_rows = tile_rows.shape[0]
    width = embed_weight.shape[1]
    capacity = 2 * in_rows // seq_count
    projected = jnp.dot(tile_rows, embed_weight, preferred_element_type=jnp.float32).astype(
        jnp.bfloat16
    )
    dest_seq = tile_route[:, 0]
    slot_index = tile_route[:, 1]
    owner_hits = (dest_seq[:, None] == jnp.arange(seq_count, dtype=jnp.int32)[None, :]).astype(
        jnp.int32
    )
    earlier = jnp.cumsum(owner_hits, axis=0) - owner_hits
    owner_rank = jnp.sum(earlier * owner_hits, axis=1)
    buffer_place = dest_seq * capacity + owner_rank
    send_pick = jnp.arange(seq_count * capacity, dtype=jnp.int32)[:, None] == buffer_place[None, :]
    outgoing = jnp.dot(
        send_pick.astype(jnp.bfloat16), projected, preferred_element_type=jnp.float32
    ).astype(jnp.bfloat16)
    outgoing_slot = jnp.sum(jnp.where(send_pick, slot_index[None, :] + 1, 0), axis=1)
    arrived, arrived_slot = (
        lax.all_to_all(
            outgoing.reshape(seq_count, capacity, width),
            "seq",
            split_axis=0,
            concat_axis=0,
            tiled=True,
        ),
        lax.all_to_all(
            outgoing_slot.reshape(seq_count, capacity),
            "seq",
            split_axis=0,
            concat_axis=0,
            tiled=True,
        ),
    )
    landing = jnp.arange(in_rows, dtype=jnp.int32)[:, None] + 1 == arrived_slot.reshape(-1)[None, :]
    embedded = jnp.dot(
        landing.astype(jnp.bfloat16), arrived.reshape(-1, width), preferred_element_type=jnp.float32
    )
    normed = layer_norm(embedded, norm_gain)
    heads_here = qkv_weight.shape[1]
    head_dim = qkv_weight.shape[3]
    weight_flat = qkv_weight.reshape(width, -1)
    qkv = jnp.dot(
        lax.all_gather(normed, "head", axis=0, tiled=True),
        weight_flat,
        preferred_element_type=jnp.float32,
    ).astype(jnp.bfloat16)
    rows_here = qkv.shape[0]
    qkv = qkv.reshape(rows_here, heads_here, 3, head_dim)
    first_head = lax.axis_index("head") * heads_here
    total_rows = rows_here * seq_count
    outputs = [[] for member in range(heads_here)]
    totals = [[] for member in range(heads_here)]
    for fraction, dilation in zip(FRACTIONS, DILATIONS):
        segment = total_rows // fraction
        per_segment = segment // dilation
        count = rows_here // dilation
        shaped = qkv.reshape(count, dilation, heads_here, 3, head_dim)
        offsets = []
        chosen = []
        for member in range(heads_here):
            offset = (first_head + member) % dilation
            offsets.append(offset)
            chosen.append(
                lax.dynamic_index_in_dim(shaped[:, :, member], offset, axis=1, keepdims=False)
            )
        chosen = jnp.stack(chosen, axis=1)
        queries = chosen[:, :, 0]
        pairs = chosen[:, :, 1:]
        if segment > rows_here:
            levels = (segment // rows_here).bit_length() - 1
            flat_rows = collect_segment(pairs.reshape(count, -1), levels, seq_index)
            pairs = flat_rows.reshape(per_segment, heads_here, 2, head_dim)
            groups = 1
        else:
            groups = rows_here // segment
        grouped_queries = queries.reshape(groups, count // groups, heads_here, head_dim)
        grouped_pairs = pairs.reshape(groups, per_segment, heads_here, 2, head_dim)
        for member in range(heads_here):
            head_out, log_total = lax.map(
                lambda block_in: attend(block_in[0], block_in[1][:, 0], block_in[1][:, 1]),
                (grouped_queries[:, :, member], grouped_pairs[:, :, member]),
            )
            full_out, full_total = expand_rows(
                head_out.reshape(count, head_dim),
                log_total.reshape(count),
                offsets[member],
                dilation,
            )
            outputs[member].append(full_out)
            totals[member].append(full_total)
    merged = [
        merge_scales(outputs[member], totals[member]).astype(jnp.bfloat16)
        for member in range(heads_here)
    ]
    attention = jnp.stack(merged, axis=1).reshape(rows_here, heads_here * head_dim)
    regrouped = lax.all_to_all(attention, "head", split_axis=0, concat_axis=1, tiled=True)
    branch = jnp.dot(
        regrouped,
        lax.all_gather(out_weight, "head", axis=0, tiled=True),
        preferred_element_type=jnp.float32,
    )
    return (embedded + branch).astype(jnp.bfloat16)


def solution(mesh):
    return jax.shard_map(
        local,
        mesh=mesh,
        in_specs=(
            P(("groups", "seq", "head"), None),
            P(("groups", "seq", "head"), None),
            P(),
            P(),
            P(None, "head", None, None),
            P("head", None),
        ),
        out_specs=P(("groups", "seq", "head"), None),
        check_vma=False,
    )
```

profile of v0, /device:TPU:0, one launch (start us, length us, event | category | flops | bytes accessed | tf_op | source)
XLA Modules:
  0.0 301.8 jit_solution(2592736077684952324)
XLA Ops:
  9.8 6.3 %all-to-all-start = ((s32[4,1,128]{2,1,0:T(1,128)}), s32[4,1,128]{2,1,0:T(1,128)S(1)}, u32[]{:S(2)}, u32[]{:S(2)}) async-start(s32[4,1,128]{2,1,0:T(1,128)} %bitcast.29), calls=%async_computation | async-start | bytes 4096 | tf_op jit(solution)/shard_map/all_to_all | solution.py:111
  16.1 3.2 %convolution_convert_fusion.1 = bf16[512,768]{1,0:T(8,128)(2,1)} fusion(bf16[256,1536]{1,0:T(8,128)(2,1)} %param.14, bf16[1536,768]{1,0:T(8,128)(2,1)S(1)} %copy-done, s32[256]{0:T(256)S(1)} %multiply_add_fusion), kind=kOutput, calls=%fused_computation.49 | convolution fusion | flops 806027264 | bytes 3933184 | tf_op jit(solution)/shard_map/dot_general | solution.py:99
  21.6 3.5 %all-to-all-start.1 = ((bf16[4,128,768]{2,1,0:T(8,128)(2,1)}), bf16[4,128,768]{2,1,0:T(8,128)(2,1)S(1)}, u32[]{:S(2)}, u32[]{:S(2)}) async-start(bf16[4,128,768]{2,1,0:T(8,128)(2,1)} %bitcast.363), calls=%async_computation.1 | async-start | bytes 1572864 | tf_op jit(solution)/shard_map/all_to_all | solution.py:104
  25.2 18.9 %all-to-all-done.1 = bf16[4,128,768]{2,1,0:T(8,128)(2,1)S(1)} async-done(((bf16[4,128,768]{2,1,0:T(8,128)(2,1)}), bf16[4,128,768]{2,1,0:T(8,128)(2,1)S(1)}, u32[]{:S(2)}, u32[]{:S(2)}) %all-to-all-start.1) | async-done | bytes 786464 | tf_op jit(solution)/shard_map/all_to_all | solution.py:104
  54.3 12.3 %all-gather.3.cloned.1.call-done = bf16[1024,768]{1,0:T(8,128)(2,1)} async-done(((bf16[256,768]{1,0:T(8,128)(2,1)}), bf16[1024,768]{1,0:T(8,128)(2,1)}) %all-gather.3.cloned.1.call-update) | async-done | bytes 1572880 | tf_op jit(solution)/shard_map/all_gather | solution.py:128
  66.6 3.8 %convolution_convert_fusion = bf16[1024,576]{0,1:T(8,128)(2,1)} fusion(bf16[1024,768]{1,0:T(8,128)(2,1)} %all-gather.3.cloned.1.call-done, bf16[768,576]{0,1:T(8,128)(2,1)} %bitcast.399), kind=kOutput, calls=%fused_computation.48 | convolution fusion | flops 906559488 | bytes 3637248 | tf_op jit(solution)/shard_map/dot_general | solution.py:127
  70.4 2.5 copy.117
  72.9 10.5 %reshape_reshape.14 = bf16[64,16,4,3,48]{4,3,2,1,0:T(4,128)(2,1)} reshape(bf16[1024,576]{1,0:T(8,128)(2,1)} %copy.117) | data formatting | bytes 2359296 | tf_op jit(solution)/shard_map/reshape;reshape | solution.py:142
  83.4 10.5 %reshape_reshape.13 = bf16[256,4,4,3,48]{4,3,2,1,0:T(4,128)(2,1)} reshape(bf16[1024,576]{1,0:T(8,128)(2,1)} %copy.117) | data formatting | bytes 2359296 | tf_op jit(solution)/shard_map/reshape;reshape | solution.py:142
  93.9 4.0 %fusion.46 = (bf16[256,4,1,3,48]{4,3,2,1,0:T(4,128)(2,1)}, bf16[256,4,1,3,48]{4,3,2,1,0:T(4,128)(2,1)S(1)}, bf16[256,4,1,3,48]{4,3,2,1,0:T(4,128)(2,1)S(1)}, bf16[256,4,1,3,48]{4,3,2,1,0:T(4,128)(2,1)}) fusion(bf16[256,4,4,3,48]{4,3,2,1,0:T(4,128)(2,1)} %reshape_reshape.13), kind=kLoop, calls=%fused_computation.230 | loop fusion | bytes 2359296 | tf_op jit(solution)/shard_map/slice | solution.py:149
  113.4 2.9 fusion.47
  131.1 2.6 reshape.1464
  137.4 18.2 %while.11 = (s32[]{:T(128)}, f32[4,256,48]{1,0,2:T(4,128)}, f32[4,256]{1,0:T(4,128)S(1)}, bf16[4,256,48]{2,1,0:T(8,128)(2,1)}, bf16[4,256,2,48]{1,3,2,0:T(8,128)(2,1)}, /*index=5*/s32[]{:T(128)}, s32[]{:T(128)}) while((s32[]{:T(128)}, f32[4,256,48]{1,0,2:T(4,128)}, f32[4,256]{1,0:T(4,128)S(1)}, bf16[4,256,48]{2,1,0:T(8,128)(2,1)}, ...), condition=%wide.region_33.34_spmd, body=%wide.region_30.33_spmd.sunk | while | flops 13041410 | bytes 1255525 | solution.py:164
  157.9 18.2 %while.10 = (s32[]{:T(128)}, f32[4,256,48]{1,0,2:T(4,128)}, f32[4,256]{1,0:T(4,128)S(1)}, bf16[4,256,48]{2,1,0:T(8,128)(2,1)}, bf16[4,256,2,48]{1,3,2,0:T(8,128)(2,1)}, /*index=5*/s32[]{:T(128)}, s32[]{:T(128)}) while((s32[]{:T(128)}, f32[4,256,48]{1,0,2:T(4,128)}, f32[4,256]{1,0:T(4,128)S(1)}, bf16[4,256,48]{2,1,0:T(8,128)(2,1)}, ...), condition=%wide.region_25.26_spmd, body=%wide.region_22.25_spmd.sunk | while | flops 13041410 | bytes 1255525 | solution.py:164
  160.1 2.3 dynamic_update_slice.74
  164.7 2.3 dynamic_update_slice.74
  169.2 2.3 dynamic_update_slice.74
  178.4 18.2 %while.9 = (s32[]{:T(128)}, f32[4,256,48]{1,0,2:T(4,128)}, f32[4,256]{1,0:T(4,128)S(1)}, bf16[4,256,48]{2,1,0:T(8,128)(2,1)}, bf16[4,256,2,48]{1,3,2,0:T(8,128)(2,1)}, /*index=5*/s32[]{:T(128)}, s32[]{:T(128)}) while((s32[]{:T(128)}, f32[4,256,48]{1,0,2:T(4,128)}, f32[4,256]{1,0:T(4,128)S(1)}, bf16[4,256,48]{2,1,0:T(8,128)(2,1)}, ...), condition=%wide.region_17.18_spmd, body=%wide.region_14.17_spmd.sunk | while | flops 13041410 | bytes 1255525 | solution.py:164
  200.1 15.1 %while.8 = (s32[]{:T(128)}, f32[4,256,48]{1,0,2:T(4,128)}, f32[4,256]{1,0:T(4,128)S(1)}, bf16[4,256,48]{2,1,0:T(8,128)(2,1)S(1)}, bf16[4,256,2,48]{1,3,2,0:T(8,128)(2,1)}, /*index=5*/s32[]{:T(128)}, s32[]{:T(128)}) while((s32[]{:T(128)}, f32[4,256,48]{1,0,2:T(4,128)}, f32[4,256]{1,0:T(4,128)S(1)}, bf16[4,256,48]{2,1,0:T(8,128)(2,1)S(1)}, ...), condition=%wide.region_9.10_spmd, body=%wide.region_6.9_spmd.sunk | while | flops 13041410 | bytes 1255525 | solution.py:164
  241.5 2.5 collective-permute-start.1
  244.0 5.2 %collective-permute-done.1 = bf16[128,384]{0,1:T(8,128)(2,1)S(1)} collective-permute-done((bf16[128,384]{0,1:T(8,128)(2,1)S(1)}, bf16[128,384]{0,1:T(8,128)(2,1)S(1)}, u32[]{:S(2)}, u32[]{:S(2)}) %collective-permute-start.1) | collective-permute-done | bytes 98336 | tf_op jit(solution)/shard_map/ppermute | solution.py:18
  281.6 3.5 %all-to-all-start.2 = ((bf16[4,256,192]{1,2,0:T(8,128)(2,1)}), bf16[4,256,192]{1,2,0:T(8,128)(2,1)S(1)}, u32[]{:S(2)}, u32[]{:S(2)}) async-start(bf16[4,256,192]{1,2,0:T(8,128)(2,1)} %copy.150), calls=%async_computation.2 | async-start | bytes 786432 | tf_op jit(solution)/shard_map/all_to_all | solution.py:181
  285.1 7.3 %all-to-all-done.2 = bf16[4,256,192]{1,2,0:T(8,128)(2,1)S(1)} async-done(((bf16[4,256,192]{1,2,0:T(8,128)(2,1)}), bf16[4,256,192]{1,2,0:T(8,128)(2,1)S(1)}, u32[]{:S(2)}, u32[]{:S(2)}) %all-to-all-start.2) | async-done | bytes 393248 | tf_op jit(solution)/shard_map/all_to_all | solution.py:181
  292.4 2.5 fusion.16
  (358 shorter events, 178.2 us)
Async XLA Ops:
  6.5 9.6 %copy-start = (bf16[1536,768]{1,0:T(8,128)(2,1)S(1)}, bf16[1536,768]{1,0:T(8,128)(2,1)}, u32[]{:S(2)}) copy-start(bf16[1536,768]{1,0:T(8,128)(2,1)} %param.16) | copy-start | bytes 7077892
  9.8 11.8 %all-to-all-start = ((s32[4,1,128]{2,1,0:T(1,128)}), s32[4,1,128]{2,1,0:T(1,128)S(1)}, u32[]{:S(2)}, u32[]{:S(2)}) async-start(s32[4,1,128]{2,1,0:T(1,128)} %bitcast.29), calls=%async_computation | async-start | bytes 4096 | tf_op jit(solution)/shard_map/all_to_all | solution.py:111
  21.6 22.4 %all-to-all-start.1 = ((bf16[4,128,768]{2,1,0:T(8,128)(2,1)}), bf16[4,128,768]{2,1,0:T(8,128)(2,1)S(1)}, u32[]{:S(2)}, u32[]{:S(2)}) async-start(bf16[4,128,768]{2,1,0:T(8,128)(2,1)} %bitcast.363), calls=%async_computation.1 | async-start | bytes 1572864 | tf_op jit(solution)/shard_map/all_to_all | solution.py:104
  25.1 21.7 %copy-start.28 = (f32[768]{0:T(1024)S(1)}, f32[768]{0:T(1024)}, u32[]{:S(2)}) copy-start(f32[768]{0:T(1024)} %param.17) | copy-start | bytes 9220
  25.1 41.5 %all-gather.3.cloned.1.call-start = ((), (), s32[]{:S(2)}) async-start(), calls=%async_computation.3 | async-start | bytes 1966080 | tf_op jit(solution)/shard_map/all_gather | solution.py:128
  47.8 237.3 %all-gather.5.cloned.1.call-start = ((), (), s32[]{:S(2)}) async-start(), calls=%async_computation.4 | async-start | bytes 1474560 | tf_op jit(solution)/shard_map/all_gather | solution.py:184
  126.2 114.2 %collective-permute-start = (bf16[64,384]{0,1:T(8,128)(2,1)}, bf16[64,384]{0,1:T(8,128)(2,1)}, u32[]{:S(2)}, u32[]{:S(2)}) collective-permute-start(bf16[64,384]{0,1:T(8,128)(2,1)} %bitcast.57), channel_id=1, source_target_pairs={{0,4},{4,0},{8,12},{12,8},{1,5},{5,1},{9,13},{13,9},{2,6},{6,2},{1... | collective-permute-start | bytes 147464 | tf_op jit(solution)/shard_map/ppermute | solution.py:18
  178.4 18.2 %copy-start.20 = (bf16[256,2,48]{0,2,1:T(8,128)(2,1)S(1)}, bf16[256,2,48]{0,2,1:T(8,128)(2,1)}, u32[]{:S(2)}) copy-start(bf16[256,2,48]{0,2,1:T(8,128)(2,1)} %get-tuple-element.389) | copy-start | bytes 147460
  215.7 10.0 %copy-start.5 = (f32[4,256,48]{1,0,2:T(4,128)S(1)}, f32[4,256,48]{1,0,2:T(4,128)}, u32[]{:S(2)}) copy-start(f32[4,256,48]{1,0,2:T(4,128)} %get-tuple-element.240) | copy-start | bytes 589828
  222.0 9.1 %copy-start.6 = (f32[4,256,48]{1,0,2:T(4,128)S(1)}, f32[4,256,48]{1,0,2:T(4,128)}, u32[]{:S(2)}) copy-start(f32[4,256,48]{1,0,2:T(4,128)} %get-tuple-element.233) | copy-start | bytes 589828
  227.3 10.9 %copy-start.4 = (f32[4,256,48]{1,0,2:T(4,128)S(1)}, f32[4,256,48]{1,0,2:T(4,128)}, u32[]{:S(2)}) copy-start(f32[4,256,48]{1,0,2:T(4,128)} %get-tuple-element.231) | copy-start | bytes 589828
  231.8 12.2 %copy-start.16 = (bf16[64,1,1,3,48]{0,4,3,2,1:T(8,128)(2,1)S(1)}, bf16[64,1,1,3,48]{0,4,3,2,1:T(8,128)(2,1)}, u32[]{:S(2)}) copy-start(bf16[64,1,1,3,48]{0,4,3,2,1:T(8,128)(2,1)} %copy.126) | copy-start | bytes 55300
  231.8 12.2 %copy-start.17 = (bf16[64,1,1,3,48]{0,4,3,2,1:T(8,128)(2,1)S(1)}, bf16[64,1,1,3,48]{0,4,3,2,1:T(8,128)(2,1)}, u32[]{:S(2)}) copy-start(bf16[64,1,1,3,48]{0,4,3,2,1:T(8,128)(2,1)} %copy.125) | copy-start | bytes 55300
  234.5 9.5 %copy-start.18 = (bf16[64,1,1,3,48]{0,4,3,2,1:T(8,128)(2,1)S(1)}, bf16[64,1,1,3,48]{0,4,3,2,1:T(8,128)(2,1)}, u32[]{:S(2)}) copy-start(bf16[64,1,1,3,48]{0,4,3,2,1:T(8,128)(2,1)} %copy.124) | copy-start | bytes 55300
  234.5 9.5 %copy-start.19 = (bf16[64,1,1,3,48]{0,4,3,2,1:T(8,128)(2,1)S(1)}, bf16[64,1,1,3,48]{0,4,3,2,1:T(8,128)(2,1)}, u32[]{:S(2)}) copy-start(bf16[64,1,1,3,48]{0,4,3,2,1:T(8,128)(2,1)} %copy.123) | copy-start | bytes 55300
  241.5 7.7 %collective-permute-start.1 = (bf16[128,384]{0,1:T(8,128)(2,1)S(1)}, bf16[128,384]{0,1:T(8,128)(2,1)S(1)}, u32[]{:S(2)}, u32[]{:S(2)}) collective-permute-start(bf16[128,384]{0,1:T(8,128)(2,1)S(1)} %pad_maximum_fusion.12), channel_id=1, source_target_pairs={{0,8},{8,0},{4,12},{12,4},{1,9},{9,1},{5,13},{13,5},{2,10},{10,2},... | collective-permute-start | bytes 294920 | tf_op jit(solution)/shard_map/ppermute | solution.py:18
  260.1 14.1 %copy-start.21 = (f32[1024]{0:T(1024)S(1)}, f32[1024]{0:T(1024)}, u32[]{:S(2)}) copy-start(f32[1024]{0:T(1024)} %broadcast_in_dim.470) | copy-start | bytes 12292
  260.1 14.8 %copy-start.22 = (f32[1024]{0:T(1024)S(1)}, f32[1024]{0:T(1024)}, u32[]{:S(2)}) copy-start(f32[1024]{0:T(1024)} %broadcast_in_dim.454) | copy-start | bytes 12292
  260.1 15.5 %copy-start.7 = (f32[1024,1,48]{0,2,1:T(8,128)S(1)}, f32[1024,1,48]{0,2,1:T(8,128)}, u32[]{:S(2)}) copy-start(f32[1024,1,48]{0,2,1:T(8,128)} %broadcast_in_dim_reshape.23) | copy-start | bytes 589828
  261.7 15.0 %copy-start.8 = (f32[1024,1,48]{0,2,1:T(8,128)S(1)}, f32[1024,1,48]{0,2,1:T(8,128)}, u32[]{:S(2)}) copy-start(f32[1024,1,48]{0,2,1:T(8,128)} %broadcast_in_dim_reshape.21) | copy-start | bytes 589828
  272.6 6.0 %copy-start.12 = (f32[1024,1,48]{0,2,1:T(8,128)S(1)}, f32[1024,1,48]{0,2,1:T(8,128)}, u32[]{:S(2)}) copy-start(f32[1024,1,48]{0,2,1:T(8,128)} %copy.129) | copy-start | bytes 589828
  272.6 6.0 %copy-start.13 = (f32[1024,1,48]{0,2,1:T(8,128)S(1)}, f32[1024,1,48]{0,2,1:T(8,128)}, u32[]{:S(2)}) copy-start(f32[1024,1,48]{0,2,1:T(8,128)} %copy.131) | copy-start | bytes 589828
  272.6 6.0 %copy-start.26 = (pred[1024]{0:T(1024)(128)(4,1)S(1)}, pred[1024]{0:T(1024)(128)(4,1)}, u32[]{:S(2)}) copy-start(pred[1024]{0:T(1024)(128)(4,1)} %broadcast_in_dim.457) | copy-start | bytes 3076
  281.6 10.8 %all-to-all-start.2 = ((bf16[4,256,192]{1,2,0:T(8,128)(2,1)}), bf16[4,256,192]{1,2,0:T(8,128)(2,1)S(1)}, u32[]{:S(2)}, u32[]{:S(2)}) async-start(bf16[4,256,192]{1,2,0:T(8,128)(2,1)} %copy.150), calls=%async_computation.2 | async-start | bytes 786432 | tf_op jit(solution)/shard_map/all_to_all | solution.py:181
  (13 other events, 59.1 us)
Sparse Core Ops, SparseCore 0:
  47.9 18.7 all-gather.2
  68.2 17.4 all-gather.4
where the time goes:
time: 306 us; the launch traced here: 302 us
  local copies, waits for them, and re-layouts  167 us (55%)
  waiting for transfers between devices  46.7 us (15%)
  matrix products  35.9 us (12%)
  other arithmetic  20.1 us (7%)
  starting transfers between devices  17.3 us (6%)
  between operations  14.1 us (5%)
    dynamic_update_slice x48, local copies, waits for them, and re-layouts, local(): lax.map(lambda block_in: attend(block_in[0], block_in[1][:, 0], block_in[...  38.2 us
    broadcast_in_dim x16, local copies, waits for them, and re-layouts, expand_rows(): jnp.where(pick_mask[None, :, None], head_out[:, None, :], 0.0)  26.5 us
    another operation x2, local copies, waits for them, and re-layouts, local(): shaped = qkv.reshape(count, dilation, heads_here, 3, head_dim)  21 us
    all_to_all x1, waiting for transfers between devices, local(): lax.all_to_all(outgoing.reshape(seq_count, capacity, width), 'seq', split...  18.9 us
    dot_general x24, matrix products, attend_block(): jnp.dot(queries, key_rows.T, preferred_element_type=jnp.float32)  17.1 us
    broadcast_in_dim x32, local copies, waits for them, and re-layouts, expand_rows(): jnp.where(pick_mask[None, :], log_total[:, None], -1e+30)  15.3 us
    dynamic_slice x12, local copies, waits for them, and re-layouts, local(): lax.dynamic_index_in_dim(shaped[:, :, member], offset, axis=1, keepdims=F...  15 us
    squeeze x18, local copies, waits for them, and re-layouts, local(): lax.map(lambda block_in: attend(block_in[0], block_in[1][:, 0], block_in[...  13.5 us
  transfers between devices with their start and end apart: 7, of which 5 were waited for; matrix products, arithmetic and copies ran while one was open for 70% of the time, Pallas kernels for 0%

commit v1 on v0

--- a/solution.py
+++ b/solution.py
@@ -1,6 +1,10 @@
+import functools
+
 import jax
 import jax.numpy as jnp
 from jax import lax
+from jax.experimental import pallas as pl
+from jax.experimental.pallas import tpu as pltpu
 from jax.sharding import PartitionSpec as P
 
 EPSILON = 1e-05
@@ -78,7 +82,7 @@
     return flat_rows
 
 
-def local(tile_rows, tile_route, embed_weight, norm_gain, qkv_weight, out_weight):
+def general(tile_rows, tile_route, embed_weight, norm_gain, qkv_weight, out_weight):
     seq_count = lax.axis_size("seq")
     seq_index = lax.axis_index("seq")
     in_rows = tile_rows.shape[0]
@@ -187,6 +191,375 @@
     return (embedded + branch).astype(jnp.bfloat16)
 
 
+HALF = 64
+
+
+def iota(shape, dim):
+    return lax.broadcasted_iota(jnp.int32, shape, dim)
+
+
+def matmul(left, right, dims=((1,), (0,))):
+    return lax.dot_general(left, right, (dims, ((), ())), preferred_element_type=jnp.float32)
+
+
+def landed_place(slot, in_rows):
+    middle, last = DILATIONS[1], DILATIONS[2]
+    inner = last // middle
+    run = in_rows // last
+    return slot % middle * (inner * run) + slot // middle % inner * run + slot // last
+
+
+def pack_kernel(seq_count, rows_ref, weight_ref, route_ref, *refs):
+    blocks = refs[:seq_count]
+    slots = refs[seq_count : 2 * seq_count]
+    pick_ref = refs[-1]
+    in_rows = rows_ref.shape[0]
+    capacity = blocks[0].shape[0]
+
+    @pl.when(pl.program_id(0) == 0)
+    def _():
+        me = lax.axis_index("seq")
+        dest = route_ref[0:1, :]
+        slot = route_ref[1:2, :]
+        shift = jnp.where(dest < me, dest - me + seq_count, dest - me)
+        hits = (iota((8, in_rows), 0) == shift).astype(jnp.float32)
+        before = (iota((in_rows, in_rows), 0) < iota((in_rows, in_rows), 1)).astype(jnp.bfloat16)
+        earlier = matmul(hits.astype(jnp.bfloat16), before)
+        base = (iota((8, in_rows), 0) * capacity).astype(jnp.float32)
+        place = jnp.sum(hits * (earlier + base), axis=0, keepdims=True).astype(jnp.int32)
+        pick = iota((seq_count * capacity, in_rows), 0) == place
+        pick_ref[...] = pick.astype(jnp.bfloat16)
+        mark = (landed_place(slot, in_rows) + 1).astype(jnp.float32)
+        marks = jnp.broadcast_to(mark, (8, in_rows)).astype(jnp.bfloat16)
+        found = matmul(marks, pick_ref[...], ((1,), (1,))).astype(jnp.int32)
+        for number in range(seq_count):
+            slots[number][...] = found[0:1, number * capacity : (number + 1) * capacity]
+
+    projected = matmul(rows_ref[...], weight_ref[...]).astype(jnp.bfloat16)
+    packed = matmul(pick_ref[...], projected).astype(jnp.bfloat16)
+    for number in range(seq_count):
+        blocks[number][...] = packed[number * capacity : (number + 1) * capacity]
+
+
+def pack(tile_rows, embed_weight, tile_route, seq_count):
+    in_rows, depth = tile_rows.shape
+    width = embed_weight.shape[1]
+    capacity = 2 * in_rows // seq_count
+    chunk = 256
+    results = pl.pallas_call(
+        functools.partial(pack_kernel, seq_count),
+        grid=(width // chunk,),
+        in_specs=[
+            pl.BlockSpec((in_rows, depth), lambda step: (0, 0)),
+            pl.BlockSpec((depth, chunk), lambda step: (0, step)),
+            pl.BlockSpec((2, in_rows), lambda step: (0, 0)),
+        ],
+        out_specs=[pl.BlockSpec((capacity, chunk), lambda step: (0, step))] * seq_count
+        + [pl.BlockSpec((1, capacity), lambda step: (0, 0))] * seq_count,
+        out_shape=[jax.ShapeDtypeStruct((capacity, width), jnp.bfloat16)] * seq_count
+        + [jax.ShapeDtypeStruct((1, capacity), jnp.int32)] * seq_count,
+        scratch_shapes=[pltpu.VMEM((seq_count * capacity, in_rows), jnp.bfloat16)],
+        cost_estimate=cost(2 * in_rows * width * (depth + seq_count * capacity)),
+        name="pack",
+    )(tile_rows, embed_weight, tile_route.T)
+    return results[:seq_count], results[seq_count:]
+
+
+def cost(flops):
+    return pl.CostEstimate(flops=flops, bytes_accessed=1 << 20, transcendentals=0)
+
+
+def land_kernel(count, *refs):
+    blocks, slots = refs[:count], refs[count : 2 * count]
+    gain_ref, rows_ref, normed_ref = refs[2 * count :]
+    in_rows = rows_ref.shape[0]
+    capacity = blocks[0].shape[0]
+    rows = jnp.zeros(rows_ref.shape, jnp.float32)
+    for block, slot in zip(blocks, slots):
+        here = (iota((in_rows, capacity), 0) + 1 == slot[...]).astype(jnp.bfloat16)
+        rows = rows + matmul(here, block[...])
+    rows_ref[...] = rows.astype(jnp.bfloat16)
+    normed_ref[...] = layer_norm(rows, gain_ref[...])
+
+
+def land(blocks, slots, norm_gain, in_rows):
+    count = len(blocks)
+    capacity, width = blocks[0].shape
+    shape = jax.ShapeDtypeStruct((in_rows, width), jnp.bfloat16)
+    return pl.pallas_call(
+        functools.partial(land_kernel, count),
+        out_shape=[shape, shape],
+        cost_estimate=cost(2 * in_rows * width * count * capacity),
+        name="land",
+    )(*blocks, *slots, norm_gain.reshape(1, width))
+
+
+def turn_kernel(rows_ref, *refs):
+    pieces = refs[:-2]
+    turned_ref, weight_ref = refs[-2:]
+    turned_ref[...] = rows_ref[...].T
+    depth = pieces[0].shape[0]
+    for number, piece in enumerate(pieces):
+        weight_ref[:, number * depth : (number + 1) * depth] = piece[...].T
+
+
+def turn(rows, pieces):
+    width = rows.shape[1]
+    inner = sum(piece.shape[0] for piece in pieces)
+    return pl.pallas_call(
+        turn_kernel,
+        out_shape=[
+            jax.ShapeDtypeStruct((width, rows.shape[0]), jnp.bfloat16),
+            jax.ShapeDtypeStruct((width, inner), jnp.bfloat16),
+        ],
+        cost_estimate=cost(2 * rows.shape[0] * width * 512),
+        name="turn",
+    )(rows, *pieces)
+
+
+def project_block(rows, weight, head_dim):
+    out = matmul(rows, weight)
+    third = out.shape[1] // 3
+    lanes = iota((1, out.shape[1]), 1)
+    ones = (lanes >= 2 * third) & (lanes % HALF == head_dim)
+    return (out + ones.astype(jnp.float32)).astype(jnp.bfloat16)
+
+
+def first_qkv_kernel(head_dim, one_ref, two_ref, weight_ref, out_ref):
+    in_rows = one_ref.shape[0]
+    weight = weight_ref[...]
+    out_ref[:in_rows] = project_block(one_ref[...], weight, head_dim)
+    out_ref[in_rows:] = project_block(two_ref[...], weight, head_dim)
+
+
+def second_qkv_kernel(head_dim, heads_here, one_ref, two_ref, weight_ref, first_ref, out_ref, far_ref):
+    in_rows = one_ref.shape[0]
+    first_qkv_kernel(head_dim, one_ref, two_ref, weight_ref, out_ref)
+    middle, last = DILATIONS[1], DILATIONS[2]
+    run = in_rows // last
+    third = heads_here * HALF
+    inner = lax.axis_index("head") % (last // middle)
+    low = iota((1, 2 * HALF), 1) < HALF
+    for number in range(4):
+        source = first_ref if number < 2 else out_ref
+        start = number % 2 * in_rows
+        for part in range(2):
+            for pair in range(heads_here // 2):
+                column = (1 + part) * third + pair * 2 * HALF
+                both = []
+                for member in (2 * pair, 2 * pair + 1):
+                    row = start + member * (in_rows // middle) + inner * run
+                    both.append(
+                        source[pl.ds(pl.multiple_of(row, run), run), column : column + 2 * HALF]
+                    )
+                far_ref[
+                    number * run : (number + 1) * run,
+                    part * third + pair * 2 * HALF : part * third + (pair + 1) * 2 * HALF,
+                ] = jnp.where(low, both[0], both[1])
+
+
+def first_qkv(one, two, weight, head_dim):
+    in_rows, width = one.shape
+    return pl.pallas_call(
+        functools.partial(first_qkv_kernel, head_dim),
+        out_shape=jax.ShapeDtypeStruct((2 * in_rows, weight.shape[1]), jnp.bfloat16),
+        cost_estimate=cost(4 * in_rows * width * weight.shape[1]),
+        name="first_qkv",
+    )(one, two, weight)
+
+
+def second_qkv(one, two, weight, first, head_dim, heads_here):
+    in_rows, width = one.shape
+    return pl.pallas_call(
+        functools.partial(second_qkv_kernel, head_dim, heads_here),
+        out_shape=[
+            jax.ShapeDtypeStruct((2 * in_rows, weight.shape[1]), jnp.bfloat16),
+            jax.ShapeDtypeStruct((4 * in_rows // DILATIONS[2], 2 * heads_here * HALF), jnp.bfloat16),
+        ],
+        cost_estimate=cost(4 * in_rows * width * weight.shape[1]),
+        name="second_qkv",
+    )(one, two, weight, first)
+
+
+def softmax_product(scores, scale, turned):
+    top = functools.reduce(jnp.maximum, [jnp.max(each, axis=0, keepdims=True) for each in scores])
+    total = None
+    for each, values in zip(scores, turned):
+        weights = jnp.exp2(each * scale - top * scale).astype(jnp.bfloat16)
+        product = matmul(values, weights)
+        total = product if total is None else total + product
+    return total, top
+
+
+def attention_kernel(head_dim, heads_here, first_ref, second_ref, *refs):
+    fars, outs = refs[:-4], refs[-4:]
+    in_rows = first_ref.shape[0] // 2
+    middle, last = DILATIONS[1], DILATIONS[2]
+    wide = in_rows // middle
+    run = in_rows // last
+    third = heads_here * HALF
+    scale = 1.4426950408889634 * head_dim ** (-0.5)
+    inner = lax.axis_index("head") % (last // middle)
+    lanes = iota((1, 2 * HALF), 1)
+    chosen = iota((1, in_rows), 1) // run % (last // middle) == inner
+    sources = [(first_ref, 0), (first_ref, in_rows), (second_ref, 0), (second_ref, in_rows)]
+    for pair in range(heads_here // 2):
+        span = slice(pair * 2 * HALF, (pair + 1) * 2 * HALF)
+        keys_at = slice(third + span.start, third + span.stop)
+        values_at = slice(2 * third + span.start, 2 * third + span.stop)
+        block_keys = [source[start : start + in_rows, keys_at] for source, start in sources]
+        block_turned = [source[start : start + in_rows, values_at].T for source, start in sources]
+        far_keys = jnp.concatenate([far[:, span] for far in fars], axis=0)
+        far_turned = jnp.concatenate(
+            [far[:, third + span.start : third + span.stop] for far in fars], axis=0
+        ).T
+        for side in range(2):
+            member = 2 * pair + side
+            mine = (lanes // HALF == side).astype(jnp.bfloat16)
+            held = slice(side * HALF, (side + 1) * HALF)
+            picked = [
+                slice(start + member * wide, start + (member + 1) * wide) for _, start in sources
+            ]
+
+            def gathered(columns):
+                return jnp.concatenate(
+                    [source[rows, columns] for (source, _), rows in zip(sources, picked)], axis=0
+                )
+
+            picked_queries = gathered(span) * mine
+            near = matmul(gathered(keys_at), picked_queries, ((1,), (1,)))
+            far = matmul(far_keys, picked_queries, ((1,), (1,)))
+            far = jnp.where(chosen, far, -1e30)
+            wide_total, wide_top = softmax_product(
+                [near, far], scale, [gathered(values_at).T[held], far_turned[held]]
+            )
+            for number in range(4):
+                source, start = sources[number]
+                queries = source[start : start + in_rows, span] * mine
+                scores = matmul(block_keys[number], queries, ((1,), (1,)))
+                total, top = softmax_product([scores], scale, [block_turned[number][held]])
+                extra, extra_top = place_lanes(wide_total, wide_top, number, member, wide)
+                tile = member * wide // 128 * 128
+                at = slice(tile, tile + 128)
+                inside = iota((1, 128), 1) // wide == member % (128 // wide)
+                extra_top = jnp.where(inside, extra_top, -1e30)
+                peak = jnp.maximum(top[:, at], extra_top)
+                old = jnp.exp2((top[:, at] - peak) * scale)
+                new = jnp.exp2((extra_top - peak) * scale)
+                merged = total[:, at] * old + jnp.where(inside, extra * new, 0.0)
+                parts = []
+                for other in range(0, in_rows, 128):
+                    parts.append(merged if other == tile else total[:, other : other + 128])
+                rows = slice(member * head_dim, (member + 1) * head_dim)
+                for index, part in enumerate(parts):
+                    done = part[:head_dim] / part[head_dim : head_dim + 1]
+                    outs[number][rows, index * 128 : (index + 1) * 128] = done.astype(jnp.bfloat16)
+
+
+def place_lanes(total, top, number, member, wide):
+    tile = number * wide // 128 * 128
+    shift = (member * wide - number * wide) % 128
+    total, top = total[:, tile : tile + 128], top[:, tile : tile + 128]
+    if shift:
+        total = pltpu.roll(total, shift, 1)
+        top = pltpu.roll(jnp.broadcast_to(top, (8, 128)), shift, 1)[:1]
+    return total, top
+
+
+def attention_blocks(first, second, fars, head_dim, heads_here):
+    in_rows = first.shape[0] // 2
+    out = jax.ShapeDtypeStruct((heads_here * head_dim, in_rows), jnp.bfloat16)
+    return pl.pallas_call(
+        functools.partial(attention_kernel, head_dim, heads_here),
+        out_shape=[out] * 4,
+        cost_estimate=cost(24 * 4 * in_rows * in_rows * 128),
+        name="attention",
+    )(first, second, *fars)
+
+
+def finish_kernel(turned_ref, weight_ref, *refs):
+    pieces, out_ref = refs[:-1], refs[-1]
+    joined = jnp.concatenate([piece[...] for piece in pieces], axis=0)
+    branch = matmul(weight_ref[...], joined)
+    mixed = (turned_ref[...].astype(jnp.float32) + branch).astype(jnp.bfloat16)
+    in_rows = out_ref.shape[0]
+    square = (in_rows, in_rows)
+    back = landed_place(iota(square, 0), in_rows) == iota(square, 1)
+    out_ref[...] = matmul(back.astype(jnp.bfloat16), mixed, ((1,), (1,))).astype(jnp.bfloat16)
+
+
+def finish(turned, weight, pieces):
+    width, in_rows = turned.shape
+    return pl.pallas_call(
+        finish_kernel,
+        out_shape=jax.ShapeDtypeStruct((in_rows, width), jnp.bfloat16),
+        cost_estimate=cost(2 * in_rows * width * (width + in_rows)),
+        name="finish",
+    )(turned, weight, *pieces)
+
+
+def across(block, bit):
+    count = lax.axis_size("head")
+    return lax.ppermute(block, "head", [(member, member ^ bit) for member in range(count)])
+
+
+def shifted(block, shift):
+    count = lax.axis_size("seq")
+    return lax.ppermute(block, "seq", [(member, (member + shift) % count) for member in range(count)])
+
+
+def all_four(block):
+    beside = across(block, 1)
+    over = across(block, 2)
+    return [block, beside, over, across(over, 1)]
+
+
+def fits(tile_rows, qkv_weight):
+    in_rows = tile_rows.shape[0]
+    seq_count, head_count = lax.axis_size("seq"), lax.axis_size("head")
+    heads_here, head_dim = qkv_weight.shape[1], qkv_weight.shape[3]
+    rows_here = in_rows * head_count
+    total_rows = rows_here * seq_count
+    segments = [total_rows // fraction for fraction in FRACTIONS]
+    return (
+        segments == [in_rows, rows_here, total_rows]
+        and head_count == 4
+        and seq_count <= 8
+        and heads_here == DILATIONS[1] == DILATIONS[2] // DILATIONS[1]
+        and in_rows == 4 * HALF
+        and head_dim % 16 == 0
+        and head_dim < HALF
+    )
+
+
+def fast(tile_rows, tile_route, embed_weight, norm_gain, qkv_weight, out_weight):
+    seq_count = lax.axis_size("seq")
+    in_rows = tile_rows.shape[0]
+    width = embed_weight.shape[1]
+    heads_here, head_dim = qkv_weight.shape[1], qkv_weight.shape[3]
+    blocks, slots = pack(tile_rows, embed_weight, tile_route, seq_count)
+    order = sorted(range(1, seq_count), key=lambda shift: -min(shift, seq_count - shift))
+    moved_slots = [shifted(slots[shift], shift) for shift in order]
+    moved = [shifted(blocks[shift], shift) for shift in order]
+    pieces = all_four(out_weight)
+    by_kind = jnp.transpose(qkv_weight, (0, 2, 1, 3))
+    weight = jnp.pad(by_kind, ((0, 0), (0, 0), (0, 0), (0, HALF - head_dim))).reshape(width, -1)
+    rows, normed = land([blocks[0]] + moved, [slots[0]] + moved_slots, norm_gain, in_rows)
+    one, two, three, four = all_four(normed)
+    turned, turned_weight = turn(rows, pieces)
+    first = first_qkv(one, two, weight, head_dim)
+    second, far = second_qkv(three, four, weight, first, head_dim, heads_here)
+    fars = [far] + [shifted(far, shift) for shift in order]
+    parts = attention_blocks(first, second, fars, head_dim, heads_here)
+    joined = [parts[0]] + [across(parts[bit], bit) for bit in range(1, 4)]
+    return finish(turned, turned_weight, joined)
+
+
+def local(tile_rows, tile_route, embed_weight, norm_gain, qkv_weight, out_weight):
+    run = fast if fits(tile_rows, qkv_weight) else general
+    return run(tile_rows, tile_route, embed_weight, norm_gain, qkv_weight, out_weight)
+
+
 def solution(mesh):
     return jax.shard_map(
         local,

time: 306 us -> 91.3 us (0.30); the launches traced: 302 us -> 91 us
  local copies, waits for them, and re-layouts: 167 us -> 6.64 us
  matrix products: 35.9 us -> 0 us
  Pallas kernels: 0 us -> 27.2 us
  other arithmetic: 20.1 us -> 0 us
  between operations: 14.1 us -> 0.13 us
  waiting for transfers between devices: 46.7 us -> 35.3 us
  starting transfers between devices: 17.3 us -> 21.7 us
    broadcast_in_dim x48 -> x0, local copies, waits for them, and re-layouts: 41.8 us -> none  [the longest x16 26.5 us: expand_rows(): jnp.where(pick_mask[None, :, None], head_out[:, None, :], 0.0)]
    dynamic_update_slice x48 -> x0, local copies, waits for them, and re-layouts: 38.2 us -> none  [local(): lax.map(lambda block_in: attend(block_in[0], block_in[1][:, 0], block_in[...]
    dot_general x52 -> x0, matrix products: 35.9 us -> none  [the longest x24 17.1 us: attend_block(): jnp.dot(queries, key_rows.T, preferred_element_type=jnp.float32)]
    ppermute x2 -> x18, waiting for transfers between devices: 5.17 us -> 35.3 us  [the longest x9 19.4 us: shifted(): lax.ppermute(block, 'seq', [(member, (member + shift) % count) for member...]
    all_to_all x3 -> x0, waiting for transfers between devices: 28.5 us -> none  [the longest x1 18.9 us: local(): lax.all_to_all(outgoing.reshape(seq_count, capacity, width), 'seq', split...]
    another operation x18 -> x0, local copies, waits for them, and re-layouts: 28.1 us -> none  [the longest x2 21 us: local(): shaped = qkv.reshape(count, dilation, heads_here, 3, head_dim)]
    pallas_call x0 -> x7, Pallas kernels: none -> 27.2 us  [the longest x1 6.62 us: attention_blocks(): pl.pallas_call(functools.partial(attention_kernel, head_dim, heads_here),...]
    squeeze x21 -> x0, local copies, waits for them, and re-layouts: 19.3 us -> none  [the longest x18 13.5 us: local(): lax.map(lambda block_in: attend(block_in[0], block_in[1][:, 0], block_in[...]
  transfers between devices with their start and end apart: 7 -> 18, of which waited for: 5 -> 8; matrix products, arithmetic and copies ran while one was open for 70% -> 2% of each run, Pallas kernels for 0% -> 18%
where the time goes in v1:
time: 91.3 us; the launch traced here: 91 us
  waiting for transfers between devices  35.3 us (39%)
  Pallas kernels  27.2 us (30%)
  starting transfers between devices  21.7 us (24%)
  local copies, waits for them, and re-layouts  6.64 us (7%)
    ppermute x9, waiting for transfers between devices, shifted(): lax.ppermute(block, 'seq', [(member, (member + shift) % count) for member...  19.4 us
    ppermute x9, starting transfers between devices, shifted(): lax.ppermute(block, 'seq', [(member, (member + shift) % count) for member...  16.6 us
    ppermute x9, waiting for transfers between devices, across(): lax.ppermute(block, 'head', [(member, member ^ bit) for member in range(c...  15.9 us
    pallas_call x1, Pallas kernels, attention_blocks(): pl.pallas_call(functools.partial(attention_kernel, head_dim, heads_here),...  6.62 us
    pallas_call x1, Pallas kernels, pack(): pl.pallas_call(functools.partial(pack_kernel, seq_count), grid=(width //...  5.12 us
    ppermute x9, starting transfers between devices, across(): lax.ppermute(block, 'head', [(member, member ^ bit) for member in range(c...  5.08 us
    unnamed x43, local copies, waits for them, and re-layouts  4.48 us
    pallas_call x1, Pallas kernels, second_qkv(): pl.pallas_call(functools.partial(second_qkv_kernel, head_dim, heads_here)...  3.43 us
  transfers between devices with their start and end apart: 18, of which 8 were waited for; matrix products, arithmetic and copies ran while one was open for 2% of the time, Pallas kernels for 18%

profile of v1, /device:TPU:0, one launch (start us, length us, event | category | flops | bytes accessed | tf_op | source)
XLA Modules:
  0.0 91.0 jit_solution(17194659530420278396)
XLA Ops:
  0.0 5.1 %pack.1 = (bf16[128,768]{1,0:T(8,128)(2,1)}, bf16[128,768]{1,0:T(8,128)(2,1)}, bf16[128,768]{1,0:T(8,128)(2,1)}, bf16[128,768]{1,0:T(8,128)(2,1)}, s32[1,128]{1,...) custom-call(bf16[256,1536]{1,0:T(8,128)(2,1)} %rows_ref.1, bf16[1536,768]{1,0:T(8,128)(2,1)} %weight_ref.1, ...), custom_call_target="tpu_custom_call" | custom-call | flops 805306368 | bytes 1048576 | tf_op jit(solution)/shard_map/pack/pallas_call | solution.py:249
  5.1 4.1 %collective-permute-start = (bf16[128,768]{1,0:T(8,128)(2,1)}, bf16[128,768]{1,0:T(8,128)(2,1)S(1)}, u32[]{:S(2)}, u32[]{:S(2)}) collective-permute-start(bf16[128,768]{1,0:T(8,128)(2,1)} %get-tuple-element.24), channel_id=1, source_target_pairs={{0,8},{4,12},{8,0},{12,4},{1,9},{5,13},{9,1},{13,5},{2,10},{6,14},... | collective-permute-start | bytes 589832 | tf_op jit(solution)/shard_map/ppermute | solution.py:508
  9.2 1.6 %collective-permute-start.1 = (bf16[128,768]{1,0:T(8,128)(2,1)}, bf16[128,768]{1,0:T(8,128)(2,1)S(1)}, u32[]{:S(2)}, u32[]{:S(2)}) collective-permute-start(bf16[128,768]{1,0:T(8,128)(2,1)} %get-tuple-element.25), channel_id=1, source_target_pairs={{0,4},{4,8},{8,12},{12,0},{1,5},{5,9},{9,13},{13,1},{2,6},{6,10},{... | collective-permute-start | bytes 589832 | tf_op jit(solution)/shard_map/ppermute | solution.py:508
  10.8 2.2 %collective-permute-start.2 = (bf16[128,768]{1,0:T(8,128)(2,1)}, bf16[128,768]{1,0:T(8,128)(2,1)S(1)}, u32[]{:S(2)}, u32[]{:S(2)}) collective-permute-start(bf16[128,768]{1,0:T(8,128)(2,1)} %get-tuple-element.26), channel_id=1, source_target_pairs={{0,12},{4,0},{8,4},{12,8},{1,13},{5,1},{9,5},{13,9},{2,14},{6,2},{... | collective-permute-start | bytes 589832 | tf_op jit(solution)/shard_map/ppermute | solution.py:508
  13.6 13.4 %collective-permute-done.3.refs_5_ = s32[1,128]{1,0:T(1,128)S(1)} collective-permute-done((s32[1,128]{1,0:T(1,128)}, s32[1,128]{1,0:T(1,128)S(1)}, u32[]{:S(2)}, u32[]{:S(2)}) %collective-permute-start.3) | collective-permute-done | bytes 544 | tf_op jit(solution)/shard_map/ppermute | solution.py:508
  27.1 3.5 %collective-permute-start.5 = (s32[1,128]{1,0:T(1,128)}, s32[1,128]{1,0:T(1,128)S(1)}, u32[]{:S(2)}, u32[]{:S(2)}) collective-permute-start(s32[1,128]{1,0:T(1,128)} %get-tuple-element.30), channel_id=1, source_target_pairs={{0,12},{4,0},{8,4},{12,8},{1,13},{5,1},{9,5},{13,9},{2,14},{6,2},{... | collective-permute-start | bytes 1544 | tf_op jit(solution)/shard_map/ppermute | solution.py:508
  32.8 2.7 %land.1 = (bf16[256,768]{1,0:T(8,128)(2,1)}, bf16[256,768]{1,0:T(8,128)(2,1)}) custom-call(bf16[128,768]{1,0:T(8,128)(2,1)} %get-tuple-element.23.refs_0_, bf16[128,768]{1,0:T(8,128)(2,1)} %copy-done.8, bf16[128,768]{1,0:T(8,128)(2,1)} %copy-done.9, bf16[128,768]{1,0:T(8,128)(2,1)} %copy-done.10, s32[1,128]{1,0:T(1,128)} %get-tuple-element.27.refs_4_, ...), custom_call_target="tpu_custom_call" | custom-call | flops 201326592 | bytes 1048576 | tf_op jit(solution)/shard_map/land/pallas_call | solution.py:289
  35.5 1.5 %collective-permute-start.10 = (bf16[256,768]{1,0:T(8,128)(2,1)}, bf16[256,768]{1,0:T(8,128)(2,1)S(1)}, u32[]{:S(2)}, u32[]{:S(2)}) collective-permute-start(bf16[256,768]{1,0:T(8,128)(2,1)} %get-tuple-element.34.one_ref), channel_id=1, source_target_pairs={{0,2},{1,3},{2,0},{3,1},{4,6},{5,7},{6,4},{7,5},{8,10},{9,11},{10,... | collective-permute-start | bytes 1179656 | tf_op jit(solution)/shard_map/ppermute | solution.py:503
  37.0 8.7 %collective-permute-done.10.one_ref = bf16[256,768]{1,0:T(8,128)(2,1)S(1)} collective-permute-done((bf16[256,768]{1,0:T(8,128)(2,1)}, bf16[256,768]{1,0:T(8,128)(2,1)S(1)}, u32[]{:S(2)}, u32[]{:S(2)}) %collective-permute-start.10) | collective-permute-done | bytes 393248 | tf_op jit(solution)/shard_map/ppermute | solution.py:503
  45.8 1.6 %collective-permute-start.7 = (bf16[192,768]{1,0:T(8,128)(2,1)S(1)}, bf16[192,768]{1,0:T(8,128)(2,1)S(1)}, u32[]{:S(2)}, u32[]{:S(2)}) collective-permute-start(bf16[192,768]{1,0:T(8,128)(2,1)S(1)} %copy-done.4), channel_id=1, source_target_pairs={{0,2},{1,3},{2,0},{3,1},{4,6},{5,7},{6,4},{7,5},{8,10},{9,11},{10,... | collective-permute-start | bytes 884744 | tf_op jit(solution)/shard_map/ppermute | solution.py:503
  47.7 1.5 %copy.9.weight_ref = bf16[768,768]{1,0:T(8,128)(2,1)} copy(bf16[768,768]{0,1:T(8,128)(2,1)S(1)} %bitcast.5) | data formatting | bytes 2359296 | tf_op jit(solution)/shard_map/reshape | solution.py:546
  49.1 6.0 %collective-permute-done.7.refs_2_ = bf16[192,768]{1,0:T(8,128)(2,1)S(1)} collective-permute-done((bf16[192,768]{1,0:T(8,128)(2,1)S(1)}, bf16[192,768]{1,0:T(8,128)(2,1)S(1)}, u32[]{:S(2)}, u32[]{:S(2)}) %collective-permute-start.7) | collective-permute-done | bytes 294944 | tf_op jit(solution)/shard_map/ppermute | solution.py:503
  55.2 0.8 copy-done.3
  56.0 3.2 %first_qkv.1.first_ref = bf16[512,768]{1,0:T(8,128)(2,1)} custom-call(bf16[256,768]{1,0:T(8,128)(2,1)} %get-tuple-element.34.one_ref, bf16[256,768]{1,0:T(8,128)(2,1)} %copy-done.3, bf16[768,768]{1,0:T(8,128)(2,1)} %copy.9.weight_ref), custom_call_target="tpu_custom_call" | custom-call | flops 603979776 | bytes 1048576 | tf_op jit(solution)/shard_map/first_qkv/pallas_call | solution.py:363
  59.9 3.4 %second_qkv.1 = (bf16[512,768]{1,0:T(8,128)(2,1)}, bf16[64,512]{1,0:T(8,128)(2,1)}) custom-call(bf16[256,768]{1,0:T(8,128)(2,1)} %copy-done.1, bf16[256,768]{1,0:T(8,128)(2,1)} %copy-done.2, bf16[768,768]{1,0:T(8,128)(2,1)} %copy.9.weight_ref, bf16[512,768]{1,0:T(8,128)(2,1)} %first_qkv.1.first_ref), custom_call_target="tpu_custom_call" | custom-call | flops 603979776 | bytes 1048576 | tf_op jit(solution)/shard_map/second_qkv/pallas_call | solution.py:373
  63.3 0.8 collective-permute-start.12
  64.1 3.5 %collective-permute-start.13 = (bf16[64,512]{1,0:T(8,128)(2,1)}, bf16[64,512]{1,0:T(8,128)(2,1)S(1)}, u32[]{:S(2)}, u32[]{:S(2)}) collective-permute-start(bf16[64,512]{1,0:T(8,128)(2,1)} %get-tuple-element.36.refs_0_), channel_id=1, source_target_pairs={{0,4},{4,8},{8,12},{12,0},{1,5},{5,9},{9,13},{13,1},{2,6},{6,10},{... | collective-permute-start | bytes 196616 | tf_op jit(solution)/shard_map/ppermute | solution.py:508
  68.0 3.9 %collective-permute-done.12.refs_1_ = bf16[64,512]{1,0:T(8,128)(2,1)S(1)} collective-permute-done((bf16[64,512]{1,0:T(8,128)(2,1)}, bf16[64,512]{1,0:T(8,128)(2,1)S(1)}, u32[]{:S(2)}, u32[]{:S(2)}) %collective-permute-start.12) | collective-permute-done | bytes 65568 | tf_op jit(solution)/shard_map/ppermute | solution.py:508
  71.9 1.2 %collective-permute-done.14.refs_3_ = bf16[64,512]{1,0:T(8,128)(2,1)S(1)} collective-permute-done((bf16[64,512]{1,0:T(8,128)(2,1)}, bf16[64,512]{1,0:T(8,128)(2,1)S(1)}, u32[]{:S(2)}, u32[]{:S(2)}) %collective-permute-start.14) | collective-permute-done | bytes 65568 | tf_op jit(solution)/shard_map/ppermute | solution.py:508
  73.7 6.6 %attention.1 = (bf16[192,256]{1,0:T(8,128)(2,1)}, bf16[192,256]{1,0:T(8,128)(2,1)}, bf16[192,256]{1,0:T(8,128)(2,1)}, bf16[192,256]{1,0:T(8,128)(2,1)}) custom-call(bf16[512,768]{1,0:T(8,128)(2,1)} %first_qkv.1.first_ref, bf16[512,768]{1,0:T(8,128)(2,1)} %get-tuple-element.35.second_ref, bf16[64,512]{1,0:T(8,128)(2,1)} %get-tuple-element.36.refs_0_, ...), custom_call_target="tpu_custom_call" | custom-call | flops 805306368 | bytes 1048576 | tf_op jit(solution)/shard_map/attention/pallas_call | solution.py:472
  80.4 1.5 %collective-permute-start.16 = (bf16[192,256]{1,0:T(8,128)(2,1)}, bf16[192,256]{1,0:T(8,128)(2,1)S(1)}, u32[]{:S(2)}, u32[]{:S(2)}) collective-permute-start(bf16[192,256]{1,0:T(8,128)(2,1)} %get-tuple-element.39), channel_id=1, source_target_pairs={{0,2},{1,3},{2,0},{3,1},{4,6},{5,7},{6,4},{7,5},{8,10},{9,11},{10,... | collective-permute-start | bytes 294920 | tf_op jit(solution)/shard_map/ppermute | solution.py:503
  83.1 3.2 %turn.1 = (bf16[768,256]{1,0:T(8,128)(2,1)}, bf16[768,768]{1,0:T(8,128)(2,1)}) custom-call(bf16[256,768]{1,0:T(8,128)(2,1)} %get-tuple-element.31.rows_ref, bf16[192,768]{1,0:T(8,128)(2,1)} %refs_0_.1, bf16[192,768]{1,0:T(8,128)(2,1)} %copy-done.6, bf16[192,768]{1,0:T(8,128)(2,1)} %copy-done.5, bf16[192,768]{1,0:T(8,128)(2,1)} %copy-done.7), custom_call_target="tpu_custom_call" | custom-call | flops 201326592 | bytes 1048576 | tf_op jit(solution)/shard_map/turn/pallas_call | solution.py:309
  86.3 1.0 %collective-permute-done.17.refs_3_ = bf16[192,256]{1,0:T(8,128)(2,1)S(1)} collective-permute-done((bf16[192,256]{1,0:T(8,128)(2,1)}, bf16[192,256]{1,0:T(8,128)(2,1)S(1)}, u32[]{:S(2)}, u32[]{:S(2)}) %collective-permute-start.17) | collective-permute-done | bytes 98336 | tf_op jit(solution)/shard_map/ppermute | solution.py:503
  88.0 3.0 %finish.1 = bf16[256,768]{1,0:T(8,128)(2,1)} custom-call(bf16[768,256]{1,0:T(8,128)(2,1)} %get-tuple-element.32.turned_ref, bf16[768,768]{1,0:T(8,128)(2,1)} %get-tuple-element.33.weight_ref, bf16[192,256]{1,0:T(8,128)(2,1)} %get-tuple-element.37.refs_0_, bf16[192,256]{1,0:T(8,128)(2,1)} %copy-done.11, bf16[192,256]{1,0:T(8,128)(2,1)} %copy-done.12, ...), custom_call_target="tpu_custom_call" | custom-call | flops 402653184 | bytes 1048576 | tf_op jit(solution)/shard_map/finish/pallas_call | solution.py:493
  (65 shorter events, 6.6 us)
Async XLA Ops:
  0.0 30.6 %copy-start.14 = (f32[768]{0:T(1024)S(1)}, f32[768]{0:T(1024)}, u32[]{:S(2)}) copy-start(f32[768]{0:T(1024)} %param.9) | copy-start | bytes 9220
  0.0 45.7 %copy-start.4 = (bf16[192,768]{1,0:T(8,128)(2,1)S(1)}, bf16[192,768]{1,0:T(8,128)(2,1)}, u32[]{:S(2)}) copy-start(bf16[192,768]{1,0:T(8,128)(2,1)} %refs_0_.1) | copy-start | bytes 884740
  0.0 47.5 %copy-start = (bf16[768,4,3,48]{0,3,2,1:T(8,128)(2,1)S(1)}, bf16[768,4,3,48]{0,3,2,1:T(8,128)(2,1)}, u32[]{:S(2)}) copy-start(bf16[768,4,3,48]{0,3,2,1:T(8,128)(2,1)} %param.10) | copy-start | bytes 2654212
  5.1 26.8 %collective-permute-start = (bf16[128,768]{1,0:T(8,128)(2,1)}, bf16[128,768]{1,0:T(8,128)(2,1)S(1)}, u32[]{:S(2)}, u32[]{:S(2)}) collective-permute-start(bf16[128,768]{1,0:T(8,128)(2,1)} %get-tuple-element.24), channel_id=1, source_target_pairs={{0,8},{4,12},{8,0},{12,4},{1,9},{5,13},{9,1},{13,5},{2,10},{6,14},... | collective-permute-start | bytes 589832 | tf_op jit(solution)/shard_map/ppermute | solution.py:508
  9.2 22.7 %collective-permute-start.1 = (bf16[128,768]{1,0:T(8,128)(2,1)}, bf16[128,768]{1,0:T(8,128)(2,1)S(1)}, u32[]{:S(2)}, u32[]{:S(2)}) collective-permute-start(bf16[128,768]{1,0:T(8,128)(2,1)} %get-tuple-element.25), channel_id=1, source_target_pairs={{0,4},{4,8},{8,12},{12,0},{1,5},{5,9},{9,13},{13,1},{2,6},{6,10},{... | collective-permute-start | bytes 589832 | tf_op jit(solution)/shard_map/ppermute | solution.py:508
  10.8 21.1 %collective-permute-start.2 = (bf16[128,768]{1,0:T(8,128)(2,1)}, bf16[128,768]{1,0:T(8,128)(2,1)S(1)}, u32[]{:S(2)}, u32[]{:S(2)}) collective-permute-start(bf16[128,768]{1,0:T(8,128)(2,1)} %get-tuple-element.26), channel_id=1, source_target_pairs={{0,12},{4,0},{8,4},{12,8},{1,13},{5,1},{9,5},{13,9},{2,14},{6,2},{... | collective-permute-start | bytes 589832 | tf_op jit(solution)/shard_map/ppermute | solution.py:508
  13.1 14.0 %collective-permute-start.3 = (s32[1,128]{1,0:T(1,128)}, s32[1,128]{1,0:T(1,128)S(1)}, u32[]{:S(2)}, u32[]{:S(2)}) collective-permute-start(s32[1,128]{1,0:T(1,128)} %get-tuple-element.28), channel_id=1, source_target_pairs={{0,8},{4,12},{8,0},{12,4},{1,9},{5,13},{9,1},{13,5},{2,10},{6,14},... | collective-permute-start | bytes 1544 | tf_op jit(solution)/shard_map/ppermute | solution.py:508
  13.1 18.1 %collective-permute-start.4 = (s32[1,128]{1,0:T(1,128)}, s32[1,128]{1,0:T(1,128)S(1)}, u32[]{:S(2)}, u32[]{:S(2)}) collective-permute-start(s32[1,128]{1,0:T(1,128)} %get-tuple-element.29), channel_id=1, source_target_pairs={{0,4},{4,8},{8,12},{12,0},{1,5},{5,9},{9,13},{13,1},{2,6},{6,10},{... | collective-permute-start | bytes 1544 | tf_op jit(solution)/shard_map/ppermute | solution.py:508
  27.1 4.9 %copy-start.15 = (s32[1,128]{1,0:T(1,128)}, s32[1,128]{1,0:T(1,128)S(1)}, u32[]{:S(2)}) copy-start(s32[1,128]{1,0:T(1,128)S(1)} %collective-permute-done.3.refs_5_) | copy-start | bytes 1540
  27.1 4.8 %collective-permute-start.5 = (s32[1,128]{1,0:T(1,128)}, s32[1,128]{1,0:T(1,128)S(1)}, u32[]{:S(2)}, u32[]{:S(2)}) collective-permute-start(s32[1,128]{1,0:T(1,128)} %get-tuple-element.30), channel_id=1, source_target_pairs={{0,12},{4,0},{8,4},{12,8},{1,13},{5,1},{9,5},{13,9},{2,14},{6,2},{... | collective-permute-start | bytes 1544 | tf_op jit(solution)/shard_map/ppermute | solution.py:508
  35.5 10.2 %collective-permute-start.10 = (bf16[256,768]{1,0:T(8,128)(2,1)}, bf16[256,768]{1,0:T(8,128)(2,1)S(1)}, u32[]{:S(2)}, u32[]{:S(2)}) collective-permute-start(bf16[256,768]{1,0:T(8,128)(2,1)} %get-tuple-element.34.one_ref), channel_id=1, source_target_pairs={{0,2},{1,3},{2,0},{3,1},{4,6},{5,7},{6,4},{7,5},{8,10},{9,11},{10,... | collective-permute-start | bytes 1179656 | tf_op jit(solution)/shard_map/ppermute | solution.py:503
  37.0 18.2 %collective-permute-start.9 = (bf16[256,768]{1,0:T(8,128)(2,1)}, bf16[256,768]{1,0:T(8,128)(2,1)S(1)}, u32[]{:S(2)}, u32[]{:S(2)}) collective-permute-start(bf16[256,768]{1,0:T(8,128)(2,1)} %get-tuple-element.34.one_ref), channel_id=1, source_target_pairs={{0,1},{1,0},{2,3},{3,2},{4,5},{5,4},{6,7},{7,6},{8,9},{9,8},{10,11... | collective-permute-start | bytes 1179656 | tf_op jit(solution)/shard_map/ppermute | solution.py:503
  45.7 1.9 %copy-start.1 = (bf16[256,768]{1,0:T(8,128)(2,1)}, bf16[256,768]{1,0:T(8,128)(2,1)S(1)}, u32[]{:S(2)}) copy-start(bf16[256,768]{1,0:T(8,128)(2,1)S(1)} %collective-permute-done.10.one_ref) | copy-start | bytes 1179652
  45.7 13.4 %collective-permute-start.11 = (bf16[256,768]{1,0:T(8,128)(2,1)S(1)}, bf16[256,768]{1,0:T(8,128)(2,1)S(1)}, u32[]{:S(2)}, u32[]{:S(2)}) collective-permute-start(bf16[256,768]{1,0:T(8,128)(2,1)S(1)} %collective-permute-done.10.one_ref), channel_id=1, source_target_pairs={{0,1},{1,0},{2,3},{3,2},{4,5},{5,4},{6,7},{7,6},{8,9},{9,8},{10,11... | collective-permute-start | bytes 1179656 | tf_op jit(solution)/shard_map/ppermute | solution.py:503
  45.8 9.4 %collective-permute-start.7 = (bf16[192,768]{1,0:T(8,128)(2,1)S(1)}, bf16[192,768]{1,0:T(8,128)(2,1)S(1)}, u32[]{:S(2)}, u32[]{:S(2)}) collective-permute-start(bf16[192,768]{1,0:T(8,128)(2,1)S(1)} %copy-done.4), channel_id=1, source_target_pairs={{0,2},{1,3},{2,0},{3,1},{4,6},{5,7},{6,4},{7,5},{8,10},{9,11},{10,... | collective-permute-start | bytes 884744 | tf_op jit(solution)/shard_map/ppermute | solution.py:503
  47.3 34.9 %collective-permute-start.6 = (bf16[192,768]{1,0:T(8,128)(2,1)S(1)}, bf16[192,768]{1,0:T(8,128)(2,1)S(1)}, u32[]{:S(2)}, u32[]{:S(2)}) collective-permute-start(bf16[192,768]{1,0:T(8,128)(2,1)S(1)} %copy-done.4), channel_id=1, source_target_pairs={{0,1},{1,0},{2,3},{3,2},{4,5},{5,4},{6,7},{7,6},{8,9},{9,8},{10,11... | collective-permute-start | bytes 884744 | tf_op jit(solution)/shard_map/ppermute | solution.py:503
  55.2 25.2 %copy-start.5 = (bf16[192,768]{1,0:T(8,128)(2,1)}, bf16[192,768]{1,0:T(8,128)(2,1)S(1)}, u32[]{:S(2)}) copy-start(bf16[192,768]{1,0:T(8,128)(2,1)S(1)} %collective-permute-done.7.refs_2_) | copy-start | bytes 884740
  55.2 27.1 %collective-permute-start.8 = (bf16[192,768]{1,0:T(8,128)(2,1)S(1)}, bf16[192,768]{1,0:T(8,128)(2,1)S(1)}, u32[]{:S(2)}, u32[]{:S(2)}) collective-permute-start(bf16[192,768]{1,0:T(8,128)(2,1)S(1)} %collective-permute-done.7.refs_2_), channel_id=1, source_target_pairs={{0,1},{1,0},{2,3},{3,2},{4,5},{5,4},{6,7},{7,6},{8,9},{9,8},{10,11... | collective-permute-start | bytes 884744 | tf_op jit(solution)/shard_map/ppermute | solution.py:503
  63.3 8.5 %collective-permute-start.12 = (bf16[64,512]{1,0:T(8,128)(2,1)}, bf16[64,512]{1,0:T(8,128)(2,1)S(1)}, u32[]{:S(2)}, u32[]{:S(2)}) collective-permute-start(bf16[64,512]{1,0:T(8,128)(2,1)} %get-tuple-element.36.refs_0_), channel_id=1, source_target_pairs={{0,8},{4,12},{8,0},{12,4},{1,9},{5,13},{9,1},{13,5},{2,10},{6,14},... | collective-permute-start | bytes 196616 | tf_op jit(solution)/shard_map/ppermute | solution.py:508
  64.1 7.7 %collective-permute-start.13 = (bf16[64,512]{1,0:T(8,128)(2,1)}, bf16[64,512]{1,0:T(8,128)(2,1)S(1)}, u32[]{:S(2)}, u32[]{:S(2)}) collective-permute-start(bf16[64,512]{1,0:T(8,128)(2,1)} %get-tuple-element.36.refs_0_), channel_id=1, source_target_pairs={{0,4},{4,8},{8,12},{12,0},{1,5},{5,9},{9,13},{13,1},{2,6},{6,10},{... | collective-permute-start | bytes 196616 | tf_op jit(solution)/shard_map/ppermute | solution.py:508
  67.7 5.4 %collective-permute-start.14 = (bf16[64,512]{1,0:T(8,128)(2,1)}, bf16[64,512]{1,0:T(8,128)(2,1)S(1)}, u32[]{:S(2)}, u32[]{:S(2)}) collective-permute-start(bf16[64,512]{1,0:T(8,128)(2,1)} %get-tuple-element.36.refs_0_), channel_id=1, source_target_pairs={{0,12},{4,0},{8,4},{12,8},{1,13},{5,1},{9,5},{13,9},{2,14},{6,2},{... | collective-permute-start | bytes 196616 | tf_op jit(solution)/shard_map/ppermute | solution.py:508
  80.4 5.9 %collective-permute-start.15 = (bf16[192,256]{1,0:T(8,128)(2,1)}, bf16[192,256]{1,0:T(8,128)(2,1)S(1)}, u32[]{:S(2)}, u32[]{:S(2)}) collective-permute-start(bf16[192,256]{1,0:T(8,128)(2,1)} %get-tuple-element.38), channel_id=1, source_target_pairs={{0,1},{1,0},{2,3},{3,2},{4,5},{5,4},{6,7},{7,6},{8,9},{9,8},{10,11... | collective-permute-start | bytes 294920 | tf_op jit(solution)/shard_map/ppermute | solution.py:503
  80.4 5.9 %collective-permute-start.16 = (bf16[192,256]{1,0:T(8,128)(2,1)}, bf16[192,256]{1,0:T(8,128)(2,1)S(1)}, u32[]{:S(2)}, u32[]{:S(2)}) collective-permute-start(bf16[192,256]{1,0:T(8,128)(2,1)} %get-tuple-element.39), channel_id=1, source_target_pairs={{0,2},{1,3},{2,0},{3,1},{4,6},{5,7},{6,4},{7,5},{8,10},{9,11},{10,... | collective-permute-start | bytes 294920 | tf_op jit(solution)/shard_map/ppermute | solution.py:503
  81.9 5.4 %collective-permute-start.17 = (bf16[192,256]{1,0:T(8,128)(2,1)}, bf16[192,256]{1,0:T(8,128)(2,1)S(1)}, u32[]{:S(2)}, u32[]{:S(2)}) collective-permute-start(bf16[192,256]{1,0:T(8,128)(2,1)} %get-tuple-element.40), channel_id=1, source_target_pairs={{0,3},{1,2},{2,1},{3,0},{4,7},{5,6},{6,5},{7,4},{8,11},{9,10},{10,... | collective-permute-start | bytes 294920 | tf_op jit(solution)/shard_map/ppermute | solution.py:503
  (15 other events, 12.6 us)

commit v2 on v1

--- a/solution.py
+++ b/solution.py
@@ -5,7 +5,9 @@
 from jax import lax
 from jax.experimental import pallas as pl
 from jax.experimental.pallas import tpu as pltpu
+
 from jax.sharding import PartitionSpec as P
+
 
 EPSILON = 1e-05
 DILATIONS = (1, 4, 16)
@@ -137,8 +139,8 @@
     qkv = qkv.reshape(rows_here, heads_here, 3, head_dim)
     first_head = lax.axis_index("head") * heads_here
     total_rows = rows_here * seq_count
-    outputs = [[] for member in range(heads_here)]
-    totals = [[] for member in range(heads_here)]
+    outputs = [[] for _ in range(heads_here)]
+    totals = [[] for _ in range(heads_here)]
     for fraction, dilation in zip(FRACTIONS, DILATIONS):
         segment = total_rows // fraction
         per_segment = segment // dilation
@@ -209,15 +211,27 @@
     return slot % middle * (inner * run) + slot // middle % inner * run + slot // last
 
 
-def pack_kernel(seq_count, rows_ref, weight_ref, route_ref, *refs):
+def pack_kernel(seq_count, rows_hbm, weight_hbm, route_ref, *refs):
     blocks = refs[:seq_count]
-    slots = refs[seq_count : 2 * seq_count]
-    pick_ref = refs[-1]
+    picks = refs[seq_count:-3]
+    rows_ref, weight_ref, arrived = refs[-3:]
     in_rows = rows_ref.shape[0]
-    capacity = blocks[0].shape[0]
-
-    @pl.when(pl.program_id(0) == 0)
-    def _():
+    chunks, _, chunk = weight_ref.shape
+    capacity = 2 * in_rows // seq_count
+    first = weight_hbm.shape[1] - chunks * chunk if not picks else 0
+    rows_copy = pltpu.make_async_copy(rows_hbm, rows_ref, arrived.at[chunks])
+    rows_copy.start()
+    copies = []
+    for number in range(chunks):
+        columns = slice(first + number * chunk, first + (number + 1) * chunk)
+        copies.append(
+            pltpu.make_async_copy(
+                weight_hbm.at[:, columns], weight_ref.at[number], arrived.at[number]
+            )
+        )
+        copies[number].start()
+
+    if picks:
         me = lax.axis_index("seq")
         dest = route_ref[0:1, :]
         slot = route_ref[1:2, :]
@@ -227,42 +241,56 @@
         earlier = matmul(hits.astype(jnp.bfloat16), before)
         base = (iota((8, in_rows), 0) * capacity).astype(jnp.float32)
         place = jnp.sum(hits * (earlier + base), axis=0, keepdims=True).astype(jnp.int32)
-        pick = iota((seq_count * capacity, in_rows), 0) == place
-        pick_ref[...] = pick.astype(jnp.bfloat16)
+        pick = (iota((seq_count * capacity, in_rows), 0) == place).astype(jnp.bfloat16)
+        picks[0][...] = pick
         mark = (landed_place(slot, in_rows) + 1).astype(jnp.float32)
         marks = jnp.broadcast_to(mark, (8, in_rows)).astype(jnp.bfloat16)
-        found = matmul(marks, pick_ref[...], ((1,), (1,))).astype(jnp.int32)
+        found = matmul(marks, pick, ((1,), (1,))).astype(jnp.bfloat16)
         for number in range(seq_count):
-            slots[number][...] = found[0:1, number * capacity : (number + 1) * capacity]
-
-    projected = matmul(rows_ref[...], weight_ref[...]).astype(jnp.bfloat16)
-    packed = matmul(pick_ref[...], projected).astype(jnp.bfloat16)
-    for number in range(seq_count):
-        blocks[number][...] = packed[number * capacity : (number + 1) * capacity]
-
-
-def pack(tile_rows, embed_weight, tile_route, seq_count):
+            spare = (blocks[number].shape[0] - capacity, blocks[number].shape[1])
+            blocks[number][capacity:] = jnp.zeros(spare, jnp.bfloat16)
+            blocks[number][capacity : capacity + 8, :capacity] = found[
+                :, number * capacity : (number + 1) * capacity
+            ]
+    else:
+        pick = route_ref[...]
+
+    rows_copy.wait()
+    for step in range(chunks):
+        copies[step].wait()
+        projected = matmul(rows_ref[...], weight_ref[step]).astype(jnp.bfloat16)
+        packed = matmul(pick, projected).astype(jnp.bfloat16)
+        columns = slice(step * chunk, (step + 1) * chunk)
+        for number in range(seq_count):
+            blocks[number][:capacity, columns] = packed[number * capacity : (number + 1) * capacity]
+
+
+def pack(tile_rows, embed_weight, route, columns, seq_count):
     in_rows, depth = tile_rows.shape
-    width = embed_weight.shape[1]
     capacity = 2 * in_rows // seq_count
     chunk = 256
+    lead = route.dtype == jnp.int32
+    hbm = pl.BlockSpec(memory_space=pltpu.HBM)
+    rows = capacity + 8 if lead else capacity
+    shapes = [jax.ShapeDtypeStruct((rows, columns), jnp.bfloat16)] * seq_count
+    if lead:
+        shapes.append(jax.ShapeDtypeStruct((seq_count * capacity, in_rows), jnp.bfloat16))
     results = pl.pallas_call(
         functools.partial(pack_kernel, seq_count),
-        grid=(width // chunk,),
-        in_specs=[
-            pl.BlockSpec((in_rows, depth), lambda step: (0, 0)),
-            pl.BlockSpec((depth, chunk), lambda step: (0, step)),
-            pl.BlockSpec((2, in_rows), lambda step: (0, 0)),
+        in_specs=[hbm, hbm, pl.BlockSpec(memory_space=pltpu.VMEM)],
+        out_shape=shapes,
+        scratch_shapes=[
+            pltpu.VMEM((in_rows, depth), jnp.bfloat16),
+            pltpu.VMEM((columns // chunk, depth, chunk), jnp.bfloat16),
+            pltpu.SemaphoreType.DMA((columns // chunk + 1,)),
         ],
-        out_specs=[pl.BlockSpec((capacity, chunk), lambda step: (0, step))] * seq_count
-        + [pl.BlockSpec((1, capacity), lambda step: (0, 0))] * seq_count,
-        out_shape=[jax.ShapeDtypeStruct((capacity, width), jnp.bfloat16)] * seq_count
-        + [jax.ShapeDtypeStruct((1, capacity), jnp.int32)] * seq_count,
-        scratch_shapes=[pltpu.VMEM((seq_count * capacity, in_rows), jnp.bfloat16)],
-        cost_estimate=cost(2 * in_rows * width * (depth + seq_count * capacity)),
-        name="pack",
-    )(tile_rows, embed_weight, tile_route.T)
-    return results[:seq_count], results[seq_count:]
+        cost_estimate=cost(2 * in_rows * columns * (depth + seq_count * capacity)),
+        compiler_params=pltpu.CompilerParams(vmem_limit_bytes=62 << 20),
+    )(tile_rows, embed_weight, route)
+    return results[:seq_count], results[-1]
+
+
+LIMIT = pltpu.CompilerParams(vmem_limit_bytes=16 << 20)
 
 
 def cost(flops):
@@ -270,51 +298,79 @@
 
 
 def land_kernel(count, *refs):
-    blocks, slots = refs[:count], refs[count : 2 * count]
-    gain_ref, rows_ref, normed_ref = refs[2 * count :]
+    blocks = refs[:count]
+    rows_ref, here_ref = refs[count:]
     in_rows = rows_ref.shape[0]
+    capacity = 2 * in_rows // count
+    rows = jnp.zeros(rows_ref.shape, jnp.float32)
+    for number, block in enumerate(blocks):
+        slot = block[capacity : capacity + 8, :capacity].astype(jnp.float32)[:1]
+        here = ((iota((in_rows, capacity), 0) + 1).astype(jnp.float32) == slot).astype(jnp.bfloat16)
+        here_ref[:, number * capacity : (number + 1) * capacity] = here
+        rows = rows + matmul(here, block[:capacity])
+    rows_ref[...] = rows.astype(jnp.bfloat16)
+
+
+def land(blocks, in_rows):
+    count = len(blocks)
+    capacity = 2 * in_rows // count
+    width = blocks[0].shape[1]
+    return pl.pallas_call(
+        functools.partial(land_kernel, count),
+        out_shape=[
+            jax.ShapeDtypeStruct((in_rows, width), jnp.bfloat16),
+            jax.ShapeDtypeStruct((in_rows, count * capacity), jnp.bfloat16),
+        ],
+        cost_estimate=cost(2 * in_rows * width * count * capacity),
+        compiler_params=LIMIT,
+        name="land_lead",
+    )(*blocks)
+
+
+def land_more_kernel(here_ref, *refs):
+    blocks, rows_ref = refs[:-1], refs[-1]
     capacity = blocks[0].shape[0]
     rows = jnp.zeros(rows_ref.shape, jnp.float32)
-    for block, slot in zip(blocks, slots):
-        here = (iota((in_rows, capacity), 0) + 1 == slot[...]).astype(jnp.bfloat16)
+    for number, block in enumerate(blocks):
+        here = here_ref[:, number * capacity : (number + 1) * capacity]
         rows = rows + matmul(here, block[...])
     rows_ref[...] = rows.astype(jnp.bfloat16)
-    normed_ref[...] = layer_norm(rows, gain_ref[...])
-
-
-def land(blocks, slots, norm_gain, in_rows):
-    count = len(blocks)
-    capacity, width = blocks[0].shape
-    shape = jax.ShapeDtypeStruct((in_rows, width), jnp.bfloat16)
+
+
+def land_more(here, blocks):
+    in_rows, total = here.shape
+    width = blocks[0].shape[1]
     return pl.pallas_call(
-        functools.partial(land_kernel, count),
-        out_shape=[shape, shape],
-        cost_estimate=cost(2 * in_rows * width * count * capacity),
-        name="land",
-    )(*blocks, *slots, norm_gain.reshape(1, width))
-
-
-def turn_kernel(rows_ref, *refs):
-    pieces = refs[:-2]
-    turned_ref, weight_ref = refs[-2:]
-    turned_ref[...] = rows_ref[...].T
-    depth = pieces[0].shape[0]
-    for number, piece in enumerate(pieces):
-        weight_ref[:, number * depth : (number + 1) * depth] = piece[...].T
-
-
-def turn(rows, pieces):
-    width = rows.shape[1]
-    inner = sum(piece.shape[0] for piece in pieces)
+        land_more_kernel,
+        out_shape=jax.ShapeDtypeStruct((in_rows, width), jnp.bfloat16),
+        cost_estimate=cost(2 * in_rows * width * total),
+        compiler_params=LIMIT,
+        name="land_rest",
+    )(here, *blocks)
+
+
+def turn_kernel(down, *refs):
+    pieces, out_ref = refs[:-1], refs[-1]
+    start = 0
+    for piece in pieces:
+        depth = piece.shape[1 if down else 0]
+        if down:
+            out_ref[start : start + depth] = piece[...].T
+        else:
+            out_ref[:, start : start + depth] = piece[...].T
+        start += depth
+
+
+def turn(pieces, down):
+    rows = sum(piece.shape[0] for piece in pieces)
+    columns = sum(piece.shape[1] for piece in pieces)
+    shape = (columns, pieces[0].shape[0]) if down else (pieces[0].shape[1], rows)
     return pl.pallas_call(
-        turn_kernel,
-        out_shape=[
-            jax.ShapeDtypeStruct((width, rows.shape[0]), jnp.bfloat16),
-            jax.ShapeDtypeStruct((width, inner), jnp.bfloat16),
-        ],
-        cost_estimate=cost(2 * rows.shape[0] * width * 512),
-        name="turn",
-    )(rows, *pieces)
+        functools.partial(turn_kernel, down),
+        out_shape=jax.ShapeDtypeStruct(shape, jnp.bfloat16),
+        cost_estimate=cost(len(pieces) * 100_000_000),
+        compiler_params=LIMIT,
+    )(*pieces)
 
 
 def project_block(rows, weight, head_dim):
@@ -325,60 +381,65 @@
     return (out + ones.astype(jnp.float32)).astype(jnp.bfloat16)
 
 
-def first_qkv_kernel(head_dim, one_ref, two_ref, weight_ref, out_ref):
-    in_rows = one_ref.shape[0]
-    weight = weight_ref[...]
-    out_ref[:in_rows] = project_block(one_ref[...], weight, head_dim)
-    out_ref[in_rows:] = project_block(two_ref[...], weight, head_dim)
-
-
-def second_qkv_kernel(head_dim, heads_here, one_ref, two_ref, weight_ref, first_ref, out_ref, far_ref):
-    in_rows = one_ref.shape[0]
-    first_qkv_kernel(head_dim, one_ref, two_ref, weight_ref, out_ref)
+def qkv_kernel(head_dim, heads_here, lead_ref, rest_ref, gain_ref, weight_ref, out_ref, far_ref):
+    in_rows = lead_ref.shape[0]
+    rows = jnp.concatenate([lead_ref[...], rest_ref[...]], axis=1).astype(jnp.float32)
+    normed = layer_norm(rows, gain_ref[...])
+    out_ref[...] = project_block(normed, weight_ref[...], head_dim)
     middle, last = DILATIONS[1], DILATIONS[2]
     run = in_rows // last
     third = heads_here * HALF
     inner = lax.axis_index("head") % (last // middle)
     low = iota((1, 2 * HALF), 1) < HALF
-    for number in range(4):
-        source = first_ref if number < 2 else out_ref
-        start = number % 2 * in_rows
-        for part in range(2):
-            for pair in range(heads_here // 2):
-                column = (1 + part) * third + pair * 2 * HALF
-                both = []
-                for member in (2 * pair, 2 * pair + 1):
-                    row = start + member * (in_rows // middle) + inner * run
-                    both.append(
-                        source[pl.ds(pl.multiple_of(row, run), run), column : column + 2 * HALF]
-                    )
-                far_ref[
-                    number * run : (number + 1) * run,
-                    part * third + pair * 2 * HALF : part * third + (pair + 1) * 2 * HALF,
-                ] = jnp.where(low, both[0], both[1])
-
-
-def first_qkv(one, two, weight, head_dim):
-    in_rows, width = one.shape
+    for column in range(third, 3 * third, 2 * HALF):
+        both = []
+        for side in range(2):
+            member = column % third // HALF + side
+            row = member * (in_rows // middle) + inner * run
+            both.append(out_ref[pl.ds(pl.multiple_of(row, run), run), column : column + 2 * HALF])
+        far_ref[:, column - third : column - third + 2 * HALF] = jnp.where(low, both[0], both[1])
+
+
+def near_kernel(head_dim, heads_here, qkv_ref, out_ref):
+    in_rows = qkv_ref.shape[0]
+    third = heads_here * HALF
+    scale = LOG2E * head_dim ** (-0.5)
+    lanes = iota((1, 2 * HALF), 1)
+    for first in range(0, third, 2 * HALF):
+        keys = qkv_ref[:, third + first : third + first + 2 * HALF]
+        turned = qkv_ref[:, 2 * third + first : 2 * third + first + 2 * HALF].T
+        for side in range(2):
+            mine = (lanes // HALF == side).astype(jnp.bfloat16)
+            queries = qkv_ref[:, first : first + 2 * HALF] * mine
+            scores = matmul(keys, queries, ((1,), (1,)))
+            values = turned[side * HALF : (side + 1) * HALF]
+            total, top = softmax_product([scores], scale, [values])
+            start = first + side * HALF
+            out_ref[start : start + HALF] = total
+            out_ref[start + HALF - 8 : start + HALF] = jnp.broadcast_to(top, (8, in_rows))
+
+
+def qkv_of(halves, gain, weight, head_dim, heads_here):
+    in_rows = halves[0].shape[0]
     return pl.pallas_call(
-        functools.partial(first_qkv_kernel, head_dim),
-        out_shape=jax.ShapeDtypeStruct((2 * in_rows, weight.shape[1]), jnp.bfloat16),
-        cost_estimate=cost(4 * in_rows * width * weight.shape[1]),
-        name="first_qkv",
-    )(one, two, weight)
-
-
-def second_qkv(one, two, weight, first, head_dim, heads_here):
-    in_rows, width = one.shape
+        functools.partial(qkv_kernel, head_dim, heads_here),
+        out_shape=[
+            jax.ShapeDtypeStruct((in_rows, weight.shape[1]), jnp.bfloat16),
+            jax.ShapeDtypeStruct((in_rows // DILATIONS[2], 2 * heads_here * HALF), jnp.bfloat16),
+        ],
+        cost_estimate=cost(2 * in_rows * weight.shape[0] * weight.shape[1]),
+        compiler_params=LIMIT,
+    )(*halves, gain, weight)
+
+
+def near(qkv, head_dim, heads_here):
+    in_rows = qkv.shape[0]
     return pl.pallas_call(
-        functools.partial(second_qkv_kernel, head_dim, heads_here),
-        out_shape=[
-            jax.ShapeDtypeStruct((2 * in_rows, weight.shape[1]), jnp.bfloat16),
-            jax.ShapeDtypeStruct((4 * in_rows // DILATIONS[2], 2 * heads_here * HALF), jnp.bfloat16),
-        ],
-        cost_estimate=cost(4 * in_rows * width * weight.shape[1]),
-        name="second_qkv",
-    )(one, two, weight, first)
+        functools.partial(near_kernel, head_dim, heads_here),
+        out_shape=jax.ShapeDtypeStruct((heads_here * HALF, in_rows), jnp.float32),
+        cost_estimate=cost(heads_here * 8 * in_rows * in_rows * 128),
+        compiler_params=LIMIT,
+    )(qkv)
 
 
 def softmax_product(scores, scale, turned):
@@ -391,24 +452,24 @@
     return total, top
 
 
-def attention_kernel(head_dim, heads_here, first_ref, second_ref, *refs):
-    fars, outs = refs[:-4], refs[-4:]
-    in_rows = first_ref.shape[0] // 2
+LOG2E = 1.4426950408889634
+
+
+def wide_kernel(head_dim, heads_here, *refs):
+    sources, fars, nears, outs = refs[:4], refs[4:-8], refs[-8:-4], refs[-4:]
+    in_rows = sources[0].shape[0]
     middle, last = DILATIONS[1], DILATIONS[2]
     wide = in_rows // middle
     run = in_rows // last
     third = heads_here * HALF
-    scale = 1.4426950408889634 * head_dim ** (-0.5)
+    scale = LOG2E * head_dim ** (-0.5)
     inner = lax.axis_index("head") % (last // middle)
     lanes = iota((1, 2 * HALF), 1)
     chosen = iota((1, in_rows), 1) // run % (last // middle) == inner
-    sources = [(first_ref, 0), (first_ref, in_rows), (second_ref, 0), (second_ref, in_rows)]
     for pair in range(heads_here // 2):
         span = slice(pair * 2 * HALF, (pair + 1) * 2 * HALF)
         keys_at = slice(third + span.start, third + span.stop)
         values_at = slice(2 * third + span.start, 2 * third + span.stop)
-        block_keys = [source[start : start + in_rows, keys_at] for source, start in sources]
-        block_turned = [source[start : start + in_rows, values_at].T for source, start in sources]
         far_keys = jnp.concatenate([far[:, span] for far in fars], axis=0)
         far_turned = jnp.concatenate(
             [far[:, third + span.start : third + span.stop] for far in fars], axis=0
@@ -417,27 +478,22 @@
             member = 2 * pair + side
             mine = (lanes // HALF == side).astype(jnp.bfloat16)
             held = slice(side * HALF, (side + 1) * HALF)
-            picked = [
-                slice(start + member * wide, start + (member + 1) * wide) for _, start in sources
-            ]
+            picked = slice(member * wide, (member + 1) * wide)
 
             def gathered(columns):
-                return jnp.concatenate(
-                    [source[rows, columns] for (source, _), rows in zip(sources, picked)], axis=0
-                )
+                return jnp.concatenate([source[picked, columns] for source in sources], axis=0)
 
             picked_queries = gathered(span) * mine
-            near = matmul(gathered(keys_at), picked_queries, ((1,), (1,)))
-            far = matmul(far_keys, picked_queries, ((1,), (1,)))
-            far = jnp.where(chosen, far, -1e30)
+            middle_scores = matmul(gathered(keys_at), picked_queries, ((1,), (1,)))
+            far_scores = matmul(far_keys, picked_queries, ((1,), (1,)))
+            far_scores = jnp.where(chosen, far_scores, -1e30)
             wide_total, wide_top = softmax_product(
-                [near, far], scale, [gathered(values_at).T[held], far_turned[held]]
+                [middle_scores, far_scores], scale, [gathered(values_at).T[held], far_turned[held]]
             )
             for number in range(4):
-                source, start = sources[number]
-                queries = source[start : start + in_rows, span] * mine
-                scores = matmul(block_keys[number], queries, ((1,), (1,)))
-                total, top = softmax_product([scores], scale, [block_turned[number][held]])
+                base = member * HALF
+                total = nears[number][base : base + HALF]
+                top = nears[number][base + HALF - 8 : base + HALF][:1]
                 extra, extra_top = place_lanes(wide_total, wide_top, number, member, wide)
                 tile = member * wide // 128 * 128
                 at = slice(tile, tile + 128)
@@ -447,13 +503,11 @@
                 old = jnp.exp2((top[:, at] - peak) * scale)
                 new = jnp.exp2((extra_top - peak) * scale)
                 merged = total[:, at] * old + jnp.where(inside, extra * new, 0.0)
-                parts = []
+                rows = slice(member * head_dim, (member + 1) * head_dim)
                 for other in range(0, in_rows, 128):
-                    parts.append(merged if other == tile else total[:, other : other + 128])
-                rows = slice(member * head_dim, (member + 1) * head_dim)
-                for index, part in enumerate(parts):
+                    part = merged if other == tile else total[:, other : other + 128]
                     done = part[:head_dim] / part[head_dim : head_dim + 1]
-                    outs[number][rows, index * 128 : (index + 1) * 128] = done.astype(jnp.bfloat16)
+                    outs[number][rows, other : other + 128] = done.astype(jnp.bfloat16)
 
 
 def place_lanes(total, top, number, member, wide):
@@ -466,15 +520,16 @@
     return total, top
 
 
-def attention_blocks(first, second, fars, head_dim, heads_here):
-    in_rows = first.shape[0] // 2
+def attention_blocks(sources, fars, nears, head_dim, heads_here):
+    in_rows = sources[0].shape[0]
     out = jax.ShapeDtypeStruct((heads_here * head_dim, in_rows), jnp.bfloat16)
     return pl.pallas_call(
-        functools.partial(attention_kernel, head_dim, heads_here),
+        functools.partial(wide_kernel, head_dim, heads_here),
         out_shape=[out] * 4,
-        cost_estimate=cost(24 * 4 * in_rows * in_rows * 128),
-        name="attention",
-    )(first, second, *fars)
+        cost_estimate=cost(8 * 4 * in_rows * in_rows * 128),
+        compiler_params=LIMIT,
+        name="wide",
+    )(*sources, *fars, *nears)
 
 
 def finish_kernel(turned_ref, weight_ref, *refs):
@@ -494,6 +549,7 @@
         finish_kernel,
         out_shape=jax.ShapeDtypeStruct((in_rows, width), jnp.bfloat16),
         cost_estimate=cost(2 * in_rows * width * (width + in_rows)),
+        compiler_params=LIMIT,
         name="finish",
     )(turned, weight, *pieces)
 
@@ -505,13 +561,8 @@
 
 def shifted(block, shift):
     count = lax.axis_size("seq")
-    return lax.ppermute(block, "seq", [(member, (member + shift) % count) for member in range(count)])
-
-
-def all_four(block):
-    beside = across(block, 1)
-    over = across(block, 2)
-    return [block, beside, over, across(over, 1)]
+    pairs = [(member, (member + shift) % count) for member in range(count)]
+    return lax.ppermute(block, "seq", pairs)
 
 
 def fits(tile_rows, qkv_weight):
@@ -537,22 +588,53 @@
     in_rows = tile_rows.shape[0]
     width = embed_weight.shape[1]
     heads_here, head_dim = qkv_weight.shape[1], qkv_weight.shape[3]
-    blocks, slots = pack(tile_rows, embed_weight, tile_route, seq_count)
+    lead_width = LEAD * width // 3
+    route = tile_route.T
     order = sorted(range(1, seq_count), key=lambda shift: -min(shift, seq_count - shift))
-    moved_slots = [shifted(slots[shift], shift) for shift in order]
-    moved = [shifted(blocks[shift], shift) for shift in order]
-    pieces = all_four(out_weight)
+    lead, pick = pack(tile_rows, embed_weight, route, lead_width, seq_count)
+    lead_in = [lead[0]] + [shifted(lead[shift], shift) for shift in order]
+    rest, _ = pack(tile_rows, embed_weight, pick, width - lead_width, seq_count)
+    rest_in = [rest[0]] + [shifted(rest[shift], shift) for shift in order]
+    rest, out_weight, qkv_weight = lax.optimization_barrier((rest, out_weight, qkv_weight))
+    out_over = across(out_weight, 2)
+    out_pieces = [out_weight, across(out_weight, 1), out_over]
+    out_pieces.append(across(out_over, 1))
+    turned_weight = turn(out_pieces, False)
     by_kind = jnp.transpose(qkv_weight, (0, 2, 1, 3))
     weight = jnp.pad(by_kind, ((0, 0), (0, 0), (0, 0), (0, HALF - head_dim))).reshape(width, -1)
-    rows, normed = land([blocks[0]] + moved, [slots[0]] + moved_slots, norm_gain, in_rows)
-    one, two, three, four = all_four(normed)
-    turned, turned_weight = turn(rows, pieces)
-    first = first_qkv(one, two, weight, head_dim)
-    second, far = second_qkv(three, four, weight, first, head_dim, heads_here)
-    fars = [far] + [shifted(far, shift) for shift in order]
-    parts = attention_blocks(first, second, fars, head_dim, heads_here)
+    lead_in, turned_weight, weight = lax.optimization_barrier((lead_in, turned_weight, weight))
+    rows_lead, here = land(lead_in, in_rows)
+    lead_over = across(rows_lead, 2)
+    lead_beside = across(rows_lead, 1)
+    lead_both = across(lead_over, 1)
+    rows_rest = land_more(here, rest_in)
+    rest_over = across(rows_rest, 2)
+    rest_beside = across(rows_rest, 1)
+    gain = norm_gain.reshape(1, width)
+    sources, nears, fars = [], [], []
+
+    def step(halves):
+        qkv, far = qkv_of(halves, gain, weight, head_dim, heads_here)
+        sources.append(qkv)
+        nears.append(near(qkv, head_dim, heads_here))
+        return far
+
+    def spread(parts):
+        far = jnp.concatenate(parts, axis=0)
+        fars.extend([far] + [shifted(far, shift) for shift in order])
+
+    far_parts = [step([rows_lead, rows_rest]), step([lead_beside, rest_beside])]
+    spread(far_parts)
+    turned = turn([rows_lead, rows_rest], True)
+    rest_both = across(rest_over, 1)
+    far_parts = [step([lead_over, rest_over]), step([lead_both, rest_both])]
+    spread(far_parts)
+    parts = attention_blocks(sources, fars, nears, head_dim, heads_here)
     joined = [parts[0]] + [across(parts[bit], bit) for bit in range(1, 4)]
     return finish(turned, turned_weight, joined)
+
+
+LEAD = 2
 
 
 def local(tile_rows, tile_route, embed_weight, norm_gain, qkv_weight, out_weight):

time: 91.3 us -> 78.5 us (0.86)
  waiting for transfers between devices: 35.3 us -> 21.4 us
  starting transfers between devices: 21.7 us -> 31.3 us
  Pallas kernels: 27.2 us -> 21.2 us
  local copies, waits for them, and re-layouts: 6.64 us -> 3.99 us
    ppermute x9 -> x12, waiting for transfers between devices: 19.4 us -> 7.96 us  [shifted(): return lax.ppermute(block, 'seq', pairs)]
    ppermute x9 -> x12, starting transfers between devices: 16.6 us -> 23.5 us  [shifted(): return lax.ppermute(block, 'seq', pairs)]
    pallas_call x6 -> x15, Pallas kernels: 24.2 us -> 19.7 us  [the longest x2 8.19 us: pack(): pl.pallas_call(functools.partial(pack_kernel, seq_count), in_specs=[hbm,...]
    unnamed x43 -> x22, local copies, waits for them, and re-layouts: 4.48 us -> 0.05 us
    optimization_barrier x0 -> x2, local copies, waits for them, and re-layouts: none -> 2.79 us  [the longest x1 1.56 us: fast(): lax.optimization_barrier((lead_in, turned_weight, weight))]
    ppermute x9 -> x12, starting transfers between devices: 5.08 us -> 7.75 us  [across(): lax.ppermute(block, 'head', [(member, member ^ bit) for member in range(c...]
    ppermute x9 -> x12, waiting for transfers between devices: 15.9 us -> 13.4 us  [across(): lax.ppermute(block, 'head', [(member, member ^ bit) for member in range(c...]
    reshape x2 -> x1, local copies, waits for them, and re-layouts: 2.06 us -> 0.01 us  [fast(): gain = norm_gain.reshape(1, width)]
  transfers between devices with their start and end apart: 18 -> 24, of which waited for: 8 -> 9; matrix products, arithmetic and copies ran while one was open for 2% -> 5% of each run, Pallas kernels for 18% -> 12%
where the time goes in v2:
time: 78.5 us; the launch traced here: 78.2 us
  starting transfers between devices  31.3 us (40%)
  waiting for transfers between devices  21.4 us (27%)
  Pallas kernels  21.2 us (27%)
  local copies, waits for them, and re-layouts  3.99 us (5%)
    ppermute x12, starting transfers between devices, shifted(): return lax.ppermute(block, 'seq', pairs)  23.5 us
    ppermute x12, waiting for transfers between devices, across(): lax.ppermute(block, 'head', [(member, member ^ bit) for member in range(c...  13.4 us
    pallas_call x2, Pallas kernels, pack(): pl.pallas_call(functools.partial(pack_kernel, seq_count), in_specs=[hbm,...  8.19 us
    ppermute x12, waiting for transfers between devices, shifted(): return lax.ppermute(block, 'seq', pairs)  7.96 us
    ppermute x12, starting transfers between devices, across(): lax.ppermute(block, 'head', [(member, member ^ bit) for member in range(c...  7.75 us
    pallas_call x4, Pallas kernels, near(): pl.pallas_call(functools.partial(near_kernel, head_dim, heads_here), out_...  5.35 us
    pallas_call x4, Pallas kernels, qkv_of(): pl.pallas_call(functools.partial(qkv_kernel, head_dim, heads_here), out_s...  2.8 us
    pallas_call x1, Pallas kernels, attention_blocks(): pl.pallas_call(functools.partial(wide_kernel, head_dim, heads_here), out_...  1.84 us
  transfers between devices with their start and end apart: 24, of which 9 were waited for; matrix products, arithmetic and copies ran while one was open for 5% of the time, Pallas kernels for 12%

profile of v2, /device:TPU:0, one launch (start us, length us, event | category | flops | bytes accessed | tf_op | source)
XLA Modules:
  0.0 78.2 jit_solution(3818080373265144296)
XLA Ops:
  0.0 4.5 %shard_map.64 = (bf16[136,512]{1,0:T(8,128)(2,1)}, bf16[136,512]{1,0:T(8,128)(2,1)}, bf16[136,512]{1,0:T(8,128)(2,1)}, bf16[136,512]{1,0:T(8,128)(2,1)}, bf16[512,256]{1,0:T(8,128)(2,1)}) custom-call(bf16[256,1536]{1,0:T(8,128)(2,1)} %rows_hbm.3, bf16[1536,768]{1,0:T(8,128)(2,1)} %weight_hbm.3, s32[2,256]{1,0:T(2,128)} %bitcast.7), custom_call_target="tpu_custom_call" | custom-call | flops 536870912 | bytes 1048576 | tf_op jit(solution)/shard_map/pallas_call | solution.py:278
  4.5 3.7 %shard_map.65 = (bf16[128,256]{1,0:T(8,128)(2,1)}, bf16[128,256]{1,0:T(8,128)(2,1)}, bf16[128,256]{1,0:T(8,128)(2,1)}, bf16[128,256]{1,0:T(8,128)(2,1)}) custom-call(bf16[256,1536]{1,0:T(8,128)(2,1)} %rows_hbm.3, bf16[1536,768]{1,0:T(8,128)(2,1)} %weight_hbm.3, bf16[512,256]{1,0:T(8,128)(2,1)} %get-tuple-element.40.route_ref), custom_call_target="tpu_custom_call" | custom-call | flops 268435456 | bytes 1048576 | tf_op jit(solution)/shard_map/pallas_call | solution.py:278
  8.3 3.0 %collective-permute-start.4 = (bf16[192,768]{1,0:T(8,128)(2,1)S(1)}, bf16[192,768]{1,0:T(8,128)(2,1)S(1)}, u32[]{:S(2)}, u32[]{:S(2)}) collective-permute-start(bf16[192,768]{1,0:T(8,128)(2,1)S(1)} %copy-done), channel_id=1, source_target_pairs={{0,2},{1,3},{2,0},{3,1},{4,6},{5,7},{6,4},{7,5},{8,10},{9,11},{10,... | collective-permute-start | bytes 884744 | tf_op jit(solution)/shard_map/ppermute | solution.py:559
  11.3 7.0 %collective-permute-done.4.refs_2_ = bf16[192,768]{1,0:T(8,128)(2,1)S(1)} collective-permute-done((bf16[192,768]{1,0:T(8,128)(2,1)S(1)}, bf16[192,768]{1,0:T(8,128)(2,1)S(1)}, u32[]{:S(2)}, u32[]{:S(2)}) %collective-permute-start.4) | collective-permute-done | bytes 294944 | tf_op jit(solution)/shard_map/ppermute | solution.py:559
  18.3 2.8 %collective-permute-start = (bf16[136,512]{1,0:T(8,128)(2,1)S(1)}, bf16[136,512]{1,0:T(8,128)(2,1)S(1)}, u32[]{:S(2)}, u32[]{:S(2)}) collective-permute-start(bf16[136,512]{1,0:T(8,128)(2,1)S(1)} %copy-done.6), channel_id=1, source_target_pairs={{0,8},{4,12},{8,0},{12,4},{1,9},{5,13},{9,1},{13,5},{2,10},{6,14},... | collective-permute-start | bytes 417800 | tf_op jit(solution)/shard_map/ppermute | solution.py:565
  21.1 1.6 %collective-permute-start.1 = (bf16[136,512]{1,0:T(8,128)(2,1)S(1)}, bf16[136,512]{1,0:T(8,128)(2,1)S(1)}, u32[]{:S(2)}, u32[]{:S(2)}) collective-permute-start(bf16[136,512]{1,0:T(8,128)(2,1)S(1)} %copy-done.5), channel_id=1, source_target_pairs={{0,4},{4,8},{8,12},{12,0},{1,5},{5,9},{9,13},{13,1},{2,6},{6,10},{... | collective-permute-start | bytes 417800 | tf_op jit(solution)/shard_map/ppermute | solution.py:565
  22.7 2.3 %collective-permute-start.2 = (bf16[136,512]{1,0:T(8,128)(2,1)S(1)}, bf16[136,512]{1,0:T(8,128)(2,1)S(1)}, u32[]{:S(2)}, u32[]{:S(2)}) collective-permute-start(bf16[136,512]{1,0:T(8,128)(2,1)S(1)} %copy-done.4), channel_id=1, source_target_pairs={{0,12},{4,0},{8,4},{12,8},{1,13},{5,1},{9,5},{13,9},{2,14},{6,2},{... | collective-permute-start | bytes 417800 | tf_op jit(solution)/shard_map/ppermute | solution.py:565
  28.1 3.7 %collective-permute-done.refs_1_ = bf16[136,512]{1,0:T(8,128)(2,1)S(1)} collective-permute-done((bf16[136,512]{1,0:T(8,128)(2,1)S(1)}, bf16[136,512]{1,0:T(8,128)(2,1)S(1)}, u32[]{:S(2)}, u32[]{:S(2)}) %collective-permute-start) | collective-permute-done | bytes 139296 | tf_op jit(solution)/shard_map/ppermute | solution.py:565
  33.5 1.6 %collective-permute-start.11 = (bf16[256,512]{1,0:T(8,128)(2,1)S(1)}, bf16[256,512]{1,0:T(8,128)(2,1)S(1)}, u32[]{:S(2)}, u32[]{:S(2)}) collective-permute-start(bf16[256,512]{1,0:T(8,128)(2,1)S(1)} %get-tuple-element.51.refs_0_.lead_ref), channel_id=1, source_target_pairs={{0,2},{1,3},{2,0},{3,1},{4,6},{5,7},{6,4},{7,5},{8,10},{9,11},{10,... | collective-permute-start | bytes 786440 | tf_op jit(solution)/shard_map/ppermute | solution.py:559
  35.1 4.0 %collective-permute-start.6 = (bf16[128,256]{1,0:T(8,128)(2,1)S(1)}, bf16[128,256]{1,0:T(8,128)(2,1)S(1)}, u32[]{:S(2)}, u32[]{:S(2)}) collective-permute-start(bf16[128,256]{1,0:T(8,128)(2,1)S(1)} %copy-done.9), channel_id=1, source_target_pairs={{0,8},{4,12},{8,0},{12,4},{1,9},{5,13},{9,1},{13,5},{2,10},{6,14},... | collective-permute-start | bytes 196616 | tf_op jit(solution)/shard_map/ppermute | solution.py:565
  39.1 3.8 %collective-permute-start.8 = (bf16[128,256]{1,0:T(8,128)(2,1)S(1)}, bf16[128,256]{1,0:T(8,128)(2,1)S(1)}, u32[]{:S(2)}, u32[]{:S(2)}) collective-permute-start(bf16[128,256]{1,0:T(8,128)(2,1)S(1)} %copy-done.7), channel_id=1, source_target_pairs={{0,12},{4,0},{8,4},{12,8},{1,13},{5,1},{9,5},{13,9},{2,14},{6,2},{... | collective-permute-start | bytes 196616 | tf_op jit(solution)/shard_map/ppermute | solution.py:565
  43.4 2.4 %collective-permute-done.7.refs_2_ = bf16[128,256]{1,0:T(8,128)(2,1)S(1)} collective-permute-done((bf16[128,256]{1,0:T(8,128)(2,1)S(1)}, bf16[128,256]{1,0:T(8,128)(2,1)S(1)}, u32[]{:S(2)}, u32[]{:S(2)}) %collective-permute-start.7) | collective-permute-done | bytes 65568 | tf_op jit(solution)/shard_map/ppermute | solution.py:565
  46.9 1.6 %copy.9.weight_ref = bf16[768,768]{1,0:T(8,128)(2,1)S(1)} copy(bf16[768,768]{0,1:T(8,128)(2,1)} %bitcast.5) | data formatting | bytes 2359296 | tf_op jit(solution)/shard_map/optimization_barrier | solution.py:605
  49.1 1.3 %shard_map.72.refs_12_ = f32[256,256]{1,0:T(8,128)S(1)} custom-call(bf16[256,768]{1,0:T(8,128)(2,1)S(1)} %get-tuple-element.55.qkv_ref.refs_0_), custom_call_target="tpu_custom_call" | custom-call | flops 268435456 | bytes 1048576 | tf_op jit(solution)/shard_map/pallas_call | solution.py:437
  50.5 1.7 %collective-permute-done.12.rest_ref = bf16[256,256]{1,0:T(8,128)(2,1)S(1)} collective-permute-done((bf16[256,256]{1,0:T(8,128)(2,1)S(1)}, bf16[256,256]{1,0:T(8,128)(2,1)S(1)}, u32[]{:S(2)}, u32[]{:S(2)}) %collective-permute-start.12) | collective-permute-done | bytes 131104 | tf_op jit(solution)/shard_map/ppermute | solution.py:559
  54.6 2.5 %collective-permute-start.16 = (bf16[32,512]{1,0:T(8,128)(2,1)S(1)}, bf16[32,512]{1,0:T(8,128)(2,1)S(1)}, u32[]{:S(2)}, u32[]{:S(2)}) collective-permute-start(bf16[32,512]{1,0:T(8,128)(2,1)S(1)} %constant_dynamic-update-slice_fusion.refs_4_), channel_id=1, source_target_pairs={{0,4},{4,8},{8,12},{12,0},{1,5},{5,9},{9,13},{13,1},{2,6},{6,10},{... | collective-permute-start | bytes 98312 | tf_op jit(solution)/shard_map/ppermute | solution.py:565
  57.1 1.4 %collective-permute-start.17 = (bf16[32,512]{1,0:T(8,128)(2,1)S(1)}, bf16[32,512]{1,0:T(8,128)(2,1)S(1)}, u32[]{:S(2)}, u32[]{:S(2)}) collective-permute-start(bf16[32,512]{1,0:T(8,128)(2,1)S(1)} %constant_dynamic-update-slice_fusion.refs_4_), channel_id=1, source_target_pairs={{0,12},{4,0},{8,4},{12,8},{1,13},{5,1},{9,5},{13,9},{2,14},{6,2},{... | collective-permute-start | bytes 98312 | tf_op jit(solution)/shard_map/ppermute | solution.py:565
  59.2 1.3 %shard_map.73.refs_13_ = f32[256,256]{1,0:T(8,128)S(1)} custom-call(bf16[256,768]{1,0:T(8,128)(2,1)S(1)} %get-tuple-element.56.qkv_ref.refs_1_), custom_call_target="tpu_custom_call" | custom-call | flops 268435456 | bytes 1048576 | tf_op jit(solution)/shard_map/pallas_call | solution.py:437
  62.1 3.2 %collective-permute-start.20 = (bf16[32,512]{1,0:T(8,128)(2,1)S(1)}, bf16[32,512]{1,0:T(8,128)(2,1)S(1)}, u32[]{:S(2)}, u32[]{:S(2)}) collective-permute-start(bf16[32,512]{1,0:T(8,128)(2,1)S(1)} %constant_dynamic-update-slice_fusion.2.refs_8_), channel_id=1, source_target_pairs={{0,12},{4,0},{8,4},{12,8},{1,13},{5,1},{9,5},{13,9},{2,14},{6,2},{... | collective-permute-start | bytes 98312 | tf_op jit(solution)/shard_map/ppermute | solution.py:565
  65.3 1.3 %shard_map.74.refs_14_ = f32[256,256]{1,0:T(8,128)S(1)} custom-call(bf16[256,768]{1,0:T(8,128)(2,1)S(1)} %get-tuple-element.57.qkv_ref.refs_2_), custom_call_target="tpu_custom_call" | custom-call | flops 268435456 | bytes 1048576 | tf_op jit(solution)/shard_map/pallas_call | solution.py:437
  66.6 1.3 %shard_map.75.refs_15_ = f32[256,256]{1,0:T(8,128)S(1)} custom-call(bf16[256,768]{1,0:T(8,128)(2,1)S(1)} %get-tuple-element.58.qkv_ref.refs_3_), custom_call_target="tpu_custom_call" | custom-call | flops 268435456 | bytes 1048576 | tf_op jit(solution)/shard_map/pallas_call | solution.py:437
  68.0 1.8 %wide.1 = (bf16[192,256]{1,0:T(8,128)(2,1)S(1)}, bf16[192,256]{1,0:T(8,128)(2,1)S(1)}, bf16[192,256]{1,0:T(8,128)(2,1)S(1)}, bf16[192,256]{1,0:T(8,128)(2,1)S(1)}) custom-call(bf16[256,768]{1,0:T(8,128)(2,1)S(1)} %get-tuple-element.55.qkv_ref.refs_0_, bf16[256,768]{1,0:T(8,128)(2,1)S(1)} %get-tuple-element.56.qkv_ref.refs_1_, ...), custom_call_target="tpu_custom_call" | custom-call | flops 268435456 | bytes 1048576 | tf_op jit(solution)/shard_map/wide/pallas_call | solution.py:526
  72.0 3.7 %collective-permute-done.22.refs_2_ = bf16[192,256]{1,0:T(8,128)(2,1)S(1)} collective-permute-done((bf16[192,256]{1,0:T(8,128)(2,1)S(1)}, bf16[192,256]{1,0:T(8,128)(2,1)S(1)}, u32[]{:S(2)}, u32[]{:S(2)}) %collective-permute-start.22) | collective-permute-done | bytes 98336 | tf_op jit(solution)/shard_map/ppermute | solution.py:559
  76.7 1.5 %finish.1 = bf16[256,768]{1,0:T(8,128)(2,1)} custom-call(bf16[768,256]{1,0:T(8,128)(2,1)S(1)} %shard_map.67.turned_ref, bf16[768,768]{1,0:T(8,128)(2,1)S(1)} %shard_map.66.weight_ref, bf16[192,256]{1,0:T(8,128)(2,1)S(1)} %get-tuple-element.63.refs_0_, bf16[192,256]{1,0:T(8,128)(2,1)S(1)} %collective-permute-done.21.refs_1_, ...), custom_call_target="tpu_custom_call" | custom-call | flops 402653184 | bytes 1048576 | tf_op jit(solution)/shard_map/finish/pallas_call | solution.py:548
  (68 shorter events, 14.9 us)
Async XLA Ops:
  8.3 10.0 %collective-permute-start.4 = (bf16[192,768]{1,0:T(8,128)(2,1)S(1)}, bf16[192,768]{1,0:T(8,128)(2,1)S(1)}, u32[]{:S(2)}, u32[]{:S(2)}) collective-permute-start(bf16[192,768]{1,0:T(8,128)(2,1)S(1)} %copy-done), channel_id=1, source_target_pairs={{0,2},{1,3},{2,0},{3,1},{4,6},{5,7},{6,4},{7,5},{8,10},{9,11},{10,... | collective-permute-start | bytes 884744 | tf_op jit(solution)/shard_map/ppermute | solution.py:559
  11.3 16.1 %collective-permute-start.3 = (bf16[192,768]{1,0:T(8,128)(2,1)S(1)}, bf16[192,768]{1,0:T(8,128)(2,1)S(1)}, u32[]{:S(2)}, u32[]{:S(2)}) collective-permute-start(bf16[192,768]{1,0:T(8,128)(2,1)S(1)} %copy-done), channel_id=1, source_target_pairs={{0,1},{1,0},{2,3},{3,2},{4,5},{5,4},{6,7},{7,6},{8,9},{9,8},{10,11... | collective-permute-start | bytes 884744 | tf_op jit(solution)/shard_map/ppermute | solution.py:559
  18.3 9.1 %collective-permute-start.5 = (bf16[192,768]{1,0:T(8,128)(2,1)S(1)}, bf16[192,768]{1,0:T(8,128)(2,1)S(1)}, u32[]{:S(2)}, u32[]{:S(2)}) collective-permute-start(bf16[192,768]{1,0:T(8,128)(2,1)S(1)} %collective-permute-done.4.refs_2_), channel_id=1, source_target_pairs={{0,1},{1,0},{2,3},{3,2},{4,5},{5,4},{6,7},{7,6},{8,9},{9,8},{10,11... | collective-permute-start | bytes 884744 | tf_op jit(solution)/shard_map/ppermute | solution.py:559
  18.3 13.5 %collective-permute-start = (bf16[136,512]{1,0:T(8,128)(2,1)S(1)}, bf16[136,512]{1,0:T(8,128)(2,1)S(1)}, u32[]{:S(2)}, u32[]{:S(2)}) collective-permute-start(bf16[136,512]{1,0:T(8,128)(2,1)S(1)} %copy-done.6), channel_id=1, source_target_pairs={{0,8},{4,12},{8,0},{12,4},{1,9},{5,13},{9,1},{13,5},{2,10},{6,14},... | collective-permute-start | bytes 417800 | tf_op jit(solution)/shard_map/ppermute | solution.py:565
  21.1 10.6 %collective-permute-start.1 = (bf16[136,512]{1,0:T(8,128)(2,1)S(1)}, bf16[136,512]{1,0:T(8,128)(2,1)S(1)}, u32[]{:S(2)}, u32[]{:S(2)}) collective-permute-start(bf16[136,512]{1,0:T(8,128)(2,1)S(1)} %copy-done.5), channel_id=1, source_target_pairs={{0,4},{4,8},{8,12},{12,0},{1,5},{5,9},{9,13},{13,1},{2,6},{6,10},{... | collective-permute-start | bytes 417800 | tf_op jit(solution)/shard_map/ppermute | solution.py:565
  22.7 10.3 %collective-permute-start.2 = (bf16[136,512]{1,0:T(8,128)(2,1)S(1)}, bf16[136,512]{1,0:T(8,128)(2,1)S(1)}, u32[]{:S(2)}, u32[]{:S(2)}) collective-permute-start(bf16[136,512]{1,0:T(8,128)(2,1)S(1)} %copy-done.4), channel_id=1, source_target_pairs={{0,12},{4,0},{8,4},{12,8},{1,13},{5,1},{9,5},{13,9},{2,14},{6,2},{... | collective-permute-start | bytes 417800 | tf_op jit(solution)/shard_map/ppermute | solution.py:565
  33.5 18.7 %collective-permute-start.11 = (bf16[256,512]{1,0:T(8,128)(2,1)S(1)}, bf16[256,512]{1,0:T(8,128)(2,1)S(1)}, u32[]{:S(2)}, u32[]{:S(2)}) collective-permute-start(bf16[256,512]{1,0:T(8,128)(2,1)S(1)} %get-tuple-element.51.refs_0_.lead_ref), channel_id=1, source_target_pairs={{0,2},{1,3},{2,0},{3,1},{4,6},{5,7},{6,4},{7,5},{8,10},{9,11},{10,... | collective-permute-start | bytes 786440 | tf_op jit(solution)/shard_map/ppermute | solution.py:559
  35.1 17.6 %collective-permute-start.9 = (bf16[256,512]{1,0:T(8,128)(2,1)S(1)}, bf16[256,512]{1,0:T(8,128)(2,1)S(1)}, u32[]{:S(2)}, u32[]{:S(2)}) collective-permute-start(bf16[256,512]{1,0:T(8,128)(2,1)S(1)} %get-tuple-element.51.refs_0_.lead_ref), channel_id=1, source_target_pairs={{0,1},{1,0},{2,3},{3,2},{4,5},{5,4},{6,7},{7,6},{8,9},{9,8},{10,11... | collective-permute-start | bytes 786440 | tf_op jit(solution)/shard_map/ppermute | solution.py:559
  35.1 8.3 %collective-permute-start.6 = (bf16[128,256]{1,0:T(8,128)(2,1)S(1)}, bf16[128,256]{1,0:T(8,128)(2,1)S(1)}, u32[]{:S(2)}, u32[]{:S(2)}) collective-permute-start(bf16[128,256]{1,0:T(8,128)(2,1)S(1)} %copy-done.9), channel_id=1, source_target_pairs={{0,8},{4,12},{8,0},{12,4},{1,9},{5,13},{9,1},{13,5},{2,10},{6,14},... | collective-permute-start | bytes 196616 | tf_op jit(solution)/shard_map/ppermute | solution.py:565
  39.1 6.7 %collective-permute-start.7 = (bf16[128,256]{1,0:T(8,128)(2,1)S(1)}, bf16[128,256]{1,0:T(8,128)(2,1)S(1)}, u32[]{:S(2)}, u32[]{:S(2)}) collective-permute-start(bf16[128,256]{1,0:T(8,128)(2,1)S(1)} %copy-done.8), channel_id=1, source_target_pairs={{0,4},{4,8},{8,12},{12,0},{1,5},{5,9},{9,13},{13,1},{2,6},{6,10},{... | collective-permute-start | bytes 196616 | tf_op jit(solution)/shard_map/ppermute | solution.py:565
  39.1 6.8 %collective-permute-start.8 = (bf16[128,256]{1,0:T(8,128)(2,1)S(1)}, bf16[128,256]{1,0:T(8,128)(2,1)S(1)}, u32[]{:S(2)}, u32[]{:S(2)}) collective-permute-start(bf16[128,256]{1,0:T(8,128)(2,1)S(1)} %copy-done.7), channel_id=1, source_target_pairs={{0,12},{4,0},{8,4},{12,8},{1,13},{5,1},{9,5},{13,9},{2,14},{6,2},{... | collective-permute-start | bytes 196616 | tf_op jit(solution)/shard_map/ppermute | solution.py:565
  46.2 6.5 %collective-permute-start.10 = (bf16[256,256]{1,0:T(8,128)(2,1)S(1)}, bf16[256,256]{1,0:T(8,128)(2,1)S(1)}, u32[]{:S(2)}, u32[]{:S(2)}) collective-permute-start(bf16[256,256]{1,0:T(8,128)(2,1)S(1)} %land_rest.1.refs_1_.rest_ref), channel_id=1, source_target_pairs={{0,1},{1,0},{2,3},{3,2},{4,5},{5,4},{6,7},{7,6},{8,9},{9,8},{10,11... | collective-permute-start | bytes 393224 | tf_op jit(solution)/shard_map/ppermute | solution.py:559
  46.3 5.9 %collective-permute-start.12 = (bf16[256,256]{1,0:T(8,128)(2,1)S(1)}, bf16[256,256]{1,0:T(8,128)(2,1)S(1)}, u32[]{:S(2)}, u32[]{:S(2)}) collective-permute-start(bf16[256,256]{1,0:T(8,128)(2,1)S(1)} %land_rest.1.refs_1_.rest_ref), channel_id=1, source_target_pairs={{0,2},{1,3},{2,0},{3,1},{4,6},{5,7},{6,4},{7,5},{8,10},{9,11},{10,... | collective-permute-start | bytes 393224 | tf_op jit(solution)/shard_map/ppermute | solution.py:559
  52.2 8.4 %collective-permute-start.14 = (bf16[256,256]{1,0:T(8,128)(2,1)S(1)}, bf16[256,256]{1,0:T(8,128)(2,1)S(1)}, u32[]{:S(2)}, u32[]{:S(2)}) collective-permute-start(bf16[256,256]{1,0:T(8,128)(2,1)S(1)} %collective-permute-done.12.rest_ref), channel_id=1, source_target_pairs={{0,1},{1,0},{2,3},{3,2},{4,5},{5,4},{6,7},{7,6},{8,9},{9,8},{10,11... | collective-permute-start | bytes 393224 | tf_op jit(solution)/shard_map/ppermute | solution.py:559
  52.2 8.4 %collective-permute-start.13 = (bf16[256,512]{1,0:T(8,128)(2,1)S(1)}, bf16[256,512]{1,0:T(8,128)(2,1)S(1)}, u32[]{:S(2)}, u32[]{:S(2)}) collective-permute-start(bf16[256,512]{1,0:T(8,128)(2,1)S(1)} %collective-permute-done.11.lead_ref), channel_id=1, source_target_pairs={{0,1},{1,0},{2,3},{3,2},{4,5},{5,4},{6,7},{7,6},{8,9},{9,8},{10,11... | collective-permute-start | bytes 786440 | tf_op jit(solution)/shard_map/ppermute | solution.py:559
  53.4 8.7 %collective-permute-start.15 = (bf16[32,512]{1,0:T(8,128)(2,1)S(1)}, bf16[32,512]{1,0:T(8,128)(2,1)S(1)}, u32[]{:S(2)}, u32[]{:S(2)}) collective-permute-start(bf16[32,512]{1,0:T(8,128)(2,1)S(1)} %constant_dynamic-update-slice_fusion.refs_4_), channel_id=1, source_target_pairs={{0,8},{4,12},{8,0},{12,4},{1,9},{5,13},{9,1},{13,5},{2,10},{6,14},... | collective-permute-start | bytes 98312 | tf_op jit(solution)/shard_map/ppermute | solution.py:565
  54.6 13.3 %collective-permute-start.16 = (bf16[32,512]{1,0:T(8,128)(2,1)S(1)}, bf16[32,512]{1,0:T(8,128)(2,1)S(1)}, u32[]{:S(2)}, u32[]{:S(2)}) collective-permute-start(bf16[32,512]{1,0:T(8,128)(2,1)S(1)} %constant_dynamic-update-slice_fusion.refs_4_), channel_id=1, source_target_pairs={{0,4},{4,8},{8,12},{12,0},{1,5},{5,9},{9,13},{13,1},{2,6},{6,10},{... | collective-permute-start | bytes 98312 | tf_op jit(solution)/shard_map/ppermute | solution.py:565
  57.1 10.9 %collective-permute-start.17 = (bf16[32,512]{1,0:T(8,128)(2,1)S(1)}, bf16[32,512]{1,0:T(8,128)(2,1)S(1)}, u32[]{:S(2)}, u32[]{:S(2)}) collective-permute-start(bf16[32,512]{1,0:T(8,128)(2,1)S(1)} %constant_dynamic-update-slice_fusion.refs_4_), channel_id=1, source_target_pairs={{0,12},{4,0},{8,4},{12,8},{1,13},{5,1},{9,5},{13,9},{2,14},{6,2},{... | collective-permute-start | bytes 98312 | tf_op jit(solution)/shard_map/ppermute | solution.py:565
  61.3 6.7 %collective-permute-start.18 = (bf16[32,512]{1,0:T(8,128)(2,1)S(1)}, bf16[32,512]{1,0:T(8,128)(2,1)S(1)}, u32[]{:S(2)}, u32[]{:S(2)}) collective-permute-start(bf16[32,512]{1,0:T(8,128)(2,1)S(1)} %constant_dynamic-update-slice_fusion.2.refs_8_), channel_id=1, source_target_pairs={{0,8},{4,12},{8,0},{12,4},{1,9},{5,13},{9,1},{13,5},{2,10},{6,14},... | collective-permute-start | bytes 98312 | tf_op jit(solution)/shard_map/ppermute | solution.py:565
  61.4 6.6 %collective-permute-start.19 = (bf16[32,512]{1,0:T(8,128)(2,1)S(1)}, bf16[32,512]{1,0:T(8,128)(2,1)S(1)}, u32[]{:S(2)}, u32[]{:S(2)}) collective-permute-start(bf16[32,512]{1,0:T(8,128)(2,1)S(1)} %constant_dynamic-update-slice_fusion.2.refs_8_), channel_id=1, source_target_pairs={{0,4},{4,8},{8,12},{12,0},{1,5},{5,9},{9,13},{13,1},{2,6},{6,10},{... | collective-permute-start | bytes 98312 | tf_op jit(solution)/shard_map/ppermute | solution.py:565
  62.1 5.9 %collective-permute-start.20 = (bf16[32,512]{1,0:T(8,128)(2,1)S(1)}, bf16[32,512]{1,0:T(8,128)(2,1)S(1)}, u32[]{:S(2)}, u32[]{:S(2)}) collective-permute-start(bf16[32,512]{1,0:T(8,128)(2,1)S(1)} %constant_dynamic-update-slice_fusion.2.refs_8_), channel_id=1, source_target_pairs={{0,12},{4,0},{8,4},{12,8},{1,13},{5,1},{9,5},{13,9},{2,14},{6,2},{... | collective-permute-start | bytes 98312 | tf_op jit(solution)/shard_map/ppermute | solution.py:565
  69.9 2.1 %collective-permute-start.21 = (bf16[192,256]{1,0:T(8,128)(2,1)S(1)}, bf16[192,256]{1,0:T(8,128)(2,1)S(1)}, u32[]{:S(2)}, u32[]{:S(2)}) collective-permute-start(bf16[192,256]{1,0:T(8,128)(2,1)S(1)} %get-tuple-element.64), channel_id=1, source_target_pairs={{0,1},{1,0},{2,3},{3,2},{4,5},{5,4},{6,7},{7,6},{8,9},{9,8},{10,11... | collective-permute-start | bytes 294920 | tf_op jit(solution)/shard_map/ppermute | solution.py:559
  69.9 5.7 %collective-permute-start.22 = (bf16[192,256]{1,0:T(8,128)(2,1)S(1)}, bf16[192,256]{1,0:T(8,128)(2,1)S(1)}, u32[]{:S(2)}, u32[]{:S(2)}) collective-permute-start(bf16[192,256]{1,0:T(8,128)(2,1)S(1)} %get-tuple-element.65), channel_id=1, source_target_pairs={{0,2},{1,3},{2,0},{3,1},{4,6},{5,7},{6,4},{7,5},{8,10},{9,11},{10,... | collective-permute-start | bytes 294920 | tf_op jit(solution)/shard_map/ppermute | solution.py:559
  70.5 6.2 %collective-permute-start.23 = (bf16[192,256]{1,0:T(8,128)(2,1)S(1)}, bf16[192,256]{1,0:T(8,128)(2,1)S(1)}, u32[]{:S(2)}, u32[]{:S(2)}) collective-permute-start(bf16[192,256]{1,0:T(8,128)(2,1)S(1)} %get-tuple-element.66), channel_id=1, source_target_pairs={{0,3},{1,2},{2,1},{3,0},{4,7},{5,6},{6,5},{7,4},{8,11},{9,10},{10,... | collective-permute-start | bytes 294920 | tf_op jit(solution)/shard_map/ppermute | solution.py:559
  (10 other events, 123.4 us)

commit v3 on v2

--- a/solution.py
+++ b/solution.py
@@ -595,14 +595,16 @@
     lead_in = [lead[0]] + [shifted(lead[shift], shift) for shift in order]
     rest, _ = pack(tile_rows, embed_weight, pick, width - lead_width, seq_count)
     rest_in = [rest[0]] + [shifted(rest[shift], shift) for shift in order]
-    rest, out_weight, qkv_weight = lax.optimization_barrier((rest, out_weight, qkv_weight))
+    lead_in[0], out_weight, qkv_weight = lax.optimization_barrier(
+        (lead_in[0], out_weight, qkv_weight)
+    )
     out_over = across(out_weight, 2)
     out_pieces = [out_weight, across(out_weight, 1), out_over]
     out_pieces.append(across(out_over, 1))
     turned_weight = turn(out_pieces, False)
     by_kind = jnp.transpose(qkv_weight, (0, 2, 1, 3))
     weight = jnp.pad(by_kind, ((0, 0), (0, 0), (0, 0), (0, HALF - head_dim))).reshape(width, -1)
-    lead_in, turned_weight, weight = lax.optimization_barrier((lead_in, turned_weight, weight))
+    lead_in, weight = lax.optimization_barrier((lead_in, weight))
     rows_lead, here = land(lead_in, in_rows)
     lead_over = across(rows_lead, 2)
     lead_beside = across(rows_lead, 1)
@@ -611,24 +613,22 @@
     rest_over = across(rows_rest, 2)
     rest_beside = across(rows_rest, 1)
     gain = norm_gain.reshape(1, width)
-    sources, nears, fars = [], [], []
+    sources, nears, far_parts = [], [], []
 
     def step(halves):
         qkv, far = qkv_of(halves, gain, weight, head_dim, heads_here)
         sources.append(qkv)
         nears.append(near(qkv, head_dim, heads_here))
-        return far
-
-    def spread(parts):
-        far = jnp.concatenate(parts, axis=0)
-        fars.extend([far] + [shifted(far, shift) for shift in order])
-
-    far_parts = [step([rows_lead, rows_rest]), step([lead_beside, rest_beside])]
-    spread(far_parts)
+        far_parts.append(far)
+
+    step([rows_lead, rows_rest])
+    step([lead_beside, rest_beside])
     turned = turn([rows_lead, rows_rest], True)
     rest_both = across(rest_over, 1)
-    far_parts = [step([lead_over, rest_over]), step([lead_both, rest_both])]
-    spread(far_parts)
+    step([lead_over, rest_over])
+    step([lead_both, rest_both])
+    far = jnp.concatenate(far_parts, axis=0)
+    fars = [far] + [shifted(far, shift) for shift in order]
     parts = attention_blocks(sources, fars, nears, head_dim, heads_here)
     joined = [parts[0]] + [across(parts[bit], bit) for bit in range(1, 4)]
     return finish(turned, turned_weight, joined)

time: 78.5 us -> 61 us (0.78)
  waiting for transfers between devices: 21.4 us -> 9.38 us
  starting transfers between devices: 31.3 us -> 27 us
  local copies, waits for them, and re-layouts: 3.99 us -> 2.82 us
    ppermute x12, waiting for transfers between devices: 13.4 us -> 5.58 us  [across(): lax.ppermute(block, 'head', [(member, member ^ bit) for member in range(c...]
    ppermute x12 -> x9, waiting for transfers between devices: 7.96 us -> 3.8 us  [shifted(): return lax.ppermute(block, 'seq', pairs)]
    ppermute x12 -> x9, starting transfers between devices: 23.5 us -> 20.2 us  [shifted(): return lax.ppermute(block, 'seq', pairs)]
    optimization_barrier x2, local copies, waits for them, and re-layouts: 2.79 us -> 1.62 us  [the longest x1 1.56 us: fast(): lead_in, weight = lax.optimization_barrier((lead_in, weight))]
    ppermute x12, starting transfers between devices: 7.75 us -> 6.86 us  [across(): lax.ppermute(block, 'head', [(member, member ^ bit) for member in range(c...]
  transfers between devices with their start and end apart: 24 -> 21, of which waited for: 9 -> 8; matrix products, arithmetic and copies ran while one was open for 5% -> 5% of each run, Pallas kernels for 12% -> 25%
where the time goes in v3:
time: 61 us; the launch traced here: 60.8 us
  starting transfers between devices  27 us (44%)
  Pallas kernels  21.2 us (35%)
  waiting for transfers between devices  9.38 us (15%)
  local copies, waits for them, and re-layouts  2.82 us (5%)
    ppermute x9, starting transfers between devices, shifted(): return lax.ppermute(block, 'seq', pairs)  20.2 us
    pallas_call x2, Pallas kernels, pack(): pl.pallas_call(functools.partial(pack_kernel, seq_count), in_specs=[hbm,...  8.2 us
    ppermute x12, starting transfers between devices, across(): lax.ppermute(block, 'head', [(member, member ^ bit) for member in range(c...  6.86 us
    ppermute x12, waiting for transfers between devices, across(): lax.ppermute(block, 'head', [(member, member ^ bit) for member in range(c...  5.58 us
    pallas_call x4, Pallas kernels, near(): pl.pallas_call(functools.partial(near_kernel, head_dim, heads_here), out_...  5.35 us
    ppermute x9, waiting for transfers between devices, shifted(): return lax.ppermute(block, 'seq', pairs)  3.8 us
    pallas_call x4, Pallas kernels, qkv_of(): pl.pallas_call(functools.partial(qkv_kernel, head_dim, heads_here), out_s...  2.8 us
    pallas_call x1, Pallas kernels, attention_blocks(): pl.pallas_call(functools.partial(wide_kernel, head_dim, heads_here), out_...  1.84 us
  transfers between devices with their start and end apart: 21, of which 8 were waited for; matrix products, arithmetic and copies ran while one was open for 5% of the time, Pallas kernels for 25%

profile of v3, /device:TPU:0, one launch (start us, length us, event | category | flops | bytes accessed | tf_op | source)
XLA Modules:
  0.0 60.8 jit_solution(6384078154996258033)
XLA Ops:
  0.0 4.5 %shard_map.64 = (bf16[136,512]{1,0:T(8,128)(2,1)}, bf16[136,512]{1,0:T(8,128)(2,1)}, bf16[136,512]{1,0:T(8,128)(2,1)}, bf16[136,512]{1,0:T(8,128)(2,1)}, bf16[512,256]{1,0:T(8,128)(2,1)}) custom-call(bf16[256,1536]{1,0:T(8,128)(2,1)} %rows_hbm.3, bf16[1536,768]{1,0:T(8,128)(2,1)} %weight_hbm.3, s32[2,256]{1,0:T(2,128)} %bitcast.7), custom_call_target="tpu_custom_call" | custom-call | flops 536870912 | bytes 1048576 | tf_op jit(solution)/shard_map/pallas_call | solution.py:278
  4.5 4.1 %collective-permute-start = (bf16[136,512]{1,0:T(8,128)(2,1)}, bf16[136,512]{1,0:T(8,128)(2,1)S(1)}, u32[]{:S(2)}, u32[]{:S(2)}) collective-permute-start(bf16[136,512]{1,0:T(8,128)(2,1)} %get-tuple-element.38), channel_id=1, source_target_pairs={{0,8},{4,12},{8,0},{12,4},{1,9},{5,13},{9,1},{13,5},{2,10},{6,14},... | collective-permute-start | bytes 417800 | tf_op jit(solution)/shard_map/ppermute | solution.py:565
  8.6 1.6 %collective-permute-start.1 = (bf16[136,512]{1,0:T(8,128)(2,1)}, bf16[136,512]{1,0:T(8,128)(2,1)S(1)}, u32[]{:S(2)}, u32[]{:S(2)}) collective-permute-start(bf16[136,512]{1,0:T(8,128)(2,1)} %get-tuple-element.39), channel_id=1, source_target_pairs={{0,4},{4,8},{8,12},{12,0},{1,5},{5,9},{9,13},{13,1},{2,6},{6,10},{... | collective-permute-start | bytes 417800 | tf_op jit(solution)/shard_map/ppermute | solution.py:565
  10.2 2.2 %collective-permute-start.2 = (bf16[136,512]{1,0:T(8,128)(2,1)}, bf16[136,512]{1,0:T(8,128)(2,1)S(1)}, u32[]{:S(2)}, u32[]{:S(2)}) collective-permute-start(bf16[136,512]{1,0:T(8,128)(2,1)} %get-tuple-element.40), channel_id=1, source_target_pairs={{0,12},{4,0},{8,4},{12,8},{1,13},{5,1},{9,5},{13,9},{2,14},{6,2},{... | collective-permute-start | bytes 417800 | tf_op jit(solution)/shard_map/ppermute | solution.py:565
  12.4 3.7 %shard_map.65 = (bf16[128,256]{1,0:T(8,128)(2,1)}, bf16[128,256]{1,0:T(8,128)(2,1)}, bf16[128,256]{1,0:T(8,128)(2,1)}, bf16[128,256]{1,0:T(8,128)(2,1)}) custom-call(bf16[256,1536]{1,0:T(8,128)(2,1)} %rows_hbm.3, bf16[1536,768]{1,0:T(8,128)(2,1)} %weight_hbm.3, bf16[512,256]{1,0:T(8,128)(2,1)} %get-tuple-element.48.route_ref), custom_call_target="tpu_custom_call" | custom-call | flops 268435456 | bytes 1048576 | tf_op jit(solution)/shard_map/pallas_call | solution.py:278
  16.3 1.6 %collective-permute-start.7 = (bf16[192,768]{1,0:T(8,128)(2,1)S(1)}, bf16[192,768]{1,0:T(8,128)(2,1)S(1)}, u32[]{:S(2)}, u32[]{:S(2)}) collective-permute-start(bf16[192,768]{1,0:T(8,128)(2,1)S(1)} %copy-done), channel_id=1, source_target_pairs={{0,2},{1,3},{2,0},{3,1},{4,6},{5,7},{6,4},{7,5},{8,10},{9,11},{10,... | collective-permute-start | bytes 884744 | tf_op jit(solution)/shard_map/ppermute | solution.py:559
  17.9 1.1 %pad.4 = bf16[768,3,4,64]{0,3,2,1:T(8,128)(2,1)} pad(bf16[768,3,4,48]{0,3,2,1:T(8,128)(2,1)S(1)} %bitcast.6, bf16[]{:T(256)} %constant.2.clone.1), padding=0_0x0_0x0_0x0_16 | pad | bytes 2064386 | tf_op jit(solution)/shard_map/jit(_pad)/pad | solution.py:606
  20.5 1.9 %collective-permute-start.11 = (bf16[256,512]{1,0:T(8,128)(2,1)S(1)}, bf16[256,512]{1,0:T(8,128)(2,1)S(1)}, u32[]{:S(2)}, u32[]{:S(2)}) collective-permute-start(bf16[256,512]{1,0:T(8,128)(2,1)S(1)} %get-tuple-element.46.refs_0_.lead_ref), channel_id=1, source_target_pairs={{0,2},{1,3},{2,0},{3,1},{4,6},{5,7},{6,4},{7,5},{8,10},{9,11},{10,... | collective-permute-start | bytes 786440 | tf_op jit(solution)/shard_map/ppermute | solution.py:559
  22.4 3.8 %collective-permute-start.4 = (bf16[128,256]{1,0:T(8,128)(2,1)S(1)}, bf16[128,256]{1,0:T(8,128)(2,1)S(1)}, u32[]{:S(2)}, u32[]{:S(2)}) collective-permute-start(bf16[128,256]{1,0:T(8,128)(2,1)S(1)} %copy-done.6), channel_id=1, source_target_pairs={{0,4},{4,8},{8,12},{12,0},{1,5},{5,9},{9,13},{13,1},{2,6},{6,10},{... | collective-permute-start | bytes 196616 | tf_op jit(solution)/shard_map/ppermute | solution.py:565
  26.2 1.6 %collective-permute-start.5 = (bf16[128,256]{1,0:T(8,128)(2,1)S(1)}, bf16[128,256]{1,0:T(8,128)(2,1)S(1)}, u32[]{:S(2)}, u32[]{:S(2)}) collective-permute-start(bf16[128,256]{1,0:T(8,128)(2,1)S(1)} %copy-done.5), channel_id=1, source_target_pairs={{0,12},{4,0},{8,4},{12,8},{1,13},{5,1},{9,5},{13,9},{2,14},{6,2},{... | collective-permute-start | bytes 196616 | tf_op jit(solution)/shard_map/ppermute | solution.py:565
  28.7 2.0 %collective-permute-done.5.refs_3_ = bf16[128,256]{1,0:T(8,128)(2,1)S(1)} collective-permute-done((bf16[128,256]{1,0:T(8,128)(2,1)S(1)}, bf16[128,256]{1,0:T(8,128)(2,1)S(1)}, u32[]{:S(2)}, u32[]{:S(2)}) %collective-permute-start.5) | collective-permute-done | bytes 65568 | tf_op jit(solution)/shard_map/ppermute | solution.py:565
  31.6 1.6 %copy.9.weight_ref = bf16[768,768]{1,0:T(8,128)(2,1)S(1)} copy(bf16[768,768]{0,1:T(8,128)(2,1)} %bitcast.5) | data formatting | bytes 2359296 | tf_op jit(solution)/shard_map/optimization_barrier | solution.py:607
  33.9 1.3 %shard_map.72.refs_8_ = f32[256,256]{1,0:T(8,128)S(1)} custom-call(bf16[256,768]{1,0:T(8,128)(2,1)S(1)} %get-tuple-element.55.qkv_ref.refs_0_), custom_call_target="tpu_custom_call" | custom-call | flops 268435456 | bytes 1048576 | tf_op jit(solution)/shard_map/pallas_call | solution.py:437
  35.5 1.4 %collective-permute-done.12.rest_ref = bf16[256,256]{1,0:T(8,128)(2,1)S(1)} collective-permute-done((bf16[256,256]{1,0:T(8,128)(2,1)S(1)}, bf16[256,256]{1,0:T(8,128)(2,1)S(1)}, u32[]{:S(2)}, u32[]{:S(2)}) %collective-permute-start.12) | collective-permute-done | bytes 131104 | tf_op jit(solution)/shard_map/ppermute | solution.py:559
  39.8 2.9 %collective-permute-start.15 = (bf16[64,512]{1,0:T(8,128)(2,1)S(1)}, bf16[64,512]{1,0:T(8,128)(2,1)S(1)}, u32[]{:S(2)}, u32[]{:S(2)}) collective-permute-start(bf16[64,512]{1,0:T(8,128)(2,1)S(1)} %constant_dynamic-update-slice_fusion.refs_4_), channel_id=1, source_target_pairs={{0,8},{4,12},{8,0},{12,4},{1,9},{5,13},{9,1},{13,5},{2,10},{6,14},... | collective-permute-start | bytes 196616 | tf_op jit(solution)/shard_map/ppermute | solution.py:565
  42.7 1.1 %collective-permute-start.16 = (bf16[64,512]{1,0:T(8,128)(2,1)S(1)}, bf16[64,512]{1,0:T(8,128)(2,1)S(1)}, u32[]{:S(2)}, u32[]{:S(2)}) collective-permute-start(bf16[64,512]{1,0:T(8,128)(2,1)S(1)} %constant_dynamic-update-slice_fusion.refs_4_), channel_id=1, source_target_pairs={{0,4},{4,8},{8,12},{12,0},{1,5},{5,9},{9,13},{13,1},{2,6},{6,10},{... | collective-permute-start | bytes 196616 | tf_op jit(solution)/shard_map/ppermute | solution.py:565
  43.8 2.7 %collective-permute-start.17 = (bf16[64,512]{1,0:T(8,128)(2,1)S(1)}, bf16[64,512]{1,0:T(8,128)(2,1)S(1)}, u32[]{:S(2)}, u32[]{:S(2)}) collective-permute-start(bf16[64,512]{1,0:T(8,128)(2,1)S(1)} %constant_dynamic-update-slice_fusion.refs_4_), channel_id=1, source_target_pairs={{0,12},{4,0},{8,4},{12,8},{1,13},{5,1},{9,5},{13,9},{2,14},{6,2},{... | collective-permute-start | bytes 196616 | tf_op jit(solution)/shard_map/ppermute | solution.py:565
  46.5 1.3 %shard_map.74.refs_10_ = f32[256,256]{1,0:T(8,128)S(1)} custom-call(bf16[256,768]{1,0:T(8,128)(2,1)S(1)} %get-tuple-element.57.qkv_ref.refs_2_), custom_call_target="tpu_custom_call" | custom-call | flops 268435456 | bytes 1048576 | tf_op jit(solution)/shard_map/pallas_call | solution.py:437
  47.9 1.3 %shard_map.73.refs_9_ = f32[256,256]{1,0:T(8,128)S(1)} custom-call(bf16[256,768]{1,0:T(8,128)(2,1)S(1)} %get-tuple-element.56.qkv_ref.refs_1_), custom_call_target="tpu_custom_call" | custom-call | flops 268435456 | bytes 1048576 | tf_op jit(solution)/shard_map/pallas_call | solution.py:437
  49.2 1.3 %shard_map.75.refs_11_ = f32[256,256]{1,0:T(8,128)S(1)} custom-call(bf16[256,768]{1,0:T(8,128)(2,1)S(1)} %get-tuple-element.58.qkv_ref.refs_3_), custom_call_target="tpu_custom_call" | custom-call | flops 268435456 | bytes 1048576 | tf_op jit(solution)/shard_map/pallas_call | solution.py:437
  50.6 1.8 %wide.1 = (bf16[192,256]{1,0:T(8,128)(2,1)S(1)}, bf16[192,256]{1,0:T(8,128)(2,1)S(1)}, bf16[192,256]{1,0:T(8,128)(2,1)S(1)}, bf16[192,256]{1,0:T(8,128)(2,1)S(1)}) custom-call(bf16[256,768]{1,0:T(8,128)(2,1)S(1)} %get-tuple-element.55.qkv_ref.refs_0_, bf16[256,768]{1,0:T(8,128)(2,1)S(1)} %get-tuple-element.56.qkv_ref.refs_1_, ...), custom_call_target="tpu_custom_call" | custom-call | flops 268435456 | bytes 1048576 | tf_op jit(solution)/shard_map/wide/pallas_call | solution.py:526
  52.9 1.5 %collective-permute-start.20 = (bf16[192,256]{1,0:T(8,128)(2,1)S(1)}, bf16[192,256]{1,0:T(8,128)(2,1)S(1)}, u32[]{:S(2)}, u32[]{:S(2)}) collective-permute-start(bf16[192,256]{1,0:T(8,128)(2,1)S(1)} %get-tuple-element.66), channel_id=1, source_target_pairs={{0,3},{1,2},{2,1},{3,0},{4,7},{5,6},{6,5},{7,4},{8,11},{9,10},{10,... | collective-permute-start | bytes 294920 | tf_op jit(solution)/shard_map/ppermute | solution.py:559
  55.2 3.0 %collective-permute-done.19.refs_2_ = bf16[192,256]{1,0:T(8,128)(2,1)S(1)} collective-permute-done((bf16[192,256]{1,0:T(8,128)(2,1)S(1)}, bf16[192,256]{1,0:T(8,128)(2,1)S(1)}, u32[]{:S(2)}, u32[]{:S(2)}) %collective-permute-start.19) | collective-permute-done | bytes 98336 | tf_op jit(solution)/shard_map/ppermute | solution.py:559
  59.3 1.5 %finish.1 = bf16[256,768]{1,0:T(8,128)(2,1)} custom-call(bf16[768,256]{1,0:T(8,128)(2,1)S(1)} %shard_map.66.turned_ref, bf16[768,768]{1,0:T(8,128)(2,1)S(1)} %shard_map.67.weight_ref, bf16[192,256]{1,0:T(8,128)(2,1)S(1)} %get-tuple-element.63.refs_0_, bf16[192,256]{1,0:T(8,128)(2,1)S(1)} %collective-permute-done.18.refs_1_, ...), custom_call_target="tpu_custom_call" | custom-call | flops 402653184 | bytes 1048576 | tf_op jit(solution)/shard_map/finish/pallas_call | solution.py:548
  (56 shorter events, 9.5 us)
Async XLA Ops:
  4.5 15.5 %collective-permute-start = (bf16[136,512]{1,0:T(8,128)(2,1)}, bf16[136,512]{1,0:T(8,128)(2,1)S(1)}, u32[]{:S(2)}, u32[]{:S(2)}) collective-permute-start(bf16[136,512]{1,0:T(8,128)(2,1)} %get-tuple-element.38), channel_id=1, source_target_pairs={{0,8},{4,12},{8,0},{12,4},{1,9},{5,13},{9,1},{13,5},{2,10},{6,14},... | collective-permute-start | bytes 417800 | tf_op jit(solution)/shard_map/ppermute | solution.py:565
  8.6 11.4 %collective-permute-start.1 = (bf16[136,512]{1,0:T(8,128)(2,1)}, bf16[136,512]{1,0:T(8,128)(2,1)S(1)}, u32[]{:S(2)}, u32[]{:S(2)}) collective-permute-start(bf16[136,512]{1,0:T(8,128)(2,1)} %get-tuple-element.39), channel_id=1, source_target_pairs={{0,4},{4,8},{8,12},{12,0},{1,5},{5,9},{9,13},{13,1},{2,6},{6,10},{... | collective-permute-start | bytes 417800 | tf_op jit(solution)/shard_map/ppermute | solution.py:565
  10.2 9.9 %collective-permute-start.2 = (bf16[136,512]{1,0:T(8,128)(2,1)}, bf16[136,512]{1,0:T(8,128)(2,1)S(1)}, u32[]{:S(2)}, u32[]{:S(2)}) collective-permute-start(bf16[136,512]{1,0:T(8,128)(2,1)} %get-tuple-element.40), channel_id=1, source_target_pairs={{0,12},{4,0},{8,4},{12,8},{1,13},{5,1},{9,5},{13,9},{2,14},{6,2},{... | collective-permute-start | bytes 417800 | tf_op jit(solution)/shard_map/ppermute | solution.py:565
  16.2 10.0 %collective-permute-start.3 = (bf16[128,256]{1,0:T(8,128)(2,1)}, bf16[128,256]{1,0:T(8,128)(2,1)S(1)}, u32[]{:S(2)}, u32[]{:S(2)}) collective-permute-start(bf16[128,256]{1,0:T(8,128)(2,1)} %get-tuple-element.50), channel_id=1, source_target_pairs={{0,8},{4,12},{8,0},{12,4},{1,9},{5,13},{9,1},{13,5},{2,10},{6,14},... | collective-permute-start | bytes 196616 | tf_op jit(solution)/shard_map/ppermute | solution.py:565
  16.3 20.6 %collective-permute-start.7 = (bf16[192,768]{1,0:T(8,128)(2,1)S(1)}, bf16[192,768]{1,0:T(8,128)(2,1)S(1)}, u32[]{:S(2)}, u32[]{:S(2)}) collective-permute-start(bf16[192,768]{1,0:T(8,128)(2,1)S(1)} %copy-done), channel_id=1, source_target_pairs={{0,2},{1,3},{2,0},{3,1},{4,6},{5,7},{6,4},{7,5},{8,10},{9,11},{10,... | collective-permute-start | bytes 884744 | tf_op jit(solution)/shard_map/ppermute | solution.py:559
  17.9 8.3 %copy-start.5 = (bf16[128,256]{1,0:T(8,128)(2,1)S(1)}, bf16[128,256]{1,0:T(8,128)(2,1)}, u32[]{:S(2)}) copy-start(bf16[128,256]{1,0:T(8,128)(2,1)} %get-tuple-element.52) | copy-start | bytes 196612
  17.9 9.9 %copy-start.4 = (f32[768]{0:T(1024)S(1)}, f32[768]{0:T(1024)}, u32[]{:S(2)}) copy-start(f32[768]{0:T(1024)} %param.9) | copy-start | bytes 9220
  17.9 12.7 %copy-start.2 = (bf16[128,256]{1,0:T(8,128)(2,1)S(1)}, bf16[128,256]{1,0:T(8,128)(2,1)}, u32[]{:S(2)}) copy-start(bf16[128,256]{1,0:T(8,128)(2,1)} %get-tuple-element.49.refs_0_) | copy-start | bytes 196612
  20.5 16.9 %collective-permute-start.11 = (bf16[256,512]{1,0:T(8,128)(2,1)S(1)}, bf16[256,512]{1,0:T(8,128)(2,1)S(1)}, u32[]{:S(2)}, u32[]{:S(2)}) collective-permute-start(bf16[256,512]{1,0:T(8,128)(2,1)S(1)} %get-tuple-element.46.refs_0_.lead_ref), channel_id=1, source_target_pairs={{0,2},{1,3},{2,0},{3,1},{4,6},{5,7},{6,4},{7,5},{8,10},{9,11},{10,... | collective-permute-start | bytes 786440 | tf_op jit(solution)/shard_map/ppermute | solution.py:559
  22.4 15.1 %collective-permute-start.9 = (bf16[256,512]{1,0:T(8,128)(2,1)S(1)}, bf16[256,512]{1,0:T(8,128)(2,1)S(1)}, u32[]{:S(2)}, u32[]{:S(2)}) collective-permute-start(bf16[256,512]{1,0:T(8,128)(2,1)S(1)} %get-tuple-element.46.refs_0_.lead_ref), channel_id=1, source_target_pairs={{0,1},{1,0},{2,3},{3,2},{4,5},{5,4},{6,7},{7,6},{8,9},{9,8},{10,11... | collective-permute-start | bytes 786440 | tf_op jit(solution)/shard_map/ppermute | solution.py:559
  22.4 6.3 %collective-permute-start.4 = (bf16[128,256]{1,0:T(8,128)(2,1)S(1)}, bf16[128,256]{1,0:T(8,128)(2,1)S(1)}, u32[]{:S(2)}, u32[]{:S(2)}) collective-permute-start(bf16[128,256]{1,0:T(8,128)(2,1)S(1)} %copy-done.6), channel_id=1, source_target_pairs={{0,4},{4,8},{8,12},{12,0},{1,5},{5,9},{9,13},{13,1},{2,6},{6,10},{... | collective-permute-start | bytes 196616 | tf_op jit(solution)/shard_map/ppermute | solution.py:565
  26.2 4.4 %collective-permute-start.5 = (bf16[128,256]{1,0:T(8,128)(2,1)S(1)}, bf16[128,256]{1,0:T(8,128)(2,1)S(1)}, u32[]{:S(2)}, u32[]{:S(2)}) collective-permute-start(bf16[128,256]{1,0:T(8,128)(2,1)S(1)} %copy-done.5), channel_id=1, source_target_pairs={{0,12},{4,0},{8,4},{12,8},{1,13},{5,1},{9,5},{13,9},{2,14},{6,2},{... | collective-permute-start | bytes 196616 | tf_op jit(solution)/shard_map/ppermute | solution.py:565
  30.9 4.3 %collective-permute-start.10 = (bf16[256,256]{1,0:T(8,128)(2,1)S(1)}, bf16[256,256]{1,0:T(8,128)(2,1)S(1)}, u32[]{:S(2)}, u32[]{:S(2)}) collective-permute-start(bf16[256,256]{1,0:T(8,128)(2,1)S(1)} %land_rest.1.refs_1_.rest_ref), channel_id=1, source_target_pairs={{0,1},{1,0},{2,3},{3,2},{4,5},{5,4},{6,7},{7,6},{8,9},{9,8},{10,11... | collective-permute-start | bytes 393224 | tf_op jit(solution)/shard_map/ppermute | solution.py:559
  31.0 5.9 %collective-permute-start.12 = (bf16[256,256]{1,0:T(8,128)(2,1)S(1)}, bf16[256,256]{1,0:T(8,128)(2,1)S(1)}, u32[]{:S(2)}, u32[]{:S(2)}) collective-permute-start(bf16[256,256]{1,0:T(8,128)(2,1)S(1)} %land_rest.1.refs_1_.rest_ref), channel_id=1, source_target_pairs={{0,2},{1,3},{2,0},{3,1},{4,6},{5,7},{6,4},{7,5},{8,10},{9,11},{10,... | collective-permute-start | bytes 393224 | tf_op jit(solution)/shard_map/ppermute | solution.py:559
  35.3 19.2 %collective-permute-start.6 = (bf16[192,768]{1,0:T(8,128)(2,1)S(1)}, bf16[192,768]{1,0:T(8,128)(2,1)S(1)}, u32[]{:S(2)}, u32[]{:S(2)}) collective-permute-start(bf16[192,768]{1,0:T(8,128)(2,1)S(1)} %copy-done), channel_id=1, source_target_pairs={{0,1},{1,0},{2,3},{3,2},{4,5},{5,4},{6,7},{7,6},{8,9},{9,8},{10,11... | collective-permute-start | bytes 884744 | tf_op jit(solution)/shard_map/ppermute | solution.py:559
  36.9 2.0 %collective-permute-start.14 = (bf16[256,256]{1,0:T(8,128)(2,1)S(1)}, bf16[256,256]{1,0:T(8,128)(2,1)S(1)}, u32[]{:S(2)}, u32[]{:S(2)}) collective-permute-start(bf16[256,256]{1,0:T(8,128)(2,1)S(1)} %collective-permute-done.12.rest_ref), channel_id=1, source_target_pairs={{0,1},{1,0},{2,3},{3,2},{4,5},{5,4},{6,7},{7,6},{8,9},{9,8},{10,11... | collective-permute-start | bytes 393224 | tf_op jit(solution)/shard_map/ppermute | solution.py:559
  36.9 17.6 %collective-permute-start.8 = (bf16[192,768]{1,0:T(8,128)(2,1)S(1)}, bf16[192,768]{1,0:T(8,128)(2,1)S(1)}, u32[]{:S(2)}, u32[]{:S(2)}) collective-permute-start(bf16[192,768]{1,0:T(8,128)(2,1)S(1)} %collective-permute-done.7.refs_2_), channel_id=1, source_target_pairs={{0,1},{1,0},{2,3},{3,2},{4,5},{5,4},{6,7},{7,6},{8,9},{9,8},{10,11... | collective-permute-start | bytes 884744 | tf_op jit(solution)/shard_map/ppermute | solution.py:559
  37.4 1.6 %collective-permute-start.13 = (bf16[256,512]{1,0:T(8,128)(2,1)S(1)}, bf16[256,512]{1,0:T(8,128)(2,1)S(1)}, u32[]{:S(2)}, u32[]{:S(2)}) collective-permute-start(bf16[256,512]{1,0:T(8,128)(2,1)S(1)} %collective-permute-done.11.lead_ref), channel_id=1, source_target_pairs={{0,1},{1,0},{2,3},{3,2},{4,5},{5,4},{6,7},{7,6},{8,9},{9,8},{10,11... | collective-permute-start | bytes 786440 | tf_op jit(solution)/shard_map/ppermute | solution.py:559
  39.8 10.8 %collective-permute-start.15 = (bf16[64,512]{1,0:T(8,128)(2,1)S(1)}, bf16[64,512]{1,0:T(8,128)(2,1)S(1)}, u32[]{:S(2)}, u32[]{:S(2)}) collective-permute-start(bf16[64,512]{1,0:T(8,128)(2,1)S(1)} %constant_dynamic-update-slice_fusion.refs_4_), channel_id=1, source_target_pairs={{0,8},{4,12},{8,0},{12,4},{1,9},{5,13},{9,1},{13,5},{2,10},{6,14},... | collective-permute-start | bytes 196616 | tf_op jit(solution)/shard_map/ppermute | solution.py:565
  42.7 7.9 %collective-permute-start.16 = (bf16[64,512]{1,0:T(8,128)(2,1)S(1)}, bf16[64,512]{1,0:T(8,128)(2,1)S(1)}, u32[]{:S(2)}, u32[]{:S(2)}) collective-permute-start(bf16[64,512]{1,0:T(8,128)(2,1)S(1)} %constant_dynamic-update-slice_fusion.refs_4_), channel_id=1, source_target_pairs={{0,4},{4,8},{8,12},{12,0},{1,5},{5,9},{9,13},{13,1},{2,6},{6,10},{... | collective-permute-start | bytes 196616 | tf_op jit(solution)/shard_map/ppermute | solution.py:565
  43.8 6.8 %collective-permute-start.17 = (bf16[64,512]{1,0:T(8,128)(2,1)S(1)}, bf16[64,512]{1,0:T(8,128)(2,1)S(1)}, u32[]{:S(2)}, u32[]{:S(2)}) collective-permute-start(bf16[64,512]{1,0:T(8,128)(2,1)S(1)} %constant_dynamic-update-slice_fusion.refs_4_), channel_id=1, source_target_pairs={{0,12},{4,0},{8,4},{12,8},{1,13},{5,1},{9,5},{13,9},{2,14},{6,2},{... | collective-permute-start | bytes 196616 | tf_op jit(solution)/shard_map/ppermute | solution.py:565
  52.4 2.8 %collective-permute-start.18 = (bf16[192,256]{1,0:T(8,128)(2,1)S(1)}, bf16[192,256]{1,0:T(8,128)(2,1)S(1)}, u32[]{:S(2)}, u32[]{:S(2)}) collective-permute-start(bf16[192,256]{1,0:T(8,128)(2,1)S(1)} %get-tuple-element.64), channel_id=1, source_target_pairs={{0,1},{1,0},{2,3},{3,2},{4,5},{5,4},{6,7},{7,6},{8,9},{9,8},{10,11... | collective-permute-start | bytes 294920 | tf_op jit(solution)/shard_map/ppermute | solution.py:559
  52.5 5.7 %collective-permute-start.19 = (bf16[192,256]{1,0:T(8,128)(2,1)S(1)}, bf16[192,256]{1,0:T(8,128)(2,1)S(1)}, u32[]{:S(2)}, u32[]{:S(2)}) collective-permute-start(bf16[192,256]{1,0:T(8,128)(2,1)S(1)} %get-tuple-element.65), channel_id=1, source_target_pairs={{0,2},{1,3},{2,0},{3,1},{4,6},{5,7},{6,4},{7,5},{8,10},{9,11},{10,... | collective-permute-start | bytes 294920 | tf_op jit(solution)/shard_map/ppermute | solution.py:559
  52.9 6.4 %collective-permute-start.20 = (bf16[192,256]{1,0:T(8,128)(2,1)S(1)}, bf16[192,256]{1,0:T(8,128)(2,1)S(1)}, u32[]{:S(2)}, u32[]{:S(2)}) collective-permute-start(bf16[192,256]{1,0:T(8,128)(2,1)S(1)} %get-tuple-element.66), channel_id=1, source_target_pairs={{0,3},{1,2},{2,1},{3,0},{4,7},{5,6},{6,5},{7,4},{8,11},{9,10},{10,... | collective-permute-start | bytes 294920 | tf_op jit(solution)/shard_map/ppermute | solution.py:559
  (4 other events, 15.9 us)

commit v4 on v3

--- a/solution.py
+++ b/solution.py
@@ -211,31 +211,42 @@
     return slot % middle * (inner * run) + slot // middle % inner * run + slot // last
 
 
+def slot_of(place, in_rows):
+    middle, last = DILATIONS[1], DILATIONS[2]
+    inner = last // middle
+    run = in_rows // last
+    return place % run * last + place // run % inner * middle + place // (inner * run)
+
+
 def pack_kernel(seq_count, rows_hbm, weight_hbm, route_ref, *refs):
     blocks = refs[:seq_count]
     picks = refs[seq_count:-3]
     rows_ref, weight_ref, arrived = refs[-3:]
-    in_rows = rows_ref.shape[0]
-    chunks, _, chunk = weight_ref.shape
+    in_rows = rows_ref.shape[1]
+    parts, depth, columns = weight_ref.shape
     capacity = 2 * in_rows // seq_count
-    first = weight_hbm.shape[1] - chunks * chunk if not picks else 0
-    rows_copy = pltpu.make_async_copy(rows_hbm, rows_ref, arrived.at[chunks])
-    rows_copy.start()
+    first = 0 if picks else weight_hbm.shape[1] - columns
     copies = []
-    for number in range(chunks):
-        columns = slice(first + number * chunk, first + (number + 1) * chunk)
+    for part in range(parts):
+        span = slice(part * depth, (part + 1) * depth)
         copies.append(
-            pltpu.make_async_copy(
-                weight_hbm.at[:, columns], weight_ref.at[number], arrived.at[number]
+            (
+                pltpu.make_async_copy(rows_hbm.at[:, span], rows_ref.at[part], arrived.at[2 * part]),
+                pltpu.make_async_copy(
+                    weight_hbm.at[span, first : first + columns],
+                    weight_ref.at[part],
+                    arrived.at[2 * part + 1],
+                ),
             )
         )
-        copies[number].start()
+        for copy in copies[part]:
+            copy.start()
 
     if picks:
         me = lax.axis_index("seq")
         dest = route_ref[0:1, :]
         slot = route_ref[1:2, :]
-        shift = jnp.where(dest < me, dest - me + seq_count, dest - me)
+        shift = dest ^ me
         hits = (iota((8, in_rows), 0) == shift).astype(jnp.float32)
         before = (iota((in_rows, in_rows), 0) < iota((in_rows, in_rows), 1)).astype(jnp.bfloat16)
         earlier = matmul(hits.astype(jnp.bfloat16), before)
@@ -255,20 +266,21 @@
     else:
         pick = route_ref[...]
 
-    rows_copy.wait()
-    for step in range(chunks):
-        copies[step].wait()
-        projected = matmul(rows_ref[...], weight_ref[step]).astype(jnp.bfloat16)
-        packed = matmul(pick, projected).astype(jnp.bfloat16)
-        columns = slice(step * chunk, (step + 1) * chunk)
-        for number in range(seq_count):
-            blocks[number][:capacity, columns] = packed[number * capacity : (number + 1) * capacity]
+    projected = None
+    for part in range(parts):
+        for copy in copies[part]:
+            copy.wait()
+        product = matmul(rows_ref[part], weight_ref[part])
+        projected = product if projected is None else projected + product
+    packed = matmul(pick, projected.astype(jnp.bfloat16)).astype(jnp.bfloat16)
+    for number in range(seq_count):
+        blocks[number][:capacity] = packed[number * capacity : (number + 1) * capacity]
 
 
 def pack(tile_rows, embed_weight, route, columns, seq_count):
     in_rows, depth = tile_rows.shape
     capacity = 2 * in_rows // seq_count
-    chunk = 256
+    parts = PARTS
     lead = route.dtype == jnp.int32
     hbm = pl.BlockSpec(memory_space=pltpu.HBM)
     rows = capacity + 8 if lead else capacity
@@ -280,9 +292,9 @@
         in_specs=[hbm, hbm, pl.BlockSpec(memory_space=pltpu.VMEM)],
         out_shape=shapes,
         scratch_shapes=[
-            pltpu.VMEM((in_rows, depth), jnp.bfloat16),
-            pltpu.VMEM((columns // chunk, depth, chunk), jnp.bfloat16),
-            pltpu.SemaphoreType.DMA((columns // chunk + 1,)),
+            pltpu.VMEM((parts, in_rows, depth // parts), jnp.bfloat16),
+            pltpu.VMEM((parts, depth // parts, columns), jnp.bfloat16),
+            pltpu.SemaphoreType.DMA((2 * parts,)),
         ],
         cost_estimate=cost(2 * in_rows * columns * (depth + seq_count * capacity)),
         compiler_params=pltpu.CompilerParams(vmem_limit_bytes=62 << 20),
@@ -374,7 +386,7 @@
 
 
 def project_block(rows, weight, head_dim):
-    out = matmul(rows, weight)
+    out = matmul(rows, weight, ((1,), (1,)))
     third = out.shape[1] // 3
     lanes = iota((1, out.shape[1]), 1)
     ones = (lanes >= 2 * third) & (lanes % HALF == head_dim)
@@ -390,14 +402,15 @@
     run = in_rows // last
     third = heads_here * HALF
     inner = lax.axis_index("head") % (last // middle)
-    low = iota((1, 2 * HALF), 1) < HALF
-    for column in range(third, 3 * third, 2 * HALF):
-        both = []
-        for side in range(2):
-            member = column % third // HALF + side
+    pieces = []
+    for part in (1, 2):
+        for member in range(heads_here):
             row = member * (in_rows // middle) + inner * run
-            both.append(out_ref[pl.ds(pl.multiple_of(row, run), run), column : column + 2 * HALF])
-        far_ref[:, column - third : column - third + 2 * HALF] = jnp.where(low, both[0], both[1])
+            tile = part * third + member // 2 * 2 * HALF
+            held = out_ref[pl.ds(pl.multiple_of(row, run), run), tile : tile + 2 * HALF]
+            start = member % 2 * HALF
+            pieces.append(held[:, start : start + head_dim])
+    far_ref[...] = jnp.concatenate(pieces, axis=1)
 
 
 def near_kernel(head_dim, heads_here, qkv_ref, out_ref):
@@ -424,8 +437,8 @@
     return pl.pallas_call(
         functools.partial(qkv_kernel, head_dim, heads_here),
         out_shape=[
-            jax.ShapeDtypeStruct((in_rows, weight.shape[1]), jnp.bfloat16),
-            jax.ShapeDtypeStruct((in_rows // DILATIONS[2], 2 * heads_here * HALF), jnp.bfloat16),
+            jax.ShapeDtypeStruct((in_rows, weight.shape[0]), jnp.bfloat16),
+            jax.ShapeDtypeStruct((in_rows // DILATIONS[2], 2 * heads_here * head_dim), jnp.bfloat16),
         ],
         cost_estimate=cost(2 * in_rows * weight.shape[0] * weight.shape[1]),
         compiler_params=LIMIT,
@@ -455,59 +468,101 @@
 LOG2E = 1.4426950408889634
 
 
-def wide_kernel(head_dim, heads_here, *refs):
-    sources, fars, nears, outs = refs[:4], refs[4:-8], refs[-8:-4], refs[-4:]
+def middle_kernel(head_dim, heads_here, *refs):
+    sources, out_ref = refs[:-1], refs[-1]
+    wide_rows = sources[0].shape[0] // DILATIONS[1]
+    third = heads_here * HALF
+    scale = LOG2E * head_dim ** (-0.5)
+    lanes = iota((1, 2 * HALF), 1)
+    for member in range(heads_here):
+        picked = slice(member * wide_rows, (member + 1) * wide_rows)
+        tile = member // 2 * 2 * HALF
+        side = member % 2
+
+        def gathered(part):
+            start = part * third + tile
+            return jnp.concatenate(
+                [source[picked, start : start + 2 * HALF] for source in sources], axis=0
+            )
+
+        queries = gathered(0) * (lanes // HALF == side).astype(jnp.bfloat16)
+        scores = matmul(gathered(1), queries, ((1,), (1,)))
+        values = gathered(2).T[side * HALF : (side + 1) * HALF]
+        total, top = softmax_product([scores], scale, [values])
+        start = member * HALF
+        out_ref[start : start + HALF] = total
+        out_ref[start + HALF - 8 : start + HALF] = jnp.broadcast_to(top, (8, total.shape[1]))
+
+
+def middle_of(sources, head_dim, heads_here):
+    lanes = len(sources) * sources[0].shape[0] // DILATIONS[1]
+    return pl.pallas_call(
+        functools.partial(middle_kernel, head_dim, heads_here),
+        out_shape=jax.ShapeDtypeStruct((heads_here * HALF, lanes), jnp.float32),
+        cost_estimate=cost(heads_here * 8 * lanes * lanes * 128),
+        compiler_params=LIMIT,
+        name="middle",
+    )(*sources)
+
+
+def joined_totals(first, first_top, second, second_top, scale):
+    peak = jnp.maximum(first_top, second_top)
+    first_weight = jnp.exp2((first_top - peak) * scale)
+    second_weight = jnp.exp2((second_top - peak) * scale)
+    return first * first_weight + second * second_weight, peak
+
+
+def wide_kernel(head_dim, heads_here, numbers, middle_ref, *refs):
+    count = len(numbers)
+    sources, fars = refs[:count], refs[count : -2 * count]
+    nears, outs = refs[-2 * count : -count], refs[-count:]
     in_rows = sources[0].shape[0]
     middle, last = DILATIONS[1], DILATIONS[2]
     wide = in_rows // middle
     run = in_rows // last
-    third = heads_here * HALF
     scale = LOG2E * head_dim ** (-0.5)
     inner = lax.axis_index("head") % (last // middle)
-    lanes = iota((1, 2 * HALF), 1)
-    chosen = iota((1, in_rows), 1) // run % (last // middle) == inner
-    for pair in range(heads_here // 2):
-        span = slice(pair * 2 * HALF, (pair + 1) * 2 * HALF)
-        keys_at = slice(third + span.start, third + span.stop)
-        values_at = slice(2 * third + span.start, 2 * third + span.stop)
-        far_keys = jnp.concatenate([far[:, span] for far in fars], axis=0)
-        far_turned = jnp.concatenate(
-            [far[:, third + span.start : third + span.stop] for far in fars], axis=0
-        ).T
-        for side in range(2):
-            member = 2 * pair + side
-            mine = (lanes // HALF == side).astype(jnp.bfloat16)
-            held = slice(side * HALF, (side + 1) * HALF)
-            picked = slice(member * wide, (member + 1) * wide)
-
-            def gathered(columns):
-                return jnp.concatenate([source[picked, columns] for source in sources], axis=0)
-
-            picked_queries = gathered(span) * mine
-            middle_scores = matmul(gathered(keys_at), picked_queries, ((1,), (1,)))
-            far_scores = matmul(far_keys, picked_queries, ((1,), (1,)))
-            far_scores = jnp.where(chosen, far_scores, -1e30)
-            wide_total, wide_top = softmax_product(
-                [middle_scores, far_scores], scale, [gathered(values_at).T[held], far_turned[held]]
-            )
-            for number in range(4):
-                base = member * HALF
-                total = nears[number][base : base + HALF]
-                top = nears[number][base + HALF - 8 : base + HALF][:1]
-                extra, extra_top = place_lanes(wide_total, wide_top, number, member, wide)
-                tile = member * wide // 128 * 128
-                at = slice(tile, tile + 128)
-                inside = iota((1, 128), 1) // wide == member % (128 // wide)
-                extra_top = jnp.where(inside, extra_top, -1e30)
-                peak = jnp.maximum(top[:, at], extra_top)
-                old = jnp.exp2((top[:, at] - peak) * scale)
-                new = jnp.exp2((extra_top - peak) * scale)
-                merged = total[:, at] * old + jnp.where(inside, extra * new, 0.0)
-                rows = slice(member * head_dim, (member + 1) * head_dim)
-                for other in range(0, in_rows, 128):
-                    part = merged if other == tile else total[:, other : other + 128]
-                    done = part[:head_dim] / part[head_dim : head_dim + 1]
-                    outs[number][rows, other : other + 128] = done.astype(jnp.bfloat16)
+    chosen = iota((1, count * wide), 1) // run % (last // middle) == inner
+    lanes_at = slice(numbers[0] * wide, (numbers[0] + count) * wide)
+    far_rows = jnp.concatenate([far[...] for far in fars], axis=0)
+    sums = (iota((HALF - head_dim, far_rows.shape[0]), 0) == 0).astype(jnp.bfloat16)
+    for member in range(heads_here):
+        base = member * HALF
+        picked = slice(member * wide, (member + 1) * wide)
+        tile = member // 2 * 2 * HALF
+        start = member % 2 * HALF
+        queries = jnp.concatenate(
+            [source[picked, tile : tile + 2 * HALF] for source in sources], axis=0
+        )[:, start : start + head_dim]
+        keys = far_rows[:, member * head_dim : (member + 1) * head_dim]
+        first = (heads_here + member) * head_dim
+        values = jnp.concatenate([far_rows[:, first : first + head_dim].T, sums], axis=0)
+        scores = jnp.where(chosen, matmul(keys, queries, ((1,), (1,))), -1e30)
+        far_total, far_top = softmax_product([scores], scale, [values])
+        wide_total, wide_top = joined_totals(
+            middle_ref[base : base + HALF, lanes_at],
+            middle_ref[base + HALF - 8 : base + HALF, lanes_at][:1],
+            far_total,
+            far_top,
+            scale,
+        )
+        for number in range(count):
+            total = nears[number][base : base + HALF]
+            top = nears[number][base + HALF - 8 : base + HALF][:1]
+            extra, extra_top = place_lanes(wide_total, wide_top, number, member, wide)
+            tile = member * wide // 128 * 128
+            at = slice(tile, tile + 128)
+            inside = iota((1, 128), 1) // wide == member % (128 // wide)
+            extra_top = jnp.where(inside, extra_top, -1e30)
+            peak = jnp.maximum(top[:, at], extra_top)
+            old = jnp.exp2((top[:, at] - peak) * scale)
+            new = jnp.exp2((extra_top - peak) * scale)
+            merged = total[:, at] * old + jnp.where(inside, extra * new, 0.0)
+            rows = slice(member * head_dim, (member + 1) * head_dim)
+            for other in range(0, in_rows, 128):
+                part = merged if other == tile else total[:, other : other + 128]
+                done = part[:head_dim] / part[head_dim : head_dim + 1]
+                outs[number][rows, other : other + 128] = done.astype(jnp.bfloat16)
 
 
 def place_lanes(total, top, number, member, wide):
@@ -520,38 +575,45 @@
     return total, top
 
 
-def attention_blocks(sources, fars, nears, head_dim, heads_here):
+def wide(middle, sources, fars, nears, numbers, head_dim, heads_here):
     in_rows = sources[0].shape[0]
     out = jax.ShapeDtypeStruct((heads_here * head_dim, in_rows), jnp.bfloat16)
     return pl.pallas_call(
-        functools.partial(wide_kernel, head_dim, heads_here),
-        out_shape=[out] * 4,
-        cost_estimate=cost(8 * 4 * in_rows * in_rows * 128),
+        functools.partial(wide_kernel, head_dim, heads_here, numbers),
+        out_shape=[out] * len(numbers),
+        cost_estimate=cost(4 * 4 * in_rows * in_rows * 128),
         compiler_params=LIMIT,
-        name="wide",
-    )(*sources, *fars, *nears)
-
-
-def finish_kernel(turned_ref, weight_ref, *refs):
+    )(
+        middle,
+        *[sources[number] for number in numbers],
+        *fars,
+        *[nears[number] for number in numbers],
+    )
+
+
+def start_kernel(turned_ref, weight_ref, *refs):
     pieces, out_ref = refs[:-1], refs[-1]
     joined = jnp.concatenate([piece[...] for piece in pieces], axis=0)
-    branch = matmul(weight_ref[...], joined)
-    mixed = (turned_ref[...].astype(jnp.float32) + branch).astype(jnp.bfloat16)
+    out_ref[...] = turned_ref[...].astype(jnp.float32) + matmul(weight_ref[...], joined)
+
+
+def finish_kernel(begun_ref, weight_ref, *refs):
+    pieces, out_ref = refs[:-1], refs[-1]
+    joined = jnp.concatenate([piece[...] for piece in pieces], axis=0)
+    mixed = (begun_ref[...] + matmul(weight_ref[...], joined)).astype(jnp.bfloat16)
     in_rows = out_ref.shape[0]
-    square = (in_rows, in_rows)
-    back = landed_place(iota(square, 0), in_rows) == iota(square, 1)
+    back = iota((in_rows, in_rows), 0) == slot_of(iota((1, in_rows), 1), in_rows)
     out_ref[...] = matmul(back.astype(jnp.bfloat16), mixed, ((1,), (1,))).astype(jnp.bfloat16)
 
 
-def finish(turned, weight, pieces):
-    width, in_rows = turned.shape
+def with_pieces(kernel, begun, weight, pieces, shape):
+    width, in_rows = begun.shape
     return pl.pallas_call(
-        finish_kernel,
-        out_shape=jax.ShapeDtypeStruct((in_rows, width), jnp.bfloat16),
+        kernel,
+        out_shape=shape,
         cost_estimate=cost(2 * in_rows * width * (width + in_rows)),
         compiler_params=LIMIT,
-        name="finish",
-    )(turned, weight, *pieces)
+    )(begun, weight, *pieces)
 
 
 def across(block, bit):
@@ -561,7 +623,7 @@
 
 def shifted(block, shift):
     count = lax.axis_size("seq")
-    pairs = [(member, (member + shift) % count) for member in range(count)]
+    pairs = [(member, member ^ shift) for member in range(count)]
     return lax.ppermute(block, "seq", pairs)
 
 
@@ -575,7 +637,7 @@
     return (
         segments == [in_rows, rows_here, total_rows]
         and head_count == 4
-        and seq_count <= 8
+        and seq_count == 4
         and heads_here == DILATIONS[1] == DILATIONS[2] // DILATIONS[1]
         and in_rows == 4 * HALF
         and head_dim % 16 == 0
@@ -588,9 +650,9 @@
     in_rows = tile_rows.shape[0]
     width = embed_weight.shape[1]
     heads_here, head_dim = qkv_weight.shape[1], qkv_weight.shape[3]
-    lead_width = LEAD * width // 3
+    lead_width = width // 2
     route = tile_route.T
-    order = sorted(range(1, seq_count), key=lambda shift: -min(shift, seq_count - shift))
+    order = sorted(range(1, seq_count), key=lambda shift: shift < seq_count // 2)
     lead, pick = pack(tile_rows, embed_weight, route, lead_width, seq_count)
     lead_in = [lead[0]] + [shifted(lead[shift], shift) for shift in order]
     rest, _ = pack(tile_rows, embed_weight, pick, width - lead_width, seq_count)
@@ -601,9 +663,10 @@
     out_over = across(out_weight, 2)
     out_pieces = [out_weight, across(out_weight, 1), out_over]
     out_pieces.append(across(out_over, 1))
-    turned_weight = turn(out_pieces, False)
-    by_kind = jnp.transpose(qkv_weight, (0, 2, 1, 3))
-    weight = jnp.pad(by_kind, ((0, 0), (0, 0), (0, 0), (0, HALF - head_dim))).reshape(width, -1)
+    turned_here = turn(out_pieces[:2], False)
+    turned_there = turn(out_pieces[2:], False)
+    by_kind = jnp.transpose(qkv_weight, (2, 1, 3, 0))
+    weight = jnp.pad(by_kind, ((0, 0), (0, 0), (0, HALF - head_dim), (0, 0))).reshape(-1, width)
     lead_in, weight = lax.optimization_barrier((lead_in, weight))
     rows_lead, here = land(lead_in, in_rows)
     lead_over = across(rows_lead, 2)
@@ -629,12 +692,18 @@
     step([lead_both, rest_both])
     far = jnp.concatenate(far_parts, axis=0)
     fars = [far] + [shifted(far, shift) for shift in order]
-    parts = attention_blocks(sources, fars, nears, head_dim, heads_here)
-    joined = [parts[0]] + [across(parts[bit], bit) for bit in range(1, 4)]
-    return finish(turned, turned_weight, joined)
-
-
-LEAD = 2
+    middle = middle_of(sources, head_dim, heads_here)
+    there = wide(middle, sources, fars, nears, (2, 3), head_dim, heads_here)
+    here = wide(middle, sources, fars, nears, (0, 1), head_dim, heads_here)
+    near_pieces = [here[0], across(here[1], 1)]
+    far_pieces = [across(there[0], 2), across(there[1], 3)]
+    shape = jax.ShapeDtypeStruct(turned.shape, jnp.float32)
+    begun = with_pieces(start_kernel, turned, turned_here, near_pieces, shape)
+    shape = jax.ShapeDtypeStruct((in_rows, width), jnp.bfloat16)
+    return with_pieces(finish_kernel, begun, turned_there, far_pieces, shape)
+
+
+PARTS = 2
 
 
 def local(tile_rows, tile_route, embed_weight, norm_gain, qkv_weight, out_weight):

time: 61 us -> 64 us (1.049)
  waiting for transfers between devices: 9.38 us -> 18.4 us
  starting transfers between devices: 27 us -> 22 us
  local copies, waits for them, and re-layouts: 2.82 us -> 0.22 us
  Pallas kernels: 21.2 us -> 22.8 us
    ppermute x12, waiting for transfers between devices: 5.58 us -> 10.3 us  [across(): lax.ppermute(block, 'head', [(member, member ^ bit) for member in range(c...]
    ppermute x9, starting transfers between devices: 20.2 us -> 15.6 us  [shifted(): return lax.ppermute(block, 'seq', pairs)]
    ppermute x9, waiting for transfers between devices: 3.8 us -> 8.13 us  [shifted(): return lax.ppermute(block, 'seq', pairs)]
    pallas_call x2 -> x5, Pallas kernels: 3.35 us -> 5.1 us  [the longest x2 1.91 us: wide(): pl.pallas_call(functools.partial(wide_kernel, head_dim, heads_here, numbe...]
    optimization_barrier x2 -> x0, local copies, waits for them, and re-layouts: 1.62 us -> none  [the longest x1 1.56 us: fast(): lead_in, weight = lax.optimization_barrier((lead_in, weight))]
    pad x1, local copies, waits for them, and re-layouts: 1.15 us -> 0.1 us  [fast(): jnp.pad(by_kind, ((0, 0), (0, 0), (0, HALF - head_dim), (0, 0)))]
  transfers between devices with their start and end apart: 21 -> 21, of which waited for: 8 -> 7; matrix products, arithmetic and copies ran while one was open for 5% -> 0% of each run, Pallas kernels for 25% -> 28%
where the time goes in v4:
time: 64 us; the launch traced here: 63.7 us
  Pallas kernels  22.8 us (36%)
  starting transfers between devices  22 us (34%)
  waiting for transfers between devices  18.4 us (29%)
    ppermute x9, starting transfers between devices, shifted(): return lax.ppermute(block, 'seq', pairs)  15.6 us
    ppermute x12, waiting for transfers between devices, across(): lax.ppermute(block, 'head', [(member, member ^ bit) for member in range(c...  10.3 us
    ppermute x9, waiting for transfers between devices, shifted(): return lax.ppermute(block, 'seq', pairs)  8.13 us
    pallas_call x2, Pallas kernels, pack(): pl.pallas_call(functools.partial(pack_kernel, seq_count), in_specs=[hbm,...  7.72 us
    ppermute x12, starting transfers between devices, across(): lax.ppermute(block, 'head', [(member, member ^ bit) for member in range(c...  6.37 us
    pallas_call x4, Pallas kernels, near(): pl.pallas_call(functools.partial(near_kernel, head_dim, heads_here), out_...  5.35 us
    pallas_call x4, Pallas kernels, qkv_of(): pl.pallas_call(functools.partial(qkv_kernel, head_dim, heads_here), out_s...  3.03 us
    pallas_call x2, Pallas kernels, wide(): pl.pallas_call(functools.partial(wide_kernel, head_dim, heads_here, numbe...  1.91 us
  transfers between devices with their start and end apart: 21, of which 7 were waited for; matrix products, arithmetic and copies ran while one was open for 0% of the time, Pallas kernels for 28%

profile of v4, /device:TPU:0, one launch (start us, length us, event | category | flops | bytes accessed | tf_op | source)
XLA Modules:
  0.0 63.7 jit_solution(10738725995042885176)
XLA Ops:
  0.0 3.8 %shard_map.64 = (bf16[136,384]{1,0:T(8,128)(2,1)}, bf16[136,384]{1,0:T(8,128)(2,1)}, bf16[136,384]{1,0:T(8,128)(2,1)}, bf16[136,384]{1,0:T(8,128)(2,1)}, bf16[512,256]{1,0:T(8,128)(2,1)}) custom-call(bf16[256,1536]{1,0:T(8,128)(2,1)} %rows_hbm.3, bf16[1536,768]{1,0:T(8,128)(2,1)} %weight_hbm.3, s32[2,256]{1,0:T(2,128)} %bitcast.8), custom_call_target="tpu_custom_call" | custom-call | flops 402653184 | bytes 1048576 | tf_op jit(solution)/shard_map/pallas_call | solution.py:290
  3.8 4.1 %collective-permute-start = (bf16[136,384]{1,0:T(8,128)(2,1)}, bf16[136,384]{1,0:T(8,128)(2,1)S(1)}, u32[]{:S(2)}, u32[]{:S(2)}) collective-permute-start(bf16[136,384]{1,0:T(8,128)(2,1)} %get-tuple-element.38), channel_id=1, source_target_pairs={{0,8},{4,12},{8,0},{12,4},{1,9},{5,13},{9,1},{13,5},{2,10},{6,14},... | collective-permute-start | bytes 313352 | tf_op jit(solution)/shard_map/ppermute | solution.py:627
  7.9 1.3 %collective-permute-start.1 = (bf16[136,384]{1,0:T(8,128)(2,1)}, bf16[136,384]{1,0:T(8,128)(2,1)S(1)}, u32[]{:S(2)}, u32[]{:S(2)}) collective-permute-start(bf16[136,384]{1,0:T(8,128)(2,1)} %get-tuple-element.39), channel_id=1, source_target_pairs={{0,12},{4,8},{8,4},{12,0},{1,13},{5,9},{9,5},{13,1},{2,14},{6,10},... | collective-permute-start | bytes 313352 | tf_op jit(solution)/shard_map/ppermute | solution.py:627
  9.5 4.0 %shard_map.65 = (bf16[128,384]{1,0:T(8,128)(2,1)}, bf16[128,384]{1,0:T(8,128)(2,1)}, bf16[128,384]{1,0:T(8,128)(2,1)}, bf16[128,384]{1,0:T(8,128)(2,1)}) custom-call(bf16[256,1536]{1,0:T(8,128)(2,1)} %rows_hbm.3, bf16[1536,768]{1,0:T(8,128)(2,1)} %weight_hbm.3, bf16[512,256]{1,0:T(8,128)(2,1)} %get-tuple-element.48.route_ref), custom_call_target="tpu_custom_call" | custom-call | flops 402653184 | bytes 1048576 | tf_op jit(solution)/shard_map/pallas_call | solution.py:290
  13.5 2.9 %collective-permute-start.3 = (bf16[128,384]{1,0:T(8,128)(2,1)}, bf16[128,384]{1,0:T(8,128)(2,1)S(1)}, u32[]{:S(2)}, u32[]{:S(2)}) collective-permute-start(bf16[128,384]{1,0:T(8,128)(2,1)} %get-tuple-element.50), channel_id=1, source_target_pairs={{0,8},{4,12},{8,0},{12,4},{1,9},{5,13},{9,1},{13,5},{2,10},{6,14},... | collective-permute-start | bytes 294920 | tf_op jit(solution)/shard_map/ppermute | solution.py:627
  16.4 1.4 %collective-permute-start.4 = (bf16[128,384]{1,0:T(8,128)(2,1)}, bf16[128,384]{1,0:T(8,128)(2,1)S(1)}, u32[]{:S(2)}, u32[]{:S(2)}) collective-permute-start(bf16[128,384]{1,0:T(8,128)(2,1)} %get-tuple-element.51), channel_id=1, source_target_pairs={{0,12},{4,8},{8,4},{12,0},{1,13},{5,9},{9,5},{13,1},{2,14},{6,10},... | collective-permute-start | bytes 294920 | tf_op jit(solution)/shard_map/ppermute | solution.py:627
  17.7 1.6 %collective-permute-start.17 = (bf16[192,768]{1,0:T(8,128)(2,1)S(1)}, bf16[192,768]{1,0:T(8,128)(2,1)S(1)}, u32[]{:S(2)}, u32[]{:S(2)}) collective-permute-start(bf16[192,768]{1,0:T(8,128)(2,1)S(1)} %copy-done), channel_id=1, source_target_pairs={{0,2},{1,3},{2,0},{3,1},{4,6},{5,7},{6,4},{7,5},{8,10},{9,11},{10,... | collective-permute-start | bytes 884744 | tf_op jit(solution)/shard_map/ppermute | solution.py:621
  19.9 5.1 %collective-permute-done.3.refs_1_ = bf16[128,384]{1,0:T(8,128)(2,1)S(1)} collective-permute-done((bf16[128,384]{1,0:T(8,128)(2,1)}, bf16[128,384]{1,0:T(8,128)(2,1)S(1)}, u32[]{:S(2)}, u32[]{:S(2)}) %collective-permute-start.3) | collective-permute-done | bytes 98336 | tf_op jit(solution)/shard_map/ppermute | solution.py:627
  25.6 1.7 %collective-permute-start.10 = (bf16[256,384]{1,0:T(8,128)(2,1)S(1)}, bf16[256,384]{1,0:T(8,128)(2,1)S(1)}, u32[]{:S(2)}, u32[]{:S(2)}) collective-permute-start(bf16[256,384]{1,0:T(8,128)(2,1)S(1)} %land_rest.1.refs_1_.rest_ref), channel_id=1, source_target_pairs={{0,2},{1,3},{2,0},{3,1},{4,6},{5,7},{6,4},{7,5},{8,10},{9,11},{10,... | collective-permute-start | bytes 589832 | tf_op jit(solution)/shard_map/ppermute | solution.py:621
  28.4 1.3 %shard_map.72.refs_6_ = f32[256,256]{1,0:T(8,128)S(1)} custom-call(bf16[256,768]{1,0:T(8,128)(2,1)S(1)} %get-tuple-element.55.refs_0_.qkv_ref), custom_call_target="tpu_custom_call" | custom-call | flops 268435456 | bytes 1048576 | tf_op jit(solution)/shard_map/pallas_call | solution.py:450
  30.4 2.9 %collective-permute-done.10.rest_ref = bf16[256,384]{1,0:T(8,128)(2,1)S(1)} collective-permute-done((bf16[256,384]{1,0:T(8,128)(2,1)S(1)}, bf16[256,384]{1,0:T(8,128)(2,1)S(1)}, u32[]{:S(2)}, u32[]{:S(2)}) %collective-permute-start.10) | collective-permute-done | bytes 196640 | tf_op jit(solution)/shard_map/ppermute | solution.py:621
  33.4 3.7 %collective-permute-done.9.lead_ref = bf16[256,384]{1,0:T(8,128)(2,1)S(1)} collective-permute-done((bf16[256,384]{1,0:T(8,128)(2,1)S(1)}, bf16[256,384]{1,0:T(8,128)(2,1)S(1)}, u32[]{:S(2)}, u32[]{:S(2)}) %collective-permute-start.9) | collective-permute-done | bytes 196640 | tf_op jit(solution)/shard_map/ppermute | solution.py:621
  38.6 1.3 %shard_map.77.refs_6_ = f32[256,256]{1,0:T(8,128)S(1)} custom-call(bf16[256,768]{1,0:T(8,128)(2,1)S(1)} %get-tuple-element.57.refs_2_.qkv_ref.refs_0_), custom_call_target="tpu_custom_call" | custom-call | flops 268435456 | bytes 1048576 | tf_op jit(solution)/shard_map/pallas_call | solution.py:450
  40.8 5.0 %collective-permute-start.13 = (bf16[64,384]{1,0:T(8,128)(2,1)S(1)}, bf16[64,384]{1,0:T(8,128)(2,1)S(1)}, u32[]{:S(2)}, u32[]{:S(2)}) collective-permute-start(bf16[64,384]{1,0:T(8,128)(2,1)S(1)} %constant_dynamic-update-slice_fusion.refs_2_), channel_id=1, source_target_pairs={{0,8},{4,12},{8,0},{12,4},{1,9},{5,13},{9,1},{13,5},{2,10},{6,14},... | collective-permute-start | bytes 147464 | tf_op jit(solution)/shard_map/ppermute | solution.py:627
  46.4 1.3 %shard_map.73.refs_7_ = f32[256,256]{1,0:T(8,128)S(1)} custom-call(bf16[256,768]{1,0:T(8,128)(2,1)S(1)} %get-tuple-element.56.refs_1_.qkv_ref), custom_call_target="tpu_custom_call" | custom-call | flops 268435456 | bytes 1048576 | tf_op jit(solution)/shard_map/pallas_call | solution.py:450
  47.8 1.3 %middle.1.middle_ref = f32[256,256]{1,0:T(8,128)S(1)} custom-call(bf16[256,768]{1,0:T(8,128)(2,1)S(1)} %get-tuple-element.55.refs_0_.qkv_ref, bf16[256,768]{1,0:T(8,128)(2,1)S(1)} %get-tuple-element.56.refs_1_.qkv_ref, bf16[256,768]{1,0:T(8,128)(2,1)S(1)} %get-tuple-element.57.refs_2_.qkv_ref.refs_0_, ...), custom_call_target="tpu_custom_call" | custom-call | flops 268435456 | bytes 1048576 | tf_op jit(solution)/shard_map/middle/pallas_call | solution.py:499
  49.1 2.9 %collective-permute-done.14.refs_4_ = bf16[64,384]{1,0:T(8,128)(2,1)S(1)} collective-permute-done((bf16[64,384]{1,0:T(8,128)(2,1)S(1)}, bf16[64,384]{1,0:T(8,128)(2,1)S(1)}, u32[]{:S(2)}, u32[]{:S(2)}) %collective-permute-start.14) | collective-permute-done | bytes 49184 | tf_op jit(solution)/shard_map/ppermute | solution.py:627
  52.0 1.0 %shard_map.74 = (bf16[192,256]{1,0:T(8,128)(2,1)S(1)}, bf16[192,256]{1,0:T(8,128)(2,1)S(1)}) custom-call(f32[256,256]{1,0:T(8,128)S(1)} %middle.1.middle_ref, bf16[256,768]{1,0:T(8,128)(2,1)S(1)} %get-tuple-element.55.refs_0_.qkv_ref, bf16[256,768]{1,0:T(8,128)(2,1)S(1)} %get-tuple-element.56.refs_1_.qkv_ref, ...), custom_call_target="tpu_custom_call" | custom-call | flops 134217728 | bytes 1048576 | tf_op jit(solution)/shard_map/pallas_call | solution.py:581
  53.0 1.3 %shard_map.78.refs_7_ = f32[256,256]{1,0:T(8,128)S(1)} custom-call(bf16[256,768]{1,0:T(8,128)(2,1)S(1)} %get-tuple-element.58.refs_3_.qkv_ref.refs_1_), custom_call_target="tpu_custom_call" | custom-call | flops 268435456 | bytes 1048576 | tf_op jit(solution)/shard_map/pallas_call | solution.py:450
  54.4 1.0 %shard_map.79 = (bf16[192,256]{1,0:T(8,128)(2,1)S(1)}, bf16[192,256]{1,0:T(8,128)(2,1)S(1)}) custom-call(f32[256,256]{1,0:T(8,128)S(1)} %middle.1.middle_ref, bf16[256,768]{1,0:T(8,128)(2,1)S(1)} %get-tuple-element.57.refs_2_.qkv_ref.refs_0_, bf16[256,768]{1,0:T(8,128)(2,1)S(1)} %get-tuple-element.58.refs_3_.qkv_ref.refs_1_, ...), custom_call_target="tpu_custom_call" | custom-call | flops 134217728 | bytes 1048576 | tf_op jit(solution)/shard_map/pallas_call | solution.py:581
  55.3 1.6 %collective-permute-start.19 = (bf16[192,256]{1,0:T(8,128)(2,1)S(1)}, bf16[192,256]{1,0:T(8,128)(2,1)S(1)}, u32[]{:S(2)}, u32[]{:S(2)}) collective-permute-start(bf16[192,256]{1,0:T(8,128)(2,1)S(1)} %get-tuple-element.65), channel_id=1, source_target_pairs={{0,2},{1,3},{2,0},{3,1},{4,6},{5,7},{6,4},{7,5},{8,10},{9,11},{10,... | collective-permute-start | bytes 294920 | tf_op jit(solution)/shard_map/ppermute | solution.py:621
  58.6 2.5 %collective-permute-done.19.refs_0_ = bf16[192,256]{1,0:T(8,128)(2,1)S(1)} collective-permute-done((bf16[192,256]{1,0:T(8,128)(2,1)S(1)}, bf16[192,256]{1,0:T(8,128)(2,1)S(1)}, u32[]{:S(2)}, u32[]{:S(2)}) %collective-permute-start.19) | collective-permute-done | bytes 98336 | tf_op jit(solution)/shard_map/ppermute | solution.py:621
  61.1 1.2 %collective-permute-done.20.refs_1_ = bf16[192,256]{1,0:T(8,128)(2,1)S(1)} collective-permute-done((bf16[192,256]{1,0:T(8,128)(2,1)S(1)}, bf16[192,256]{1,0:T(8,128)(2,1)S(1)}, u32[]{:S(2)}, u32[]{:S(2)}) %collective-permute-start.20) | collective-permute-done | bytes 98336 | tf_op jit(solution)/shard_map/ppermute | solution.py:621
  62.2 1.5 %shard_map.80 = bf16[256,768]{1,0:T(8,128)(2,1)} custom-call(f32[768,256]{1,0:T(8,128)S(1)} %shard_map.75.begun_ref, bf16[768,384]{1,0:T(8,128)(2,1)S(1)} %shard_map.76.weight_ref, bf16[192,256]{1,0:T(8,128)(2,1)S(1)} %collective-permute-done.19.refs_0_, bf16[192,256]{1,0:T(8,128)(2,1)S(1)} %collective-permute-done.20.refs_1_), custom_call_target="tpu_custom_call" | custom-call | flops 402653184 | bytes 1048576 | tf_op jit(solution)/shard_map/pallas_call | solution.py:611
  (55 shorter events, 7.8 us)
Async XLA Ops:
  3.8 14.0 %copy-start = (bf16[192,768]{1,0:T(8,128)(2,1)S(1)}, bf16[192,768]{1,0:T(8,128)(2,1)}, u32[]{:S(2)}) copy-start(bf16[192,768]{1,0:T(8,128)(2,1)} %refs_0_) | copy-start | bytes 884740
  3.8 15.5 %copy-start.3 = (bf16[768,4,3,48]{0,3,2,1:T(8,128)(2,1)S(1)}, bf16[768,4,3,48]{0,3,2,1:T(8,128)(2,1)}, u32[]{:S(2)}) copy-start(bf16[768,4,3,48]{0,3,2,1:T(8,128)(2,1)} %param.10) | copy-start | bytes 2654212
  3.8 13.9 %collective-permute-start = (bf16[136,384]{1,0:T(8,128)(2,1)}, bf16[136,384]{1,0:T(8,128)(2,1)S(1)}, u32[]{:S(2)}, u32[]{:S(2)}) collective-permute-start(bf16[136,384]{1,0:T(8,128)(2,1)} %get-tuple-element.38), channel_id=1, source_target_pairs={{0,8},{4,12},{8,0},{12,4},{1,9},{5,13},{9,1},{13,5},{2,10},{6,14},... | collective-permute-start | bytes 313352 | tf_op jit(solution)/shard_map/ppermute | solution.py:627
  7.9 9.8 %collective-permute-start.1 = (bf16[136,384]{1,0:T(8,128)(2,1)}, bf16[136,384]{1,0:T(8,128)(2,1)S(1)}, u32[]{:S(2)}, u32[]{:S(2)}) collective-permute-start(bf16[136,384]{1,0:T(8,128)(2,1)} %get-tuple-element.39), channel_id=1, source_target_pairs={{0,12},{4,8},{8,4},{12,0},{1,13},{5,9},{9,5},{13,1},{2,14},{6,10},... | collective-permute-start | bytes 313352 | tf_op jit(solution)/shard_map/ppermute | solution.py:627
  9.3 10.2 %collective-permute-start.2 = (bf16[136,384]{1,0:T(8,128)(2,1)}, bf16[136,384]{1,0:T(8,128)(2,1)S(1)}, u32[]{:S(2)}, u32[]{:S(2)}) collective-permute-start(bf16[136,384]{1,0:T(8,128)(2,1)} %get-tuple-element.40), channel_id=1, source_target_pairs={{0,4},{4,0},{8,12},{12,8},{1,5},{5,1},{9,13},{13,9},{2,6},{6,2},{1... | collective-permute-start | bytes 313352 | tf_op jit(solution)/shard_map/ppermute | solution.py:627
  13.5 11.6 %copy-start.2 = (bf16[128,384]{1,0:T(8,128)(2,1)S(1)}, bf16[128,384]{1,0:T(8,128)(2,1)}, u32[]{:S(2)}) copy-start(bf16[128,384]{1,0:T(8,128)(2,1)} %get-tuple-element.49.refs_0_) | copy-start | bytes 294916
  13.5 11.5 %collective-permute-start.3 = (bf16[128,384]{1,0:T(8,128)(2,1)}, bf16[128,384]{1,0:T(8,128)(2,1)S(1)}, u32[]{:S(2)}, u32[]{:S(2)}) collective-permute-start(bf16[128,384]{1,0:T(8,128)(2,1)} %get-tuple-element.50), channel_id=1, source_target_pairs={{0,8},{4,12},{8,0},{12,4},{1,9},{5,13},{9,1},{13,5},{2,10},{6,14},... | collective-permute-start | bytes 294920 | tf_op jit(solution)/shard_map/ppermute | solution.py:627
  16.4 8.6 %collective-permute-start.4 = (bf16[128,384]{1,0:T(8,128)(2,1)}, bf16[128,384]{1,0:T(8,128)(2,1)S(1)}, u32[]{:S(2)}, u32[]{:S(2)}) collective-permute-start(bf16[128,384]{1,0:T(8,128)(2,1)} %get-tuple-element.51), channel_id=1, source_target_pairs={{0,12},{4,8},{8,4},{12,0},{1,13},{5,9},{9,5},{13,1},{2,14},{6,10},... | collective-permute-start | bytes 294920 | tf_op jit(solution)/shard_map/ppermute | solution.py:627
  17.7 7.4 %collective-permute-start.5 = (bf16[128,384]{1,0:T(8,128)(2,1)}, bf16[128,384]{1,0:T(8,128)(2,1)S(1)}, u32[]{:S(2)}, u32[]{:S(2)}) collective-permute-start(bf16[128,384]{1,0:T(8,128)(2,1)} %get-tuple-element.52), channel_id=1, source_target_pairs={{0,4},{4,0},{8,12},{12,8},{1,5},{5,1},{9,13},{13,9},{2,6},{6,2},{1... | collective-permute-start | bytes 294920 | tf_op jit(solution)/shard_map/ppermute | solution.py:627
  17.7 12.0 %collective-permute-start.17 = (bf16[192,768]{1,0:T(8,128)(2,1)S(1)}, bf16[192,768]{1,0:T(8,128)(2,1)S(1)}, u32[]{:S(2)}, u32[]{:S(2)}) collective-permute-start(bf16[192,768]{1,0:T(8,128)(2,1)S(1)} %copy-done), channel_id=1, source_target_pairs={{0,2},{1,3},{2,0},{3,1},{4,6},{5,7},{6,4},{7,5},{8,10},{9,11},{10,... | collective-permute-start | bytes 884744 | tf_op jit(solution)/shard_map/ppermute | solution.py:621
  25.5 4.9 %collective-permute-start.8 = (bf16[256,384]{1,0:T(8,128)(2,1)S(1)}, bf16[256,384]{1,0:T(8,128)(2,1)S(1)}, u32[]{:S(2)}, u32[]{:S(2)}) collective-permute-start(bf16[256,384]{1,0:T(8,128)(2,1)S(1)} %land_rest.1.refs_1_.rest_ref), channel_id=1, source_target_pairs={{0,1},{1,0},{2,3},{3,2},{4,5},{5,4},{6,7},{7,6},{8,9},{9,8},{10,11... | collective-permute-start | bytes 589832 | tf_op jit(solution)/shard_map/ppermute | solution.py:621
  25.6 7.8 %collective-permute-start.10 = (bf16[256,384]{1,0:T(8,128)(2,1)S(1)}, bf16[256,384]{1,0:T(8,128)(2,1)S(1)}, u32[]{:S(2)}, u32[]{:S(2)}) collective-permute-start(bf16[256,384]{1,0:T(8,128)(2,1)S(1)} %land_rest.1.refs_1_.rest_ref), channel_id=1, source_target_pairs={{0,2},{1,3},{2,0},{3,1},{4,6},{5,7},{6,4},{7,5},{8,10},{9,11},{10,... | collective-permute-start | bytes 589832 | tf_op jit(solution)/shard_map/ppermute | solution.py:621
  27.3 9.8 %collective-permute-start.9 = (bf16[256,384]{1,0:T(8,128)(2,1)S(1)}, bf16[256,384]{1,0:T(8,128)(2,1)S(1)}, u32[]{:S(2)}, u32[]{:S(2)}) collective-permute-start(bf16[256,384]{1,0:T(8,128)(2,1)S(1)} %get-tuple-element.46.refs_0_.lead_ref), channel_id=1, source_target_pairs={{0,2},{1,3},{2,0},{3,1},{4,6},{5,7},{6,4},{7,5},{8,10},{9,11},{10,... | collective-permute-start | bytes 589832 | tf_op jit(solution)/shard_map/ppermute | solution.py:621
  27.6 9.4 %collective-permute-start.7 = (bf16[256,384]{1,0:T(8,128)(2,1)S(1)}, bf16[256,384]{1,0:T(8,128)(2,1)S(1)}, u32[]{:S(2)}, u32[]{:S(2)}) collective-permute-start(bf16[256,384]{1,0:T(8,128)(2,1)S(1)} %get-tuple-element.46.refs_0_.lead_ref), channel_id=1, source_target_pairs={{0,1},{1,0},{2,3},{3,2},{4,5},{5,4},{6,7},{7,6},{8,9},{9,8},{10,11... | collective-permute-start | bytes 589832 | tf_op jit(solution)/shard_map/ppermute | solution.py:621
  29.8 27.6 %collective-permute-start.6 = (bf16[192,768]{1,0:T(8,128)(2,1)S(1)}, bf16[192,768]{1,0:T(8,128)(2,1)S(1)}, u32[]{:S(2)}, u32[]{:S(2)}) collective-permute-start(bf16[192,768]{1,0:T(8,128)(2,1)S(1)} %copy-done), channel_id=1, source_target_pairs={{0,1},{1,0},{2,3},{3,2},{4,5},{5,4},{6,7},{7,6},{8,9},{9,8},{10,11... | collective-permute-start | bytes 884744 | tf_op jit(solution)/shard_map/ppermute | solution.py:621
  30.4 27.5 %collective-permute-start.18 = (bf16[192,768]{1,0:T(8,128)(2,1)S(1)}, bf16[192,768]{1,0:T(8,128)(2,1)S(1)}, u32[]{:S(2)}, u32[]{:S(2)}) collective-permute-start(bf16[192,768]{1,0:T(8,128)(2,1)S(1)} %collective-permute-done.17.refs_0_), channel_id=1, source_target_pairs={{0,1},{1,0},{2,3},{3,2},{4,5},{5,4},{6,7},{7,6},{8,9},{9,8},{10,11... | collective-permute-start | bytes 884744 | tf_op jit(solution)/shard_map/ppermute | solution.py:621
  33.4 6.6 %collective-permute-start.12 = (bf16[256,384]{1,0:T(8,128)(2,1)S(1)}, bf16[256,384]{1,0:T(8,128)(2,1)S(1)}, u32[]{:S(2)}, u32[]{:S(2)}) collective-permute-start(bf16[256,384]{1,0:T(8,128)(2,1)S(1)} %collective-permute-done.10.rest_ref), channel_id=1, source_target_pairs={{0,1},{1,0},{2,3},{3,2},{4,5},{5,4},{6,7},{7,6},{8,9},{9,8},{10,11... | collective-permute-start | bytes 589832 | tf_op jit(solution)/shard_map/ppermute | solution.py:621
  37.1 2.9 %collective-permute-start.11 = (bf16[256,384]{1,0:T(8,128)(2,1)S(1)}, bf16[256,384]{1,0:T(8,128)(2,1)S(1)}, u32[]{:S(2)}, u32[]{:S(2)}) collective-permute-start(bf16[256,384]{1,0:T(8,128)(2,1)S(1)} %collective-permute-done.9.lead_ref), channel_id=1, source_target_pairs={{0,1},{1,0},{2,3},{3,2},{4,5},{5,4},{6,7},{7,6},{8,9},{9,8},{10,11... | collective-permute-start | bytes 589832 | tf_op jit(solution)/shard_map/ppermute | solution.py:621
  40.8 8.4 %collective-permute-start.13 = (bf16[64,384]{1,0:T(8,128)(2,1)S(1)}, bf16[64,384]{1,0:T(8,128)(2,1)S(1)}, u32[]{:S(2)}, u32[]{:S(2)}) collective-permute-start(bf16[64,384]{1,0:T(8,128)(2,1)S(1)} %constant_dynamic-update-slice_fusion.refs_2_), channel_id=1, source_target_pairs={{0,8},{4,12},{8,0},{12,4},{1,9},{5,13},{9,1},{13,5},{2,10},{6,14},... | collective-permute-start | bytes 147464 | tf_op jit(solution)/shard_map/ppermute | solution.py:627
  45.8 6.2 %collective-permute-start.14 = (bf16[64,384]{1,0:T(8,128)(2,1)S(1)}, bf16[64,384]{1,0:T(8,128)(2,1)S(1)}, u32[]{:S(2)}, u32[]{:S(2)}) collective-permute-start(bf16[64,384]{1,0:T(8,128)(2,1)S(1)} %constant_dynamic-update-slice_fusion.refs_2_), channel_id=1, source_target_pairs={{0,12},{4,8},{8,4},{12,0},{1,13},{5,9},{9,5},{13,1},{2,14},{6,10},... | collective-permute-start | bytes 147464 | tf_op jit(solution)/shard_map/ppermute | solution.py:627
  45.8 6.2 %collective-permute-start.15 = (bf16[64,384]{1,0:T(8,128)(2,1)S(1)}, bf16[64,384]{1,0:T(8,128)(2,1)S(1)}, u32[]{:S(2)}, u32[]{:S(2)}) collective-permute-start(bf16[64,384]{1,0:T(8,128)(2,1)S(1)} %constant_dynamic-update-slice_fusion.refs_2_), channel_id=1, source_target_pairs={{0,4},{4,0},{8,12},{12,8},{1,5},{5,1},{9,13},{13,9},{2,6},{6,2},{1... | collective-permute-start | bytes 147464 | tf_op jit(solution)/shard_map/ppermute | solution.py:627
  53.0 5.3 %collective-permute-start.16 = (bf16[192,256]{1,0:T(8,128)(2,1)S(1)}, bf16[192,256]{1,0:T(8,128)(2,1)S(1)}, u32[]{:S(2)}, u32[]{:S(2)}) collective-permute-start(bf16[192,256]{1,0:T(8,128)(2,1)S(1)} %get-tuple-element.64), channel_id=1, source_target_pairs={{0,1},{1,0},{2,3},{3,2},{4,5},{5,4},{6,7},{7,6},{8,9},{9,8},{10,11... | collective-permute-start | bytes 294920 | tf_op jit(solution)/shard_map/ppermute | solution.py:621
  55.3 5.7 %collective-permute-start.19 = (bf16[192,256]{1,0:T(8,128)(2,1)S(1)}, bf16[192,256]{1,0:T(8,128)(2,1)S(1)}, u32[]{:S(2)}, u32[]{:S(2)}) collective-permute-start(bf16[192,256]{1,0:T(8,128)(2,1)S(1)} %get-tuple-element.65), channel_id=1, source_target_pairs={{0,2},{1,3},{2,0},{3,1},{4,6},{5,7},{6,4},{7,5},{8,10},{9,11},{10,... | collective-permute-start | bytes 294920 | tf_op jit(solution)/shard_map/ppermute | solution.py:621
  56.9 5.3 %collective-permute-start.20 = (bf16[192,256]{1,0:T(8,128)(2,1)S(1)}, bf16[192,256]{1,0:T(8,128)(2,1)S(1)}, u32[]{:S(2)}, u32[]{:S(2)}) collective-permute-start(bf16[192,256]{1,0:T(8,128)(2,1)S(1)} %get-tuple-element.66), channel_id=1, source_target_pairs={{0,3},{1,2},{2,1},{3,0},{4,7},{5,6},{6,5},{7,4},{8,11},{9,10},{10,... | collective-permute-start | bytes 294920 | tf_op jit(solution)/shard_map/ppermute | solution.py:621
  (2 other events, 14.4 us)

commit v5 on v4

--- a/solution.py
+++ b/solution.py
@@ -297,7 +297,7 @@
             pltpu.SemaphoreType.DMA((2 * parts,)),
         ],
         cost_estimate=cost(2 * in_rows * columns * (depth + seq_count * capacity)),
-        compiler_params=pltpu.CompilerParams(vmem_limit_bytes=62 << 20),
+        compiler_params=pltpu.CompilerParams(vmem_limit_bytes=54000 << 10),
     )(tile_rows, embed_weight, route)
     return results[:seq_count], results[-1]
 
@@ -691,7 +691,7 @@
     step([lead_over, rest_over])
     step([lead_both, rest_both])
     far = jnp.concatenate(far_parts, axis=0)
-    fars = [far] + [shifted(far, shift) for shift in order]
+    fars = [far] + [shifted(far, shift) for shift in (3, 2, 1)]
     middle = middle_of(sources, head_dim, heads_here)
     there = wide(middle, sources, fars, nears, (2, 3), head_dim, heads_here)
     here = wide(middle, sources, fars, nears, (0, 1), head_dim, heads_here)
@@ -703,7 +703,7 @@
     return with_pieces(finish_kernel, begun, turned_there, far_pieces, shape)
 
 
-PARTS = 2
+PARTS = 3
 
 
 def local(tile_rows, tile_route, embed_weight, norm_gain, qkv_weight, out_weight):

time: 64 us -> 61.3 us (0.958)
  Pallas kernels: 22.8 us -> 19.8 us
  waiting for transfers between devices: 18.4 us -> 17.4 us
  starting transfers between devices: 22 us -> 22.8 us
  local copies, waits for them, and re-layouts: 0.22 us -> 0.9 us
    pallas_call x2, Pallas kernels: 7.72 us -> 4.7 us  [pack(): pl.pallas_call(functools.partial(pack_kernel, seq_count), in_specs=[hbm,...]
    ppermute x9, waiting for transfers between devices: 8.13 us -> 7.1 us  [shifted(): return lax.ppermute(block, 'seq', pairs)]
    ppermute x12, starting transfers between devices: 6.37 us -> 7.15 us  [across(): lax.ppermute(block, 'head', [(member, member ^ bit) for member in range(c...]
    unnamed x14 -> x12, local copies, waits for them, and re-layouts: 0.11 us -> 0.78 us
  transfers between devices with their start and end apart: 21 -> 21, of which waited for: 7 -> 8; matrix products, arithmetic and copies ran while one was open for 0% -> 0% of each run, Pallas kernels for 28% -> 26%
where the time goes in v5:
time: 61.3 us; the launch traced here: 61.1 us
  starting transfers between devices  22.8 us (37%)
  Pallas kernels  19.8 us (32%)
  waiting for transfers between devices  17.4 us (28%)
  local copies, waits for them, and re-layouts  0.9 us (1%)
    ppermute x9, starting transfers between devices, shifted(): return lax.ppermute(block, 'seq', pairs)  15.6 us
    ppermute x12, waiting for transfers between devices, across(): lax.ppermute(block, 'head', [(member, member ^ bit) for member in range(c...  10.3 us
    ppermute x12, starting transfers between devices, across(): lax.ppermute(block, 'head', [(member, member ^ bit) for member in range(c...  7.15 us
    ppermute x9, waiting for transfers between devices, shifted(): return lax.ppermute(block, 'seq', pairs)  7.1 us
    pallas_call x4, Pallas kernels, near(): pl.pallas_call(functools.partial(near_kernel, head_dim, heads_here), out_...  5.34 us
    pallas_call x2, Pallas kernels, pack(): pl.pallas_call(functools.partial(pack_kernel, seq_count), in_specs=[hbm,...  4.7 us
    pallas_call x4, Pallas kernels, qkv_of(): pl.pallas_call(functools.partial(qkv_kernel, head_dim, heads_here), out_s...  3.03 us
    pallas_call x2, Pallas kernels, wide(): pl.pallas_call(functools.partial(wide_kernel, head_dim, heads_here, numbe...  1.91 us
  transfers between devices with their start and end apart: 21, of which 8 were waited for; matrix products, arithmetic and copies ran while one was open for 0% of the time, Pallas kernels for 26%

profile of v5, /device:TPU:0, one launch (start us, length us, event | category | flops | bytes accessed | tf_op | source)
XLA Modules:
  0.0 61.1 jit_solution(17755685636026568818)
XLA Ops:
  0.7 2.4 %shard_map.64 = (bf16[136,384]{1,0:T(8,128)(2,1)S(1)}, bf16[136,384]{1,0:T(8,128)(2,1)S(1)}, bf16[136,384]{1,0:T(8,128)(2,1)S(1)}, bf16[136,384]{1,0:T(8,128)(2,1)S(1)}, bf16[512,256]{1,0:T(8,128)(2,1)S(1)}) custom-call(bf16[256,1536]{1,0:T(8,128)(2,1)} %rows_hbm.3, bf16[1536,768]{1,0:T(8,128)(2,1)} %weight_hbm.3, s32[2,256]{1,0:T(2,128)S(1)} %bitcast.7), custom_call_target="tpu_custom_call" | custom-call | flops 402653184 | bytes 1048576 | tf_op jit(solution)/shard_map/pallas_call | solution.py:290
  3.1 4.1 %collective-permute-start = (bf16[136,384]{1,0:T(8,128)(2,1)S(1)}, bf16[136,384]{1,0:T(8,128)(2,1)S(1)}, u32[]{:S(2)}, u32[]{:S(2)}) collective-permute-start(bf16[136,384]{1,0:T(8,128)(2,1)S(1)} %get-tuple-element.38), channel_id=1, source_target_pairs={{0,8},{4,12},{8,0},{12,4},{1,9},{5,13},{9,1},{13,5},{2,10},{6,14},... | collective-permute-start | bytes 313352 | tf_op jit(solution)/shard_map/ppermute | solution.py:627
  7.2 1.3 %collective-permute-start.1 = (bf16[136,384]{1,0:T(8,128)(2,1)S(1)}, bf16[136,384]{1,0:T(8,128)(2,1)S(1)}, u32[]{:S(2)}, u32[]{:S(2)}) collective-permute-start(bf16[136,384]{1,0:T(8,128)(2,1)S(1)} %get-tuple-element.39), channel_id=1, source_target_pairs={{0,12},{4,8},{8,4},{12,0},{1,13},{5,9},{9,5},{13,1},{2,14},{6,10},... | collective-permute-start | bytes 313352 | tf_op jit(solution)/shard_map/ppermute | solution.py:627
  8.8 2.3 %shard_map.65 = (bf16[128,384]{1,0:T(8,128)(2,1)S(1)}, bf16[128,384]{1,0:T(8,128)(2,1)S(1)}, bf16[128,384]{1,0:T(8,128)(2,1)S(1)}, bf16[128,384]{1,0:T(8,128)(2,1)S(1)}) custom-call(bf16[256,1536]{1,0:T(8,128)(2,1)} %rows_hbm.3, bf16[1536,768]{1,0:T(8,128)(2,1)} %weight_hbm.3, bf16[512,256]{1,0:T(8,128)(2,1)S(1)} %get-tuple-element.48.route_ref), custom_call_target="tpu_custom_call" | custom-call | flops 402653184 | bytes 1048576 | tf_op jit(solution)/shard_map/pallas_call | solution.py:290
  11.1 2.9 %collective-permute-start.3 = (bf16[128,384]{1,0:T(8,128)(2,1)S(1)}, bf16[128,384]{1,0:T(8,128)(2,1)S(1)}, u32[]{:S(2)}, u32[]{:S(2)}) collective-permute-start(bf16[128,384]{1,0:T(8,128)(2,1)S(1)} %get-tuple-element.50), channel_id=1, source_target_pairs={{0,8},{4,12},{8,0},{12,4},{1,9},{5,13},{9,1},{13,5},{2,10},{6,14},... | collective-permute-start | bytes 294920 | tf_op jit(solution)/shard_map/ppermute | solution.py:627
  14.0 1.3 %collective-permute-start.4 = (bf16[128,384]{1,0:T(8,128)(2,1)S(1)}, bf16[128,384]{1,0:T(8,128)(2,1)S(1)}, u32[]{:S(2)}, u32[]{:S(2)}) collective-permute-start(bf16[128,384]{1,0:T(8,128)(2,1)S(1)} %get-tuple-element.51), channel_id=1, source_target_pairs={{0,12},{4,8},{8,4},{12,0},{1,13},{5,9},{9,5},{13,1},{2,14},{6,10},... | collective-permute-start | bytes 294920 | tf_op jit(solution)/shard_map/ppermute | solution.py:627
  16.1 2.3 %collective-permute-start.17 = (bf16[192,768]{1,0:T(8,128)(2,1)S(1)}, bf16[192,768]{1,0:T(8,128)(2,1)S(1)}, u32[]{:S(2)}, u32[]{:S(2)}) collective-permute-start(bf16[192,768]{1,0:T(8,128)(2,1)S(1)} %copy-done), channel_id=1, source_target_pairs={{0,2},{1,3},{2,0},{3,1},{4,6},{5,7},{6,4},{7,5},{8,10},{9,11},{10,... | collective-permute-start | bytes 884744 | tf_op jit(solution)/shard_map/ppermute | solution.py:621
  19.0 5.1 %collective-permute-done.3.refs_1_ = bf16[128,384]{1,0:T(8,128)(2,1)S(1)} collective-permute-done((bf16[128,384]{1,0:T(8,128)(2,1)S(1)}, bf16[128,384]{1,0:T(8,128)(2,1)S(1)}, u32[]{:S(2)}, u32[]{:S(2)}) %collective-permute-start.3) | collective-permute-done | bytes 98336 | tf_op jit(solution)/shard_map/ppermute | solution.py:627
  24.5 1.8 %collective-permute-start.10 = (bf16[256,384]{1,0:T(8,128)(2,1)S(1)}, bf16[256,384]{1,0:T(8,128)(2,1)S(1)}, u32[]{:S(2)}, u32[]{:S(2)}) collective-permute-start(bf16[256,384]{1,0:T(8,128)(2,1)S(1)} %land_rest.1.refs_1_.rest_ref), channel_id=1, source_target_pairs={{0,2},{1,3},{2,0},{3,1},{4,6},{5,7},{6,4},{7,5},{8,10},{9,11},{10,... | collective-permute-start | bytes 589832 | tf_op jit(solution)/shard_map/ppermute | solution.py:621
  27.4 1.3 %shard_map.72.refs_6_ = f32[256,256]{1,0:T(8,128)S(1)} custom-call(bf16[256,768]{1,0:T(8,128)(2,1)S(1)} %get-tuple-element.55.refs_0_.qkv_ref), custom_call_target="tpu_custom_call" | custom-call | flops 268435456 | bytes 1048576 | tf_op jit(solution)/shard_map/pallas_call | solution.py:450
  29.4 2.9 %collective-permute-done.10.rest_ref = bf16[256,384]{1,0:T(8,128)(2,1)S(1)} collective-permute-done((bf16[256,384]{1,0:T(8,128)(2,1)S(1)}, bf16[256,384]{1,0:T(8,128)(2,1)S(1)}, u32[]{:S(2)}, u32[]{:S(2)}) %collective-permute-start.10) | collective-permute-done | bytes 196640 | tf_op jit(solution)/shard_map/ppermute | solution.py:621
  32.4 3.7 %collective-permute-done.9.lead_ref = bf16[256,384]{1,0:T(8,128)(2,1)S(1)} collective-permute-done((bf16[256,384]{1,0:T(8,128)(2,1)S(1)}, bf16[256,384]{1,0:T(8,128)(2,1)S(1)}, u32[]{:S(2)}, u32[]{:S(2)}) %collective-permute-start.9) | collective-permute-done | bytes 196640 | tf_op jit(solution)/shard_map/ppermute | solution.py:621
  37.6 1.3 %shard_map.77.refs_6_ = f32[256,256]{1,0:T(8,128)S(1)} custom-call(bf16[256,768]{1,0:T(8,128)(2,1)S(1)} %get-tuple-element.57.refs_2_.qkv_ref.refs_0_), custom_call_target="tpu_custom_call" | custom-call | flops 268435456 | bytes 1048576 | tf_op jit(solution)/shard_map/pallas_call | solution.py:450
  39.8 3.8 %collective-permute-start.13 = (bf16[64,384]{1,0:T(8,128)(2,1)S(1)}, bf16[64,384]{1,0:T(8,128)(2,1)S(1)}, u32[]{:S(2)}, u32[]{:S(2)}) collective-permute-start(bf16[64,384]{1,0:T(8,128)(2,1)S(1)} %constant_dynamic-update-slice_fusion.refs_2_), channel_id=1, source_target_pairs={{0,12},{4,8},{8,4},{12,0},{1,13},{5,9},{9,5},{13,1},{2,14},{6,10},... | collective-permute-start | bytes 147464 | tf_op jit(solution)/shard_map/ppermute | solution.py:627
  43.5 1.4 %collective-permute-start.14 = (bf16[64,384]{1,0:T(8,128)(2,1)S(1)}, bf16[64,384]{1,0:T(8,128)(2,1)S(1)}, u32[]{:S(2)}, u32[]{:S(2)}) collective-permute-start(bf16[64,384]{1,0:T(8,128)(2,1)S(1)} %constant_dynamic-update-slice_fusion.refs_2_), channel_id=1, source_target_pairs={{0,8},{4,12},{8,0},{12,4},{1,9},{5,13},{9,1},{13,5},{2,10},{6,14},... | collective-permute-start | bytes 147464 | tf_op jit(solution)/shard_map/ppermute | solution.py:627
  45.5 1.3 %shard_map.73.refs_7_ = f32[256,256]{1,0:T(8,128)S(1)} custom-call(bf16[256,768]{1,0:T(8,128)(2,1)S(1)} %get-tuple-element.56.refs_1_.qkv_ref), custom_call_target="tpu_custom_call" | custom-call | flops 268435456 | bytes 1048576 | tf_op jit(solution)/shard_map/pallas_call | solution.py:450
  46.8 1.3 %middle.1.middle_ref = f32[256,256]{1,0:T(8,128)S(1)} custom-call(bf16[256,768]{1,0:T(8,128)(2,1)S(1)} %get-tuple-element.55.refs_0_.qkv_ref, bf16[256,768]{1,0:T(8,128)(2,1)S(1)} %get-tuple-element.56.refs_1_.qkv_ref, bf16[256,768]{1,0:T(8,128)(2,1)S(1)} %get-tuple-element.57.refs_2_.qkv_ref.refs_0_, ...), custom_call_target="tpu_custom_call" | custom-call | flops 268435456 | bytes 1048576 | tf_op jit(solution)/shard_map/middle/pallas_call | solution.py:499
  49.4 1.0 %shard_map.74 = (bf16[192,256]{1,0:T(8,128)(2,1)S(1)}, bf16[192,256]{1,0:T(8,128)(2,1)S(1)}) custom-call(f32[256,256]{1,0:T(8,128)S(1)} %middle.1.middle_ref, bf16[256,768]{1,0:T(8,128)(2,1)S(1)} %get-tuple-element.55.refs_0_.qkv_ref, bf16[256,768]{1,0:T(8,128)(2,1)S(1)} %get-tuple-element.56.refs_1_.qkv_ref, ...), custom_call_target="tpu_custom_call" | custom-call | flops 134217728 | bytes 1048576 | tf_op jit(solution)/shard_map/pallas_call | solution.py:581
  50.5 1.3 %shard_map.78.refs_7_ = f32[256,256]{1,0:T(8,128)S(1)} custom-call(bf16[256,768]{1,0:T(8,128)(2,1)S(1)} %get-tuple-element.58.refs_3_.qkv_ref.refs_1_), custom_call_target="tpu_custom_call" | custom-call | flops 268435456 | bytes 1048576 | tf_op jit(solution)/shard_map/pallas_call | solution.py:450
  51.8 1.0 %shard_map.79 = (bf16[192,256]{1,0:T(8,128)(2,1)S(1)}, bf16[192,256]{1,0:T(8,128)(2,1)S(1)}) custom-call(f32[256,256]{1,0:T(8,128)S(1)} %middle.1.middle_ref, bf16[256,768]{1,0:T(8,128)(2,1)S(1)} %get-tuple-element.57.refs_2_.qkv_ref.refs_0_, bf16[256,768]{1,0:T(8,128)(2,1)S(1)} %get-tuple-element.58.refs_3_.qkv_ref.refs_1_, ...), custom_call_target="tpu_custom_call" | custom-call | flops 134217728 | bytes 1048576 | tf_op jit(solution)/shard_map/pallas_call | solution.py:581
  52.8 1.6 %collective-permute-start.19 = (bf16[192,256]{1,0:T(8,128)(2,1)S(1)}, bf16[192,256]{1,0:T(8,128)(2,1)S(1)}, u32[]{:S(2)}, u32[]{:S(2)}) collective-permute-start(bf16[192,256]{1,0:T(8,128)(2,1)S(1)} %get-tuple-element.65), channel_id=1, source_target_pairs={{0,2},{1,3},{2,0},{3,1},{4,6},{5,7},{6,4},{7,5},{8,10},{9,11},{10,... | collective-permute-start | bytes 294920 | tf_op jit(solution)/shard_map/ppermute | solution.py:621
  56.0 2.5 %collective-permute-done.19.refs_0_ = bf16[192,256]{1,0:T(8,128)(2,1)S(1)} collective-permute-done((bf16[192,256]{1,0:T(8,128)(2,1)S(1)}, bf16[192,256]{1,0:T(8,128)(2,1)S(1)}, u32[]{:S(2)}, u32[]{:S(2)}) %collective-permute-start.19) | collective-permute-done | bytes 98336 | tf_op jit(solution)/shard_map/ppermute | solution.py:621
  58.5 1.2 %collective-permute-done.20.refs_1_ = bf16[192,256]{1,0:T(8,128)(2,1)S(1)} collective-permute-done((bf16[192,256]{1,0:T(8,128)(2,1)S(1)}, bf16[192,256]{1,0:T(8,128)(2,1)S(1)}, u32[]{:S(2)}, u32[]{:S(2)}) %collective-permute-start.20) | collective-permute-done | bytes 98336 | tf_op jit(solution)/shard_map/ppermute | solution.py:621
  59.7 1.5 %shard_map.80 = bf16[256,768]{1,0:T(8,128)(2,1)} custom-call(f32[768,256]{1,0:T(8,128)S(1)} %shard_map.75.begun_ref, bf16[768,384]{1,0:T(8,128)(2,1)S(1)} %shard_map.76.weight_ref, bf16[192,256]{1,0:T(8,128)(2,1)S(1)} %collective-permute-done.19.refs_0_, bf16[192,256]{1,0:T(8,128)(2,1)S(1)} %collective-permute-done.20.refs_1_), custom_call_target="tpu_custom_call" | custom-call | flops 402653184 | bytes 1048576 | tf_op jit(solution)/shard_map/pallas_call | solution.py:611
  (53 shorter events, 10.1 us)
Async XLA Ops:
  3.1 13.1 %copy-start = (bf16[192,768]{1,0:T(8,128)(2,1)S(1)}, bf16[192,768]{1,0:T(8,128)(2,1)}, u32[]{:S(2)}) copy-start(bf16[192,768]{1,0:T(8,128)(2,1)} %refs_0_) | copy-start | bytes 884740
  3.1 15.4 %copy-start.2 = (bf16[768,4,3,48]{0,3,2,1:T(8,128)(2,1)S(1)}, bf16[768,4,3,48]{0,3,2,1:T(8,128)(2,1)}, u32[]{:S(2)}) copy-start(bf16[768,4,3,48]{0,3,2,1:T(8,128)(2,1)} %param.10) | copy-start | bytes 2654212
  3.1 13.0 %collective-permute-start = (bf16[136,384]{1,0:T(8,128)(2,1)S(1)}, bf16[136,384]{1,0:T(8,128)(2,1)S(1)}, u32[]{:S(2)}, u32[]{:S(2)}) collective-permute-start(bf16[136,384]{1,0:T(8,128)(2,1)S(1)} %get-tuple-element.38), channel_id=1, source_target_pairs={{0,8},{4,12},{8,0},{12,4},{1,9},{5,13},{9,1},{13,5},{2,10},{6,14},... | collective-permute-start | bytes 313352 | tf_op jit(solution)/shard_map/ppermute | solution.py:627
  7.2 8.9 %collective-permute-start.1 = (bf16[136,384]{1,0:T(8,128)(2,1)S(1)}, bf16[136,384]{1,0:T(8,128)(2,1)S(1)}, u32[]{:S(2)}, u32[]{:S(2)}) collective-permute-start(bf16[136,384]{1,0:T(8,128)(2,1)S(1)} %get-tuple-element.39), channel_id=1, source_target_pairs={{0,12},{4,8},{8,4},{12,0},{1,13},{5,9},{9,5},{13,1},{2,14},{6,10},... | collective-permute-start | bytes 313352 | tf_op jit(solution)/shard_map/ppermute | solution.py:627
  8.6 10.1 %collective-permute-start.2 = (bf16[136,384]{1,0:T(8,128)(2,1)S(1)}, bf16[136,384]{1,0:T(8,128)(2,1)S(1)}, u32[]{:S(2)}, u32[]{:S(2)}) collective-permute-start(bf16[136,384]{1,0:T(8,128)(2,1)S(1)} %get-tuple-element.40), channel_id=1, source_target_pairs={{0,4},{4,0},{8,12},{12,8},{1,5},{5,1},{9,13},{13,9},{2,6},{6,2},{1... | collective-permute-start | bytes 313352 | tf_op jit(solution)/shard_map/ppermute | solution.py:627
  11.1 13.0 %collective-permute-start.3 = (bf16[128,384]{1,0:T(8,128)(2,1)S(1)}, bf16[128,384]{1,0:T(8,128)(2,1)S(1)}, u32[]{:S(2)}, u32[]{:S(2)}) collective-permute-start(bf16[128,384]{1,0:T(8,128)(2,1)S(1)} %get-tuple-element.50), channel_id=1, source_target_pairs={{0,8},{4,12},{8,0},{12,4},{1,9},{5,13},{9,1},{13,5},{2,10},{6,14},... | collective-permute-start | bytes 294920 | tf_op jit(solution)/shard_map/ppermute | solution.py:627
  14.0 10.1 %collective-permute-start.4 = (bf16[128,384]{1,0:T(8,128)(2,1)S(1)}, bf16[128,384]{1,0:T(8,128)(2,1)S(1)}, u32[]{:S(2)}, u32[]{:S(2)}) collective-permute-start(bf16[128,384]{1,0:T(8,128)(2,1)S(1)} %get-tuple-element.51), channel_id=1, source_target_pairs={{0,12},{4,8},{8,4},{12,0},{1,13},{5,9},{9,5},{13,1},{2,14},{6,10},... | collective-permute-start | bytes 294920 | tf_op jit(solution)/shard_map/ppermute | solution.py:627
  16.1 8.0 %collective-permute-start.5 = (bf16[128,384]{1,0:T(8,128)(2,1)S(1)}, bf16[128,384]{1,0:T(8,128)(2,1)S(1)}, u32[]{:S(2)}, u32[]{:S(2)}) collective-permute-start(bf16[128,384]{1,0:T(8,128)(2,1)S(1)} %get-tuple-element.52), channel_id=1, source_target_pairs={{0,4},{4,0},{8,12},{12,8},{1,5},{5,1},{9,13},{13,9},{2,6},{6,2},{1... | collective-permute-start | bytes 294920 | tf_op jit(solution)/shard_map/ppermute | solution.py:627
  16.1 12.6 %collective-permute-start.17 = (bf16[192,768]{1,0:T(8,128)(2,1)S(1)}, bf16[192,768]{1,0:T(8,128)(2,1)S(1)}, u32[]{:S(2)}, u32[]{:S(2)}) collective-permute-start(bf16[192,768]{1,0:T(8,128)(2,1)S(1)} %copy-done), channel_id=1, source_target_pairs={{0,2},{1,3},{2,0},{3,1},{4,6},{5,7},{6,4},{7,5},{8,10},{9,11},{10,... | collective-permute-start | bytes 884744 | tf_op jit(solution)/shard_map/ppermute | solution.py:621
  18.5 8.2 %copy-start.3 = (f32[768]{0:T(1024)S(1)}, f32[768]{0:T(1024)}, u32[]{:S(2)}) copy-start(f32[768]{0:T(1024)} %param.9) | copy-start | bytes 9220
  24.5 4.9 %collective-permute-start.8 = (bf16[256,384]{1,0:T(8,128)(2,1)S(1)}, bf16[256,384]{1,0:T(8,128)(2,1)S(1)}, u32[]{:S(2)}, u32[]{:S(2)}) collective-permute-start(bf16[256,384]{1,0:T(8,128)(2,1)S(1)} %land_rest.1.refs_1_.rest_ref), channel_id=1, source_target_pairs={{0,1},{1,0},{2,3},{3,2},{4,5},{5,4},{6,7},{7,6},{8,9},{9,8},{10,11... | collective-permute-start | bytes 589832 | tf_op jit(solution)/shard_map/ppermute | solution.py:621
  24.5 7.8 %collective-permute-start.10 = (bf16[256,384]{1,0:T(8,128)(2,1)S(1)}, bf16[256,384]{1,0:T(8,128)(2,1)S(1)}, u32[]{:S(2)}, u32[]{:S(2)}) collective-permute-start(bf16[256,384]{1,0:T(8,128)(2,1)S(1)} %land_rest.1.refs_1_.rest_ref), channel_id=1, source_target_pairs={{0,2},{1,3},{2,0},{3,1},{4,6},{5,7},{6,4},{7,5},{8,10},{9,11},{10,... | collective-permute-start | bytes 589832 | tf_op jit(solution)/shard_map/ppermute | solution.py:621
  26.4 9.7 %collective-permute-start.9 = (bf16[256,384]{1,0:T(8,128)(2,1)S(1)}, bf16[256,384]{1,0:T(8,128)(2,1)S(1)}, u32[]{:S(2)}, u32[]{:S(2)}) collective-permute-start(bf16[256,384]{1,0:T(8,128)(2,1)S(1)} %get-tuple-element.46.refs_0_.lead_ref), channel_id=1, source_target_pairs={{0,2},{1,3},{2,0},{3,1},{4,6},{5,7},{6,4},{7,5},{8,10},{9,11},{10,... | collective-permute-start | bytes 589832 | tf_op jit(solution)/shard_map/ppermute | solution.py:621
  26.6 9.4 %collective-permute-start.7 = (bf16[256,384]{1,0:T(8,128)(2,1)S(1)}, bf16[256,384]{1,0:T(8,128)(2,1)S(1)}, u32[]{:S(2)}, u32[]{:S(2)}) collective-permute-start(bf16[256,384]{1,0:T(8,128)(2,1)S(1)} %get-tuple-element.46.refs_0_.lead_ref), channel_id=1, source_target_pairs={{0,1},{1,0},{2,3},{3,2},{4,5},{5,4},{6,7},{7,6},{8,9},{9,8},{10,11... | collective-permute-start | bytes 589832 | tf_op jit(solution)/shard_map/ppermute | solution.py:621
  28.8 26.1 %collective-permute-start.6 = (bf16[192,768]{1,0:T(8,128)(2,1)S(1)}, bf16[192,768]{1,0:T(8,128)(2,1)S(1)}, u32[]{:S(2)}, u32[]{:S(2)}) collective-permute-start(bf16[192,768]{1,0:T(8,128)(2,1)S(1)} %copy-done), channel_id=1, source_target_pairs={{0,1},{1,0},{2,3},{3,2},{4,5},{5,4},{6,7},{7,6},{8,9},{9,8},{10,11... | collective-permute-start | bytes 884744 | tf_op jit(solution)/shard_map/ppermute | solution.py:621
  29.4 25.9 %collective-permute-start.18 = (bf16[192,768]{1,0:T(8,128)(2,1)S(1)}, bf16[192,768]{1,0:T(8,128)(2,1)S(1)}, u32[]{:S(2)}, u32[]{:S(2)}) collective-permute-start(bf16[192,768]{1,0:T(8,128)(2,1)S(1)} %collective-permute-done.17.refs_0_), channel_id=1, source_target_pairs={{0,1},{1,0},{2,3},{3,2},{4,5},{5,4},{6,7},{7,6},{8,9},{9,8},{10,11... | collective-permute-start | bytes 884744 | tf_op jit(solution)/shard_map/ppermute | solution.py:621
  32.4 6.6 %collective-permute-start.12 = (bf16[256,384]{1,0:T(8,128)(2,1)S(1)}, bf16[256,384]{1,0:T(8,128)(2,1)S(1)}, u32[]{:S(2)}, u32[]{:S(2)}) collective-permute-start(bf16[256,384]{1,0:T(8,128)(2,1)S(1)} %collective-permute-done.10.rest_ref), channel_id=1, source_target_pairs={{0,1},{1,0},{2,3},{3,2},{4,5},{5,4},{6,7},{7,6},{8,9},{9,8},{10,11... | collective-permute-start | bytes 589832 | tf_op jit(solution)/shard_map/ppermute | solution.py:621
  36.1 2.9 %collective-permute-start.11 = (bf16[256,384]{1,0:T(8,128)(2,1)S(1)}, bf16[256,384]{1,0:T(8,128)(2,1)S(1)}, u32[]{:S(2)}, u32[]{:S(2)}) collective-permute-start(bf16[256,384]{1,0:T(8,128)(2,1)S(1)} %collective-permute-done.9.lead_ref), channel_id=1, source_target_pairs={{0,1},{1,0},{2,3},{3,2},{4,5},{5,4},{6,7},{7,6},{8,9},{9,8},{10,11... | collective-permute-start | bytes 589832 | tf_op jit(solution)/shard_map/ppermute | solution.py:621
  39.8 8.4 %collective-permute-start.13 = (bf16[64,384]{1,0:T(8,128)(2,1)S(1)}, bf16[64,384]{1,0:T(8,128)(2,1)S(1)}, u32[]{:S(2)}, u32[]{:S(2)}) collective-permute-start(bf16[64,384]{1,0:T(8,128)(2,1)S(1)} %constant_dynamic-update-slice_fusion.refs_2_), channel_id=1, source_target_pairs={{0,12},{4,8},{8,4},{12,0},{1,13},{5,9},{9,5},{13,1},{2,14},{6,10},... | collective-permute-start | bytes 147464 | tf_op jit(solution)/shard_map/ppermute | solution.py:627
  43.5 5.0 %collective-permute-start.14 = (bf16[64,384]{1,0:T(8,128)(2,1)S(1)}, bf16[64,384]{1,0:T(8,128)(2,1)S(1)}, u32[]{:S(2)}, u32[]{:S(2)}) collective-permute-start(bf16[64,384]{1,0:T(8,128)(2,1)S(1)} %constant_dynamic-update-slice_fusion.refs_2_), channel_id=1, source_target_pairs={{0,8},{4,12},{8,0},{12,4},{1,9},{5,13},{9,1},{13,5},{2,10},{6,14},... | collective-permute-start | bytes 147464 | tf_op jit(solution)/shard_map/ppermute | solution.py:627
  45.0 4.4 %collective-permute-start.15 = (bf16[64,384]{1,0:T(8,128)(2,1)S(1)}, bf16[64,384]{1,0:T(8,128)(2,1)S(1)}, u32[]{:S(2)}, u32[]{:S(2)}) collective-permute-start(bf16[64,384]{1,0:T(8,128)(2,1)S(1)} %constant_dynamic-update-slice_fusion.refs_2_), channel_id=1, source_target_pairs={{0,4},{4,0},{8,12},{12,8},{1,5},{5,1},{9,13},{13,9},{2,6},{6,2},{1... | collective-permute-start | bytes 147464 | tf_op jit(solution)/shard_map/ppermute | solution.py:627
  50.4 5.3 %collective-permute-start.16 = (bf16[192,256]{1,0:T(8,128)(2,1)S(1)}, bf16[192,256]{1,0:T(8,128)(2,1)S(1)}, u32[]{:S(2)}, u32[]{:S(2)}) collective-permute-start(bf16[192,256]{1,0:T(8,128)(2,1)S(1)} %get-tuple-element.64), channel_id=1, source_target_pairs={{0,1},{1,0},{2,3},{3,2},{4,5},{5,4},{6,7},{7,6},{8,9},{9,8},{10,11... | collective-permute-start | bytes 294920 | tf_op jit(solution)/shard_map/ppermute | solution.py:621
  52.8 5.7 %collective-permute-start.19 = (bf16[192,256]{1,0:T(8,128)(2,1)S(1)}, bf16[192,256]{1,0:T(8,128)(2,1)S(1)}, u32[]{:S(2)}, u32[]{:S(2)}) collective-permute-start(bf16[192,256]{1,0:T(8,128)(2,1)S(1)} %get-tuple-element.65), channel_id=1, source_target_pairs={{0,2},{1,3},{2,0},{3,1},{4,6},{5,7},{6,4},{7,5},{8,10},{9,11},{10,... | collective-permute-start | bytes 294920 | tf_op jit(solution)/shard_map/ppermute | solution.py:621
  54.3 5.3 %collective-permute-start.20 = (bf16[192,256]{1,0:T(8,128)(2,1)S(1)}, bf16[192,256]{1,0:T(8,128)(2,1)S(1)}, u32[]{:S(2)}, u32[]{:S(2)}) collective-permute-start(bf16[192,256]{1,0:T(8,128)(2,1)S(1)} %get-tuple-element.66), channel_id=1, source_target_pairs={{0,3},{1,2},{2,1},{3,0},{4,7},{5,6},{6,5},{7,4},{8,11},{9,10},{10,... | collective-permute-start | bytes 294920 | tf_op jit(solution)/shard_map/ppermute | solution.py:621
  (1 other events, 0.7 us)
